TPU v7x, 128 devices: a whole 4x4x4 slice. The times are simulated.
128 devices in a mesh: col: 16 (over x, y), cuts: 8 (over z, core).
Axes of the slice: x: 4, y: 4, z: 4, core: 2. Of those that a mesh axis runs over, the one named last changes fastest.
Arguments:
- layout: int32 [16, 16], P(None, 'col'), may hold values from 0 to 15
- assign: int32 [32, 16], P('cuts', 'col'), may hold values from 0 to 3
- edge: bfloat16 [16, 64, 128], replicated, may hold values from -3 to 3
- gate_left: bfloat16 [16, 16, 64, 128], P('col'), may hold values from -1.5 to 1.5
- gate_right: bfloat16 [16, 16, 64, 128], P('col'), may hold values from -1.5 to 1.5
- phase_angle: float32 [4, 64], replicated, may hold values from -3.140625 to 3.140625
- close: float32 [16, 64, 128], replicated, may hold values from -6 to 6
Outputs:
- slice_amplitude: float32 [32, 2], P('cuts')
- slice_log: float32 [32], P('cuts')
- total_amp: float32 [2], replicated
- top_log: float32 [], replicated
All inputs are finite; a program needn't handle non-finite values. Where the computation divides by a largest or mean magnitude, that divisor is 1e-20 or more.
Results may differ from a plain program's by a relative error of at most 0.0003.
Values sent between devices are 32-bit elements; how exact they have to be, the bound alone decides.
No kernel may reach another device: no remote copies, remote signals or barrier semaphores. Data moves between devices by JAX's collectives and lax.ppermute only.
A program may use at most 64 MiB of HBM per device.

v0:
```python
import math

import jax
import jax.numpy as jnp
from jax import lax
from jax.sharding import Mesh
from jax.sharding import PartitionSpec as P

BLK = 1
COL = ("col_0", "col_1")


def from_behind(value, axis, by):
    length = lax.axis_size(axis)
    pairs = [(i, i + by) for i in range(length) if 0 <= i + by < length]
    return lax.ppermute(value, axis, pairs)


def over_axes(value, axes):
    for axis in axes:
        value = lax.psum(value, axis)
    return value


def from_everyone(value, axis):
    length = lax.axis_size(axis)
    return lax.all_to_all(
        jnp.broadcast_to(value[None], (length, *value.shape)), axis, 0, 0, tiled=True
    )


def of_everyone(value, axis):
    return from_everyone(value, axis).max(axis=0)


def taken_together(value, axis):
    everything = from_everyone(value, axis)
    return jnp.sum(everything, axis=0)


def one_hot(values, count, dtype):
    return (values[..., None] == jnp.arange(count, dtype=jnp.int32)).astype(dtype)


def sweep_column(board, left_sel, right_sel, cosine, sine):
    width = board.shape[-2]
    below = jnp.concatenate([board[:, 1:], jnp.zeros_like(board[:, :1])], axis=1)
    mixed = board + 0.5 * below
    left_four = left_sel.reshape(left_sel.shape[0], width, 2, width)
    stacked = jnp.einsum("rpka,srab->srkpb", left_four, mixed, precision=lax.Precision.HIGHEST)
    former = stacked[:, :, 0]
    latter = stacked[:, :, 1]
    real_part = former[..., :width] - latter[..., width:]
    imag_part = former[..., width:] + latter[..., :width]
    from_real = jnp.einsum("srab,rbq->sraq", real_part, right_sel, precision=lax.Precision.HIGHEST)
    from_imag = jnp.einsum("srab,rbq->sraq", imag_part, right_sel, precision=lax.Precision.HIGHEST)
    out_real = from_real[..., :width] - from_imag[..., width:]
    out_imag = from_real[..., width:] + from_imag[..., :width]
    cos_rows = cosine[:, None, None, :]
    sin_rows = sine[:, None, None, :]
    turned_real = out_real * cos_rows - out_imag * sin_rows
    turned_imag = out_real * sin_rows + out_imag * cos_rows
    peaks = jnp.maximum(
        jnp.max(jnp.abs(turned_real), axis=(1, 2, 3)), jnp.max(jnp.abs(turned_imag), axis=(1, 2, 3))
    )
    peaks = jnp.maximum(peaks, 1.0)
    board = jnp.concatenate([turned_real, turned_imag], -1) / peaks[:, None, None, None]
    return (board, jnp.log(peaks))


def amplitude(board, close):
    width = close.shape[-1] // 2
    b_real = board[..., :width]
    b_imag = board[..., width:]
    c_real = close[..., :width]
    c_imag = close[..., width:]
    factor = 1.0 / math.sqrt(close.shape[0] * width * width)
    amp_real = jnp.sum(b_real * c_real - b_imag * c_imag, axis=(1, 2, 3)) * factor
    amp_imag = jnp.sum(b_real * c_imag + b_imag * c_real, axis=(1, 2, 3)) * factor
    return jnp.stack([amp_real, amp_imag], -1)


def body(layout, assign, edge, gate_left, gate_right, phase_angle, close):
    sections = lax.axis_size(COL)
    place = lax.axis_index(COL)
    kinds = gate_left.shape[1]
    values = phase_angle.shape[0]
    per_device = assign.shape[0]
    group = BLK
    groups = per_device // group
    row_hot = one_hot(layout.T, kinds, jnp.bfloat16)
    left_all = jnp.einsum("crg,cgpq->crpq", row_hot, gate_left, preferred_element_type=jnp.float32)
    right_all = jnp.einsum(
        "crg,cgpq->crpq", row_hot, gate_right, preferred_element_type=jnp.float32
    )
    cos_table = jnp.cos(phase_angle)
    sin_table = jnp.sin(phase_angle)
    start_board = edge.astype(jnp.float32)[None]

    def run_columns(board, assign_group):
        value_hot = one_hot(assign_group, values, jnp.float32)
        cos_sel = jnp.einsum("scq,qb->scb", value_hot, cos_table, precision=lax.Precision.HIGHEST)
        sin_sel = jnp.einsum("scq,qb->scb", value_hot, sin_table, precision=lax.Precision.HIGHEST)
        board, scales = sweep_column(board, left_all[0], right_all[0], cos_sel[:, 0], sin_sel[:, 0])
        return (board, scales)

    def section(step, carry):
        held_board, amps, logs = carry
        index = step - place
        valid = jnp.logical_and(index >= 0, index < groups)
        safe = jnp.clip(index, 0, groups - 1)
        first = place == 0
        board = jnp.where(first, start_board, held_board)
        assign_group = lax.dynamic_slice_in_dim(assign, safe * group, group, 0)
        board, scales = lax.cond(
            valid,
            lambda: run_columns(board, assign_group),
            lambda: (board, jnp.zeros((group,), jnp.float32)),
        )
        keep = jnp.logical_and(valid, place == sections - 1)
        amps = jnp.where(
            keep,
            lax.dynamic_update_slice_in_dim(amps, amplitude(board, close), safe * group, 0),
            amps,
        )
        logs = jnp.where(
            valid, lax.dynamic_update_slice_in_dim(logs, scales, safe * group, 0), logs
        )
        held_board = from_behind(board, COL, 1)
        return (held_board, amps, logs)

    initial = (
        start_board,
        jnp.zeros((per_device, 2), jnp.float32),
        jnp.zeros((per_device,), jnp.float32),
    )
    unused_board, amps, logs = lax.fori_loop(0, sections + groups - 1, section, initial)
    amps, logs = (over_axes(amps, COL), over_axes(logs, COL))
    local_top = jnp.max(logs)
    top_log = of_everyone(local_top, "cuts")
    partial_sum = jnp.sum(amps * jnp.exp(logs - top_log)[:, None], axis=0)
    total_amp = taken_together(partial_sum, "cuts")
    return (amps, logs, total_amp, top_log)


def solution(mesh):
    split = Mesh(mesh.devices.reshape(4, 4, mesh.shape["cuts"]), ("col_0", "col_1", "cuts"))
    placed = (
        P(None, COL),
        P("cuts", COL),
        P(),
        P(COL, None, None, None),
        P(COL, None, None, None),
        P(),
        P(),
    )
    return jax.shard_map(
        body,
        mesh=split,
        in_specs=placed,
        out_specs=(P("cuts", None), P("cuts"), P(), P()),
        check_vma=False,
    )
```

profile of v0, /device:TPU:0, one launch (start us, length us, event | category | flops | bytes accessed | tf_op | source)
XLA Modules:
  0.0 458.1 jit_solution(4643942819988756618)
XLA Ops:
  6.2 368.8 %while.18 = (s32[]{:T(128)}, f32[1,16,64,128]{3,2,1,0:T(8,128)S(1)}, f32[4,2]{0,1:T(2,128)S(1)}, f32[4]{0:T(128)S(1)}, s32[]{:T(128)}, /*index=5*/pred[]{:T(512)...) while((s32[]{:T(128)}, ...), condition=%wide.region_7.8_spmd, body=%wide.region_0.7_spmd.sunk | while | flops 404756480 | bytes 22449744 | solution.py:137
  7.0 8.9 %conditional.2 = (f32[1,16,64,128]{3,2,1,0:T(8,128)S(1)}, f32[1]{0:T(128)}) conditional(s32[]{:T(128)} %convert_element_type.12, f32[1,16,64,128]{3,2,1,0:T(8,128)S(1)} %broadcast_select_fusion.2, (f32[1,16,64,128]{3,2,1,0:T(8,128)S(1)}, f32[1,16,64,128]{3,2,1,0:T(8,128)}, f32[1,16,64,128]{3,2,1,0:T(8,128)S(1)}, s32[4,1]{0,1:T(1,128)S(1)}, s32[]{:T(128)}, ...), branch_computations={%region_1.1_spmd, %region_2.4_spmd} | conditional | flops 404101120 | bytes 13536336 | solution.py:115
  7.1 1.7 squeeze.14
  8.7 1.0 convolution_bitcast_fusion
  13.5 1.0 abs_reduce_fusion.1
  16.0 1.3 collective-permute-start
  17.3 1.0 fusion.39
  19.8 8.2 %collective-permute-done = f32[1,16,64,128]{3,2,1,0:T(8,128)S(1)} collective-permute-done((f32[1,16,64,128]{3,2,1,0:T(8,128)S(1)}, f32[1,16,64,128]{3,2,1,0:T(8,128)S(1)}, u32[]{:S(2)}, u32[]{:S(2)}) %collective-permute-start) | collective-permute-done | bytes 524320 | tf_op jit(solution)/shard_map/while/body/eval_jaxpr/ppermute | solution.py:16
  28.8 8.9 %conditional.2 = (f32[1,16,64,128]{3,2,1,0:T(8,128)S(1)}, f32[1]{0:T(128)}) conditional(s32[]{:T(128)} %convert_element_type.12, f32[1,16,64,128]{3,2,1,0:T(8,128)S(1)} %broadcast_select_fusion.2, (f32[1,16,64,128]{3,2,1,0:T(8,128)S(1)}, f32[1,16,64,128]{3,2,1,0:T(8,128)}, f32[1,16,64,128]{3,2,1,0:T(8,128)S(1)}, s32[4,1]{0,1:T(1,128)S(1)}, s32[]{:T(128)}, ...), branch_computations={%region_1.1_spmd, %region_2.4_spmd} | conditional | flops 404101120 | bytes 13536336 | solution.py:115
  28.9 1.7 squeeze.14
  30.5 1.0 convolution_bitcast_fusion
  35.3 1.0 abs_reduce_fusion.1
  37.8 4.4 collective-permute-start
  44.7 7.3 %collective-permute-done = f32[1,16,64,128]{3,2,1,0:T(8,128)S(1)} collective-permute-done((f32[1,16,64,128]{3,2,1,0:T(8,128)S(1)}, f32[1,16,64,128]{3,2,1,0:T(8,128)S(1)}, u32[]{:S(2)}, u32[]{:S(2)}) %collective-permute-start) | collective-permute-done | bytes 524320 | tf_op jit(solution)/shard_map/while/body/eval_jaxpr/ppermute | solution.py:16
  52.9 8.9 %conditional.2 = (f32[1,16,64,128]{3,2,1,0:T(8,128)S(1)}, f32[1]{0:T(128)}) conditional(s32[]{:T(128)} %convert_element_type.12, f32[1,16,64,128]{3,2,1,0:T(8,128)S(1)} %broadcast_select_fusion.2, (f32[1,16,64,128]{3,2,1,0:T(8,128)S(1)}, f32[1,16,64,128]{3,2,1,0:T(8,128)}, f32[1,16,64,128]{3,2,1,0:T(8,128)S(1)}, s32[4,1]{0,1:T(1,128)S(1)}, s32[]{:T(128)}, ...), branch_computations={%region_1.1_spmd, %region_2.4_spmd} | conditional | flops 404101120 | bytes 13536336 | solution.py:115
  52.9 1.7 squeeze.14
  54.6 1.0 convolution_bitcast_fusion
  59.3 1.0 abs_reduce_fusion.1
  61.8 4.4 collective-permute-start
  68.8 6.5 %collective-permute-done = f32[1,16,64,128]{3,2,1,0:T(8,128)S(1)} collective-permute-done((f32[1,16,64,128]{3,2,1,0:T(8,128)S(1)}, f32[1,16,64,128]{3,2,1,0:T(8,128)S(1)}, u32[]{:S(2)}, u32[]{:S(2)}) %collective-permute-start) | collective-permute-done | bytes 524320 | tf_op jit(solution)/shard_map/while/body/eval_jaxpr/ppermute | solution.py:16
  76.0 8.9 %conditional.2 = (f32[1,16,64,128]{3,2,1,0:T(8,128)S(1)}, f32[1]{0:T(128)}) conditional(s32[]{:T(128)} %convert_element_type.12, f32[1,16,64,128]{3,2,1,0:T(8,128)S(1)} %broadcast_select_fusion.2, (f32[1,16,64,128]{3,2,1,0:T(8,128)S(1)}, f32[1,16,64,128]{3,2,1,0:T(8,128)}, f32[1,16,64,128]{3,2,1,0:T(8,128)S(1)}, s32[4,1]{0,1:T(1,128)S(1)}, s32[]{:T(128)}, ...), branch_computations={%region_1.1_spmd, %region_2.4_spmd} | conditional | flops 404101120 | bytes 13536336 | solution.py:115
  76.1 1.7 squeeze.14
  77.7 1.0 convolution_bitcast_fusion
  82.5 1.0 abs_reduce_fusion.1
  85.0 4.4 collective-permute-start
  91.9 5.6 %collective-permute-done = f32[1,16,64,128]{3,2,1,0:T(8,128)S(1)} collective-permute-done((f32[1,16,64,128]{3,2,1,0:T(8,128)S(1)}, f32[1,16,64,128]{3,2,1,0:T(8,128)S(1)}, u32[]{:S(2)}, u32[]{:S(2)}) %collective-permute-start) | collective-permute-done | bytes 524320 | tf_op jit(solution)/shard_map/while/body/eval_jaxpr/ppermute | solution.py:16
  98.4 13.4 %collective-permute-start = (f32[1,16,64,128]{3,2,1,0:T(8,128)S(1)}, f32[1,16,64,128]{3,2,1,0:T(8,128)S(1)}, u32[]{:S(2)}, u32[]{:S(2)}) collective-permute-start(f32[1,16,64,128]{3,2,1,0:T(8,128)S(1)} %get-tuple-element.477), channel_id=1, source_target_pairs={{0,8},{8,16},{16,24},{24,32},{32,40},{40,48},{48,56},{56,64},{64,7... | collective-permute-start | bytes 1572872 | tf_op jit(solution)/shard_map/while/body/eval_jaxpr/ppermute | solution.py:16
  111.7 1.0 fusion.39
  114.3 4.8 %collective-permute-done = f32[1,16,64,128]{3,2,1,0:T(8,128)S(1)} collective-permute-done((f32[1,16,64,128]{3,2,1,0:T(8,128)S(1)}, f32[1,16,64,128]{3,2,1,0:T(8,128)S(1)}, u32[]{:S(2)}, u32[]{:S(2)}) %collective-permute-start) | collective-permute-done | bytes 524320 | tf_op jit(solution)/shard_map/while/body/eval_jaxpr/ppermute | solution.py:16
  119.8 4.4 collective-permute-start
  124.2 1.0 fusion.39
  126.8 4.1 collective-permute-done
  131.7 12.2 %collective-permute-start = (f32[1,16,64,128]{3,2,1,0:T(8,128)S(1)}, f32[1,16,64,128]{3,2,1,0:T(8,128)S(1)}, u32[]{:S(2)}, u32[]{:S(2)}) collective-permute-start(f32[1,16,64,128]{3,2,1,0:T(8,128)S(1)} %get-tuple-element.477), channel_id=1, source_target_pairs={{0,8},{8,16},{16,24},{24,32},{32,40},{40,48},{48,56},{56,64},{64,7... | collective-permute-start | bytes 1572872 | tf_op jit(solution)/shard_map/while/body/eval_jaxpr/ppermute | solution.py:16
  146.5 5.1 %collective-permute-done = f32[1,16,64,128]{3,2,1,0:T(8,128)S(1)} collective-permute-done((f32[1,16,64,128]{3,2,1,0:T(8,128)S(1)}, f32[1,16,64,128]{3,2,1,0:T(8,128)S(1)}, u32[]{:S(2)}, u32[]{:S(2)}) %collective-permute-start) | collective-permute-done | bytes 524320 | tf_op jit(solution)/shard_map/while/body/eval_jaxpr/ppermute | solution.py:16
  152.4 4.4 collective-permute-start
  159.3 4.1 collective-permute-done
  164.3 13.4 %collective-permute-start = (f32[1,16,64,128]{3,2,1,0:T(8,128)S(1)}, f32[1,16,64,128]{3,2,1,0:T(8,128)S(1)}, u32[]{:S(2)}, u32[]{:S(2)}) collective-permute-start(f32[1,16,64,128]{3,2,1,0:T(8,128)S(1)} %get-tuple-element.477), channel_id=1, source_target_pairs={{0,8},{8,16},{16,24},{24,32},{32,40},{40,48},{48,56},{56,64},{64,7... | collective-permute-start | bytes 1572872 | tf_op jit(solution)/shard_map/while/body/eval_jaxpr/ppermute | solution.py:16
  180.2 4.1 collective-permute-done
  185.2 6.5 %collective-permute-start = (f32[1,16,64,128]{3,2,1,0:T(8,128)S(1)}, f32[1,16,64,128]{3,2,1,0:T(8,128)S(1)}, u32[]{:S(2)}, u32[]{:S(2)}) collective-permute-start(f32[1,16,64,128]{3,2,1,0:T(8,128)S(1)} %get-tuple-element.477), channel_id=1, source_target_pairs={{0,8},{8,16},{16,24},{24,32},{32,40},{40,48},{48,56},{56,64},{64,7... | collective-permute-start | bytes 1572872 | tf_op jit(solution)/shard_map/while/body/eval_jaxpr/ppermute | solution.py:16
  194.2 4.1 collective-permute-done
  199.2 17.6 %collective-permute-start = (f32[1,16,64,128]{3,2,1,0:T(8,128)S(1)}, f32[1,16,64,128]{3,2,1,0:T(8,128)S(1)}, u32[]{:S(2)}, u32[]{:S(2)}) collective-permute-start(f32[1,16,64,128]{3,2,1,0:T(8,128)S(1)} %get-tuple-element.477), channel_id=1, source_target_pairs={{0,8},{8,16},{16,24},{24,32},{32,40},{40,48},{48,56},{56,64},{64,7... | collective-permute-start | bytes 1572872 | tf_op jit(solution)/shard_map/while/body/eval_jaxpr/ppermute | solution.py:16
  216.8 1.0 fusion.39
  219.3 6.5 %collective-permute-done = f32[1,16,64,128]{3,2,1,0:T(8,128)S(1)} collective-permute-done((f32[1,16,64,128]{3,2,1,0:T(8,128)S(1)}, f32[1,16,64,128]{3,2,1,0:T(8,128)S(1)}, u32[]{:S(2)}, u32[]{:S(2)}) %collective-permute-start) | collective-permute-done | bytes 524320 | tf_op jit(solution)/shard_map/while/body/eval_jaxpr/ppermute | solution.py:16
  226.6 4.4 collective-permute-start
  233.5 7.2 %collective-permute-done = f32[1,16,64,128]{3,2,1,0:T(8,128)S(1)} collective-permute-done((f32[1,16,64,128]{3,2,1,0:T(8,128)S(1)}, f32[1,16,64,128]{3,2,1,0:T(8,128)S(1)}, u32[]{:S(2)}, u32[]{:S(2)}) %collective-permute-start) | collective-permute-done | bytes 524320 | tf_op jit(solution)/shard_map/while/body/eval_jaxpr/ppermute | solution.py:16
  241.6 19.5 %collective-permute-start = (f32[1,16,64,128]{3,2,1,0:T(8,128)S(1)}, f32[1,16,64,128]{3,2,1,0:T(8,128)S(1)}, u32[]{:S(2)}, u32[]{:S(2)}) collective-permute-start(f32[1,16,64,128]{3,2,1,0:T(8,128)S(1)} %get-tuple-element.477), channel_id=1, source_target_pairs={{0,8},{8,16},{16,24},{24,32},{32,40},{40,48},{48,56},{56,64},{64,7... | collective-permute-start | bytes 1572872 | tf_op jit(solution)/shard_map/while/body/eval_jaxpr/ppermute | solution.py:16
  261.1 1.0 fusion.39
  263.6 9.2 %collective-permute-done = f32[1,16,64,128]{3,2,1,0:T(8,128)S(1)} collective-permute-done((f32[1,16,64,128]{3,2,1,0:T(8,128)S(1)}, f32[1,16,64,128]{3,2,1,0:T(8,128)S(1)}, u32[]{:S(2)}, u32[]{:S(2)}) %collective-permute-start) | collective-permute-done | bytes 524320 | tf_op jit(solution)/shard_map/while/body/eval_jaxpr/ppermute | solution.py:16
  273.6 6.8 %collective-permute-start = (f32[1,16,64,128]{3,2,1,0:T(8,128)S(1)}, f32[1,16,64,128]{3,2,1,0:T(8,128)S(1)}, u32[]{:S(2)}, u32[]{:S(2)}) collective-permute-start(f32[1,16,64,128]{3,2,1,0:T(8,128)S(1)} %get-tuple-element.477), channel_id=1, source_target_pairs={{0,8},{8,16},{16,24},{24,32},{32,40},{40,48},{48,56},{56,64},{64,7... | collective-permute-start | bytes 1572872 | tf_op jit(solution)/shard_map/while/body/eval_jaxpr/ppermute | solution.py:16
  282.9 8.0 %collective-permute-done = f32[1,16,64,128]{3,2,1,0:T(8,128)S(1)} collective-permute-done((f32[1,16,64,128]{3,2,1,0:T(8,128)S(1)}, f32[1,16,64,128]{3,2,1,0:T(8,128)S(1)}, u32[]{:S(2)}, u32[]{:S(2)}) %collective-permute-start) | collective-permute-done | bytes 524320 | tf_op jit(solution)/shard_map/while/body/eval_jaxpr/ppermute | solution.py:16
  291.7 5.6 %collective-permute-start = (f32[1,16,64,128]{3,2,1,0:T(8,128)S(1)}, f32[1,16,64,128]{3,2,1,0:T(8,128)S(1)}, u32[]{:S(2)}, u32[]{:S(2)}) collective-permute-start(f32[1,16,64,128]{3,2,1,0:T(8,128)S(1)} %get-tuple-element.477), channel_id=1, source_target_pairs={{0,8},{8,16},{16,24},{24,32},{32,40},{40,48},{48,56},{56,64},{64,7... | collective-permute-start | bytes 1572872 | tf_op jit(solution)/shard_map/while/body/eval_jaxpr/ppermute | solution.py:16
  299.9 6.9 %collective-permute-done = f32[1,16,64,128]{3,2,1,0:T(8,128)S(1)} collective-permute-done((f32[1,16,64,128]{3,2,1,0:T(8,128)S(1)}, f32[1,16,64,128]{3,2,1,0:T(8,128)S(1)}, u32[]{:S(2)}, u32[]{:S(2)}) %collective-permute-start) | collective-permute-done | bytes 524320 | tf_op jit(solution)/shard_map/while/body/eval_jaxpr/ppermute | solution.py:16
  307.6 6.5 %collective-permute-start = (f32[1,16,64,128]{3,2,1,0:T(8,128)S(1)}, f32[1,16,64,128]{3,2,1,0:T(8,128)S(1)}, u32[]{:S(2)}, u32[]{:S(2)}) collective-permute-start(f32[1,16,64,128]{3,2,1,0:T(8,128)S(1)} %get-tuple-element.477), channel_id=1, source_target_pairs={{0,8},{8,16},{16,24},{24,32},{32,40},{40,48},{48,56},{56,64},{64,7... | collective-permute-start | bytes 1572872 | tf_op jit(solution)/shard_map/while/body/eval_jaxpr/ppermute | solution.py:16
  316.6 6.0 %collective-permute-done = f32[1,16,64,128]{3,2,1,0:T(8,128)S(1)} collective-permute-done((f32[1,16,64,128]{3,2,1,0:T(8,128)S(1)}, f32[1,16,64,128]{3,2,1,0:T(8,128)S(1)}, u32[]{:S(2)}, u32[]{:S(2)}) %collective-permute-start) | collective-permute-done | bytes 524320 | tf_op jit(solution)/shard_map/while/body/eval_jaxpr/ppermute | solution.py:16
  323.5 6.5 %collective-permute-start = (f32[1,16,64,128]{3,2,1,0:T(8,128)S(1)}, f32[1,16,64,128]{3,2,1,0:T(8,128)S(1)}, u32[]{:S(2)}, u32[]{:S(2)}) collective-permute-start(f32[1,16,64,128]{3,2,1,0:T(8,128)S(1)} %get-tuple-element.477), channel_id=1, source_target_pairs={{0,8},{8,16},{16,24},{24,32},{32,40},{40,48},{48,56},{56,64},{64,7... | collective-permute-start | bytes 1572872 | tf_op jit(solution)/shard_map/while/body/eval_jaxpr/ppermute | solution.py:16
  332.5 5.2 %collective-permute-done = f32[1,16,64,128]{3,2,1,0:T(8,128)S(1)} collective-permute-done((f32[1,16,64,128]{3,2,1,0:T(8,128)S(1)}, f32[1,16,64,128]{3,2,1,0:T(8,128)S(1)}, u32[]{:S(2)}, u32[]{:S(2)}) %collective-permute-start) | collective-permute-done | bytes 524320 | tf_op jit(solution)/shard_map/while/body/eval_jaxpr/ppermute | solution.py:16
  338.5 6.5 %collective-permute-start = (f32[1,16,64,128]{3,2,1,0:T(8,128)S(1)}, f32[1,16,64,128]{3,2,1,0:T(8,128)S(1)}, u32[]{:S(2)}, u32[]{:S(2)}) collective-permute-start(f32[1,16,64,128]{3,2,1,0:T(8,128)S(1)} %get-tuple-element.477), channel_id=1, source_target_pairs={{0,8},{8,16},{16,24},{24,32},{32,40},{40,48},{48,56},{56,64},{64,7... | collective-permute-start | bytes 1572872 | tf_op jit(solution)/shard_map/while/body/eval_jaxpr/ppermute | solution.py:16
  347.5 4.3 collective-permute-done
  352.6 15.7 %collective-permute-start = (f32[1,16,64,128]{3,2,1,0:T(8,128)S(1)}, f32[1,16,64,128]{3,2,1,0:T(8,128)S(1)}, u32[]{:S(2)}, u32[]{:S(2)}) collective-permute-start(f32[1,16,64,128]{3,2,1,0:T(8,128)S(1)} %get-tuple-element.477), channel_id=1, source_target_pairs={{0,8},{8,16},{16,24},{24,32},{32,40},{40,48},{48,56},{56,64},{64,7... | collective-permute-start | bytes 1572872 | tf_op jit(solution)/shard_map/while/body/eval_jaxpr/ppermute | solution.py:16
  370.9 4.1 collective-permute-done
  375.0 42.8 %all-reduce.2 = (f32[4,2]{0,1:T(2,128)S(1)}, f32[4]{0:T(128)S(1)}) all-reduce(f32[4,2]{0,1:T(2,128)S(1)} %get-tuple-element.300, f32[4]{0:T(128)S(1)} %get-tuple-element.301), channel_id=1, replica_groups=mesh['col_0'=4,'col_1'=4,'cuts'=8] {'col_0'}, use_global_device_ids=true, to_apply=%region_8.9 | all-reduce | flops 12 | bytes 96 | tf_op jit(solution)/shard_map/psum | solution.py:21
  417.8 14.5 %all-reduce.1 = (f32[4,2]{0,1:T(2,128)S(1)}, f32[4]{0:T(128)S(1)}) all-reduce(f32[4,2]{0,1:T(2,128)S(1)} %get-tuple-element.376, f32[4]{0:T(128)S(1)} %get-tuple-element.377), channel_id=1, replica_groups=mesh['col_0'=4,'col_1'=4,'cuts'=8] {'col_1'}, use_global_device_ids=true, to_apply=%region_9.10 | all-reduce | flops 12 | bytes 96 | tf_op jit(solution)/shard_map/psum | solution.py:21
  433.6 14.9 %all_to_all.12 = f32[8,1,1]{2,1,0:T(1,128)S(1)} all-to-all(f32[8,1,1]{2,1,0:T(1,128)S(1)} %broadcast_in_dim.43), channel_id=1, replica_groups=mesh['col_0'=4,'col_1'=4,'cuts'=8] {'cuts'}, dimensions={0} | all-to-all | bytes 64 | tf_op jit(solution)/shard_map/all_to_all | solution.py:27
  449.9 7.6 %all_to_all.13 = f32[8,1,2]{2,1,0:T(1,128)S(1)} all-to-all(f32[8,1,2]{2,1,0:T(1,128)S(1)} %broadcast_in_dim.44), channel_id=1, replica_groups=mesh['col_0'=4,'col_1'=4,'cuts'=8] {'cuts'}, dimensions={0} | all-to-all | bytes 128 | tf_op jit(solution)/shard_map/all_to_all | solution.py:27
  (247 shorter events, 59.6 us)
Async XLA Ops:
  0.6 1.0 copy-start
  2.5 1.0 copy-start.5
  3.8 1.0 copy-start.4
  4.8 1.0 copy-start.1
  5.5 0.7 copy-start.9
  6.2 0.8 copy-start.2
  16.0 12.0 %collective-permute-start = (f32[1,16,64,128]{3,2,1,0:T(8,128)S(1)}, f32[1,16,64,128]{3,2,1,0:T(8,128)S(1)}, u32[]{:S(2)}, u32[]{:S(2)}) collective-permute-start(f32[1,16,64,128]{3,2,1,0:T(8,128)S(1)} %get-tuple-element.477), channel_id=1, source_target_pairs={{0,8},{8,16},{16,24},{24,32},{32,40},{40,48},{48,56},{56,64},{64,7... | collective-permute-start | bytes 1572872 | tf_op jit(solution)/shard_map/while/body/eval_jaxpr/ppermute | solution.py:16
  17.3 10.7 %copy-start.3 = (f32[1,16,64,128]{3,2,1,0:T(8,128)S(1)}, f32[1,16,64,128]{3,2,1,0:T(8,128)}, u32[]{:S(2)}) copy-start(f32[1,16,64,128]{3,2,1,0:T(8,128)} %copy-done.2) | copy-start | bytes 1572868 | tf_op jit(solution)/shard_map/while
  28.0 0.8 copy-start.2
  37.8 14.3 %collective-permute-start = (f32[1,16,64,128]{3,2,1,0:T(8,128)S(1)}, f32[1,16,64,128]{3,2,1,0:T(8,128)S(1)}, u32[]{:S(2)}, u32[]{:S(2)}) collective-permute-start(f32[1,16,64,128]{3,2,1,0:T(8,128)S(1)} %get-tuple-element.477), channel_id=1, source_target_pairs={{0,8},{8,16},{16,24},{24,32},{32,40},{40,48},{48,56},{56,64},{64,7... | collective-permute-start | bytes 1572872 | tf_op jit(solution)/shard_map/while/body/eval_jaxpr/ppermute | solution.py:16
  42.2 9.9 %copy-start.3 = (f32[1,16,64,128]{3,2,1,0:T(8,128)S(1)}, f32[1,16,64,128]{3,2,1,0:T(8,128)}, u32[]{:S(2)}) copy-start(f32[1,16,64,128]{3,2,1,0:T(8,128)} %copy-done.2) | copy-start | bytes 1572868 | tf_op jit(solution)/shard_map/while
  52.1 0.8 copy-start.2
  61.8 13.4 %collective-permute-start = (f32[1,16,64,128]{3,2,1,0:T(8,128)S(1)}, f32[1,16,64,128]{3,2,1,0:T(8,128)S(1)}, u32[]{:S(2)}, u32[]{:S(2)}) collective-permute-start(f32[1,16,64,128]{3,2,1,0:T(8,128)S(1)} %get-tuple-element.477), channel_id=1, source_target_pairs={{0,8},{8,16},{16,24},{24,32},{32,40},{40,48},{48,56},{56,64},{64,7... | collective-permute-start | bytes 1572872 | tf_op jit(solution)/shard_map/while/body/eval_jaxpr/ppermute | solution.py:16
  66.2 9.0 %copy-start.3 = (f32[1,16,64,128]{3,2,1,0:T(8,128)S(1)}, f32[1,16,64,128]{3,2,1,0:T(8,128)}, u32[]{:S(2)}) copy-start(f32[1,16,64,128]{3,2,1,0:T(8,128)} %copy-done.2) | copy-start | bytes 1572868 | tf_op jit(solution)/shard_map/while
  75.2 0.8 copy-start.2
  85.0 12.6 %collective-permute-start = (f32[1,16,64,128]{3,2,1,0:T(8,128)S(1)}, f32[1,16,64,128]{3,2,1,0:T(8,128)S(1)}, u32[]{:S(2)}, u32[]{:S(2)}) collective-permute-start(f32[1,16,64,128]{3,2,1,0:T(8,128)S(1)} %get-tuple-element.477), channel_id=1, source_target_pairs={{0,8},{8,16},{16,24},{24,32},{32,40},{40,48},{48,56},{56,64},{64,7... | collective-permute-start | bytes 1572872 | tf_op jit(solution)/shard_map/while/body/eval_jaxpr/ppermute | solution.py:16
  89.4 8.1 %copy-start.3 = (f32[1,16,64,128]{3,2,1,0:T(8,128)S(1)}, f32[1,16,64,128]{3,2,1,0:T(8,128)}, u32[]{:S(2)}) copy-start(f32[1,16,64,128]{3,2,1,0:T(8,128)} %copy-done.2) | copy-start | bytes 1572868 | tf_op jit(solution)/shard_map/while
  97.5 0.8 copy-start.2
  98.4 20.6 %collective-permute-start = (f32[1,16,64,128]{3,2,1,0:T(8,128)S(1)}, f32[1,16,64,128]{3,2,1,0:T(8,128)S(1)}, u32[]{:S(2)}, u32[]{:S(2)}) collective-permute-start(f32[1,16,64,128]{3,2,1,0:T(8,128)S(1)} %get-tuple-element.477), channel_id=1, source_target_pairs={{0,8},{8,16},{16,24},{24,32},{32,40},{40,48},{48,56},{56,64},{64,7... | collective-permute-start | bytes 1572872 | tf_op jit(solution)/shard_map/while/body/eval_jaxpr/ppermute | solution.py:16
  111.7 7.3 %copy-start.3 = (f32[1,16,64,128]{3,2,1,0:T(8,128)S(1)}, f32[1,16,64,128]{3,2,1,0:T(8,128)}, u32[]{:S(2)}) copy-start(f32[1,16,64,128]{3,2,1,0:T(8,128)} %copy-done.2) | copy-start | bytes 1572868 | tf_op jit(solution)/shard_map/while
  119.0 0.8 copy-start.2
  119.8 11.1 %collective-permute-start = (f32[1,16,64,128]{3,2,1,0:T(8,128)S(1)}, f32[1,16,64,128]{3,2,1,0:T(8,128)S(1)}, u32[]{:S(2)}, u32[]{:S(2)}) collective-permute-start(f32[1,16,64,128]{3,2,1,0:T(8,128)S(1)} %get-tuple-element.477), channel_id=1, source_target_pairs={{0,8},{8,16},{16,24},{24,32},{32,40},{40,48},{48,56},{56,64},{64,7... | collective-permute-start | bytes 1572872 | tf_op jit(solution)/shard_map/while/body/eval_jaxpr/ppermute | solution.py:16
  124.2 6.7 %copy-start.3 = (f32[1,16,64,128]{3,2,1,0:T(8,128)S(1)}, f32[1,16,64,128]{3,2,1,0:T(8,128)}, u32[]{:S(2)}) copy-start(f32[1,16,64,128]{3,2,1,0:T(8,128)} %copy-done.2) | copy-start | bytes 1572868 | tf_op jit(solution)/shard_map/while
  130.9 0.8 copy-start.2
  131.7 19.9 %collective-permute-start = (f32[1,16,64,128]{3,2,1,0:T(8,128)S(1)}, f32[1,16,64,128]{3,2,1,0:T(8,128)S(1)}, u32[]{:S(2)}, u32[]{:S(2)}) collective-permute-start(f32[1,16,64,128]{3,2,1,0:T(8,128)S(1)} %get-tuple-element.477), channel_id=1, source_target_pairs={{0,8},{8,16},{16,24},{24,32},{32,40},{40,48},{48,56},{56,64},{64,7... | collective-permute-start | bytes 1572872 | tf_op jit(solution)/shard_map/while/body/eval_jaxpr/ppermute | solution.py:16
  143.9 7.7 %copy-start.3 = (f32[1,16,64,128]{3,2,1,0:T(8,128)S(1)}, f32[1,16,64,128]{3,2,1,0:T(8,128)}, u32[]{:S(2)}) copy-start(f32[1,16,64,128]{3,2,1,0:T(8,128)} %copy-done.2) | copy-start | bytes 1572868 | tf_op jit(solution)/shard_map/while
  151.6 0.8 copy-start.2
  152.4 11.1 %collective-permute-start = (f32[1,16,64,128]{3,2,1,0:T(8,128)S(1)}, f32[1,16,64,128]{3,2,1,0:T(8,128)S(1)}, u32[]{:S(2)}, u32[]{:S(2)}) collective-permute-start(f32[1,16,64,128]{3,2,1,0:T(8,128)S(1)} %get-tuple-element.477), channel_id=1, source_target_pairs={{0,8},{8,16},{16,24},{24,32},{32,40},{40,48},{48,56},{56,64},{64,7... | collective-permute-start | bytes 1572872 | tf_op jit(solution)/shard_map/while/body/eval_jaxpr/ppermute | solution.py:16
  156.8 6.7 %copy-start.3 = (f32[1,16,64,128]{3,2,1,0:T(8,128)S(1)}, f32[1,16,64,128]{3,2,1,0:T(8,128)}, u32[]{:S(2)}) copy-start(f32[1,16,64,128]{3,2,1,0:T(8,128)} %copy-done.2) | copy-start | bytes 1572868 | tf_op jit(solution)/shard_map/while
  163.5 0.8 copy-start.2
  164.3 20.1 %collective-permute-start = (f32[1,16,64,128]{3,2,1,0:T(8,128)S(1)}, f32[1,16,64,128]{3,2,1,0:T(8,128)S(1)}, u32[]{:S(2)}, u32[]{:S(2)}) collective-permute-start(f32[1,16,64,128]{3,2,1,0:T(8,128)S(1)} %get-tuple-element.477), channel_id=1, source_target_pairs={{0,8},{8,16},{16,24},{24,32},{32,40},{40,48},{48,56},{56,64},{64,7... | collective-permute-start | bytes 1572872 | tf_op jit(solution)/shard_map/while/body/eval_jaxpr/ppermute | solution.py:16
  177.7 6.7 %copy-start.3 = (f32[1,16,64,128]{3,2,1,0:T(8,128)S(1)}, f32[1,16,64,128]{3,2,1,0:T(8,128)}, u32[]{:S(2)}) copy-start(f32[1,16,64,128]{3,2,1,0:T(8,128)} %copy-done.2) | copy-start | bytes 1572868 | tf_op jit(solution)/shard_map/while
  184.4 0.8 copy-start.2
  185.2 13.2 %collective-permute-start = (f32[1,16,64,128]{3,2,1,0:T(8,128)S(1)}, f32[1,16,64,128]{3,2,1,0:T(8,128)S(1)}, u32[]{:S(2)}, u32[]{:S(2)}) collective-permute-start(f32[1,16,64,128]{3,2,1,0:T(8,128)S(1)} %get-tuple-element.477), channel_id=1, source_target_pairs={{0,8},{8,16},{16,24},{24,32},{32,40},{40,48},{48,56},{56,64},{64,7... | collective-permute-start | bytes 1572872 | tf_op jit(solution)/shard_map/while/body/eval_jaxpr/ppermute | solution.py:16
  191.7 6.7 %copy-start.3 = (f32[1,16,64,128]{3,2,1,0:T(8,128)S(1)}, f32[1,16,64,128]{3,2,1,0:T(8,128)}, u32[]{:S(2)}) copy-start(f32[1,16,64,128]{3,2,1,0:T(8,128)} %copy-done.2) | copy-start | bytes 1572868 | tf_op jit(solution)/shard_map/while
  198.3 0.8 copy-start.2
  199.2 26.6 %collective-permute-start = (f32[1,16,64,128]{3,2,1,0:T(8,128)S(1)}, f32[1,16,64,128]{3,2,1,0:T(8,128)S(1)}, u32[]{:S(2)}, u32[]{:S(2)}) collective-permute-start(f32[1,16,64,128]{3,2,1,0:T(8,128)S(1)} %get-tuple-element.477), channel_id=1, source_target_pairs={{0,8},{8,16},{16,24},{24,32},{32,40},{40,48},{48,56},{56,64},{64,7... | collective-permute-start | bytes 1572872 | tf_op jit(solution)/shard_map/while/body/eval_jaxpr/ppermute | solution.py:16
  216.8 9.0 %copy-start.3 = (f32[1,16,64,128]{3,2,1,0:T(8,128)S(1)}, f32[1,16,64,128]{3,2,1,0:T(8,128)}, u32[]{:S(2)}) copy-start(f32[1,16,64,128]{3,2,1,0:T(8,128)} %copy-done.2) | copy-start | bytes 1572868 | tf_op jit(solution)/shard_map/while
  225.8 0.8 copy-start.2
  226.6 14.1 %collective-permute-start = (f32[1,16,64,128]{3,2,1,0:T(8,128)S(1)}, f32[1,16,64,128]{3,2,1,0:T(8,128)S(1)}, u32[]{:S(2)}, u32[]{:S(2)}) collective-permute-start(f32[1,16,64,128]{3,2,1,0:T(8,128)S(1)} %get-tuple-element.477), channel_id=1, source_target_pairs={{0,8},{8,16},{16,24},{24,32},{32,40},{40,48},{48,56},{56,64},{64,7... | collective-permute-start | bytes 1572872 | tf_op jit(solution)/shard_map/while/body/eval_jaxpr/ppermute | solution.py:16
  231.0 9.7 %copy-start.3 = (f32[1,16,64,128]{3,2,1,0:T(8,128)S(1)}, f32[1,16,64,128]{3,2,1,0:T(8,128)}, u32[]{:S(2)}) copy-start(f32[1,16,64,128]{3,2,1,0:T(8,128)} %copy-done.2) | copy-start | bytes 1572868 | tf_op jit(solution)/shard_map/while
  240.7 0.8 copy-start.2
  241.6 31.2 %collective-permute-start = (f32[1,16,64,128]{3,2,1,0:T(8,128)S(1)}, f32[1,16,64,128]{3,2,1,0:T(8,128)S(1)}, u32[]{:S(2)}, u32[]{:S(2)}) collective-permute-start(f32[1,16,64,128]{3,2,1,0:T(8,128)S(1)} %get-tuple-element.477), channel_id=1, source_target_pairs={{0,8},{8,16},{16,24},{24,32},{32,40},{40,48},{48,56},{56,64},{64,7... | collective-permute-start | bytes 1572872 | tf_op jit(solution)/shard_map/while/body/eval_jaxpr/ppermute | solution.py:16
  261.1 11.7 %copy-start.3 = (f32[1,16,64,128]{3,2,1,0:T(8,128)S(1)}, f32[1,16,64,128]{3,2,1,0:T(8,128)}, u32[]{:S(2)}) copy-start(f32[1,16,64,128]{3,2,1,0:T(8,128)} %copy-done.2) | copy-start | bytes 1572868 | tf_op jit(solution)/shard_map/while
  272.8 0.8 copy-start.2
  273.6 17.3 %collective-permute-start = (f32[1,16,64,128]{3,2,1,0:T(8,128)S(1)}, f32[1,16,64,128]{3,2,1,0:T(8,128)S(1)}, u32[]{:S(2)}, u32[]{:S(2)}) collective-permute-start(f32[1,16,64,128]{3,2,1,0:T(8,128)S(1)} %get-tuple-element.477), channel_id=1, source_target_pairs={{0,8},{8,16},{16,24},{24,32},{32,40},{40,48},{48,56},{56,64},{64,7... | collective-permute-start | bytes 1572872 | tf_op jit(solution)/shard_map/while/body/eval_jaxpr/ppermute | solution.py:16
  280.4 10.5 %copy-start.3 = (f32[1,16,64,128]{3,2,1,0:T(8,128)S(1)}, f32[1,16,64,128]{3,2,1,0:T(8,128)}, u32[]{:S(2)}) copy-start(f32[1,16,64,128]{3,2,1,0:T(8,128)} %copy-done.2) | copy-start | bytes 1572868 | tf_op jit(solution)/shard_map/while
  290.9 0.8 copy-start.2
  291.7 15.0 %collective-permute-start = (f32[1,16,64,128]{3,2,1,0:T(8,128)S(1)}, f32[1,16,64,128]{3,2,1,0:T(8,128)S(1)}, u32[]{:S(2)}, u32[]{:S(2)}) collective-permute-start(f32[1,16,64,128]{3,2,1,0:T(8,128)S(1)} %get-tuple-element.477), channel_id=1, source_target_pairs={{0,8},{8,16},{16,24},{24,32},{32,40},{40,48},{48,56},{56,64},{64,7... | collective-permute-start | bytes 1572872 | tf_op jit(solution)/shard_map/while/body/eval_jaxpr/ppermute | solution.py:16
  297.4 9.4 %copy-start.3 = (f32[1,16,64,128]{3,2,1,0:T(8,128)S(1)}, f32[1,16,64,128]{3,2,1,0:T(8,128)}, u32[]{:S(2)}) copy-start(f32[1,16,64,128]{3,2,1,0:T(8,128)} %copy-done.2) | copy-start | bytes 1572868 | tf_op jit(solution)/shard_map/while
  306.8 0.8 copy-start.2
  307.6 15.1 %collective-permute-start = (f32[1,16,64,128]{3,2,1,0:T(8,128)S(1)}, f32[1,16,64,128]{3,2,1,0:T(8,128)S(1)}, u32[]{:S(2)}, u32[]{:S(2)}) collective-permute-start(f32[1,16,64,128]{3,2,1,0:T(8,128)S(1)} %get-tuple-element.477), channel_id=1, source_target_pairs={{0,8},{8,16},{16,24},{24,32},{32,40},{40,48},{48,56},{56,64},{64,7... | collective-permute-start | bytes 1572872 | tf_op jit(solution)/shard_map/while/body/eval_jaxpr/ppermute | solution.py:16
  314.1 8.5 %copy-start.3 = (f32[1,16,64,128]{3,2,1,0:T(8,128)S(1)}, f32[1,16,64,128]{3,2,1,0:T(8,128)}, u32[]{:S(2)}) copy-start(f32[1,16,64,128]{3,2,1,0:T(8,128)} %copy-done.2) | copy-start | bytes 1572868 | tf_op jit(solution)/shard_map/while
  322.7 0.8 copy-start.2
  323.5 14.2 %collective-permute-start = (f32[1,16,64,128]{3,2,1,0:T(8,128)S(1)}, f32[1,16,64,128]{3,2,1,0:T(8,128)S(1)}, u32[]{:S(2)}, u32[]{:S(2)}) collective-permute-start(f32[1,16,64,128]{3,2,1,0:T(8,128)S(1)} %get-tuple-element.477), channel_id=1, source_target_pairs={{0,8},{8,16},{16,24},{24,32},{32,40},{40,48},{48,56},{56,64},{64,7... | collective-permute-start | bytes 1572872 | tf_op jit(solution)/shard_map/while/body/eval_jaxpr/ppermute | solution.py:16
  330.0 7.7 %copy-start.3 = (f32[1,16,64,128]{3,2,1,0:T(8,128)S(1)}, f32[1,16,64,128]{3,2,1,0:T(8,128)}, u32[]{:S(2)}) copy-start(f32[1,16,64,128]{3,2,1,0:T(8,128)} %copy-done.2) | copy-start | bytes 1572868 | tf_op jit(solution)/shard_map/while
  337.7 0.8 copy-start.2
  338.5 13.3 %collective-permute-start = (f32[1,16,64,128]{3,2,1,0:T(8,128)S(1)}, f32[1,16,64,128]{3,2,1,0:T(8,128)S(1)}, u32[]{:S(2)}, u32[]{:S(2)}) collective-permute-start(f32[1,16,64,128]{3,2,1,0:T(8,128)S(1)} %get-tuple-element.477), channel_id=1, source_target_pairs={{0,8},{8,16},{16,24},{24,32},{32,40},{40,48},{48,56},{56,64},{64,7... | collective-permute-start | bytes 1572872 | tf_op jit(solution)/shard_map/while/body/eval_jaxpr/ppermute | solution.py:16
  345.0 6.8 %copy-start.3 = (f32[1,16,64,128]{3,2,1,0:T(8,128)S(1)}, f32[1,16,64,128]{3,2,1,0:T(8,128)}, u32[]{:S(2)}) copy-start(f32[1,16,64,128]{3,2,1,0:T(8,128)} %copy-done.2) | copy-start | bytes 1572868 | tf_op jit(solution)/shard_map/while
  351.8 0.8 copy-start.2
  352.6 22.4 %collective-permute-start = (f32[1,16,64,128]{3,2,1,0:T(8,128)S(1)}, f32[1,16,64,128]{3,2,1,0:T(8,128)S(1)}, u32[]{:S(2)}, u32[]{:S(2)}) collective-permute-start(f32[1,16,64,128]{3,2,1,0:T(8,128)S(1)} %get-tuple-element.477), channel_id=1, source_target_pairs={{0,8},{8,16},{16,24},{24,32},{32,40},{40,48},{48,56},{56,64},{64,7... | collective-permute-start | bytes 1572872 | tf_op jit(solution)/shard_map/while/body/eval_jaxpr/ppermute | solution.py:16
  368.4 6.7 %copy-start.3 = (f32[1,16,64,128]{3,2,1,0:T(8,128)S(1)}, f32[1,16,64,128]{3,2,1,0:T(8,128)}, u32[]{:S(2)}) copy-start(f32[1,16,64,128]{3,2,1,0:T(8,128)} %copy-done.2) | copy-start | bytes 1572868 | tf_op jit(solution)/shard_map/while
  432.3 16.8 %copy-start.10 = (f32[4]{0:T(128)}, f32[4]{0:T(128)S(1)}, u32[]{:S(2)}) copy-start(f32[4]{0:T(128)S(1)} %get-tuple-element.375) | copy-start | bytes 52
  432.3 17.5 %copy-start.8 = (f32[4,2]{0,1:T(2,128)}, f32[4,2]{0,1:T(2,128)S(1)}, u32[]{:S(2)}) copy-start(f32[4,2]{0,1:T(2,128)S(1)} %get-tuple-element.374) | copy-start | bytes 100
  (2 other events, 1.3 us)
where the time goes:
time: 460 us; the launch traced here: 458 us
  starting transfers between devices  158 us (34%)
  waiting for transfers between devices  111 us (24%)
  blocking collectives  79.9 us (17%)
  other arithmetic  31.4 us (7%)
  local copies, waits for them, and re-layouts  31.3 us (7%)
  loops' own time  28.7 us (6%)
  matrix products  16.6 us (4%)
    ppermute x19, starting transfers between devices, from_behind(): return lax.ppermute(value, axis, pairs)  158 us
    ppermute x19, waiting for transfers between devices, from_behind(): return lax.ppermute(value, axis, pairs)  111 us
    psum x2, blocking collectives, over_axes(): value = lax.psum(value, axis)  57.3 us
    another operation x1, loops' own time, body(): lax.fori_loop(0, sections + groups - 1, section, initial)  23.5 us
    all_to_all x2, blocking collectives, from_everyone(): lax.all_to_all(jnp.broadcast_to(value[None], (length, *value.shape)), axi...  22.6 us
    reduce_sum x19, other arithmetic, amplitude(): jnp.sum(b_real * c_real - b_imag * c_imag, axis=(1, 2, 3)) * factor  18.4 us
    while x76, local copies, waits for them, and re-layouts  14.3 us
  transfers between devices with their start and end apart: 19, of which 19 were waited for; matrix products, arithmetic and copies ran while one was open for 5% of the time, Pallas kernels for 0%

commit v1 on v0

v1 whole, which is shorter than its diff:
```python
import math

import jax
import jax.numpy as jnp
from jax import lax
from jax.experimental import pallas as pl
from jax.experimental.pallas import tpu as pltpu
from jax.sharding import Mesh
from jax.sharding import PartitionSpec as P

AXES = ("s", "xp", "q", "yp", "z", "c")
GRID = ("s", "xp", "q", "yp")
NC = 8
NR = 8
W = 64
BLOCK = 4 * 2 * W + 8
BOARD = NR * W + 8
HALO = NC * W + 16
F32 = jnp.float32
BF16 = jnp.bfloat16


def vmem():
    return pl.BlockSpec(memory_space=pltpu.VMEM)


def smem():
    return pl.BlockSpec(memory_space=pltpu.SMEM)


def sign_row():
    lane = lax.broadcasted_iota(jnp.int32, (1, 2 * W), 1)
    return jnp.where(lane < W, -1.0, 1.0).astype(F32)


def times_i(x, sign):
    return pltpu.roll(x, W, 1) * sign


def pack_kernel(layout, assign, left, right, out):
    core = lax.axis_index("c")
    for t in range(4):
        row = jnp.full((1, 2 * W), assign[t, 0].astype(F32), F32)
        for dest in range(8):
            out[dest, pl.ds(8 * W + t, 1), :] = row
    for dest in range(8):
        out[dest, pl.ds(8 * W + 4, 4), :] = jnp.zeros((4, 2 * W), F32)
    for half in range(2):
        for k in range(4):
            kind = layout[(1 - half) * NR + 4 * core + k, 0]
            a = left[0, kind].astype(F32)
            b = right[0, kind].astype(F32)
            for xp in range(2):
                for yp in range(2):
                    dest = 4 * xp + 2 * half + yp
                    out[dest, pl.ds(2 * W * k, W), :] = a
                    out[dest, pl.ds(2 * W * k + W, W), :] = b


def unpack_gates(mine, other, lefts, rights, core, sign):
    def place(j, unused):
        for source, part in ((mine, core), (other, 1 - core)):
            for k in range(4):
                row = 4 * part + k
                lefts[j, row] = source[j, pl.ds(2 * W * k, W), :].astype(BF16)
                r = source[j, pl.ds(2 * W * k + W, W), :]
                rights[j, row, pl.ds(0, W), :] = r.astype(BF16)
                rights[j, row, pl.ds(W, W), :] = times_i(r, sign).astype(BF16)
        return unused

    lax.fori_loop(0, NC, place, 0)


def halves(x):
    high = x.astype(BF16)
    return high, (x - high.astype(F32)).astype(BF16)


def sweep(state, lefts, rights, mine, cosine, sine, halo_in, halo_out, peaks, own, start, sign):
    p0, mix0, rho0 = start

    def column(j, carry):
        p, rho_mix, rho = carry
        value = mine[j, pl.ds(8 * W + own, 1), :]
        cos_row = jnp.zeros((1, 2 * W), F32)
        sin_row = jnp.zeros((1, 2 * W), F32)
        for v in range(4):
            hit = value == float(v)
            cos_row = jnp.where(hit, cosine[pl.ds(v, 1), :], cos_row)
            sin_row = jnp.where(hit, sine[pl.ds(v, 1), :], sin_row)
        scale = 1.0 / p
        cos_row = cos_row * scale
        sin_row = sin_row * scale
        boards = [state[k] for k in range(NR)]
        halo_out[pl.ds(pl.multiple_of(j * W, W), W), :] = boards[0]
        if halo_in is None:
            below = None
        else:
            below = halo_in[pl.ds(pl.multiple_of(j * W, W), W), :] * rho_mix
        top = jnp.zeros((8, 2 * W), F32)
        for k in range(NR):
            after = boards[k + 1] if k + 1 < NR else below
            mixed = boards[k] if after is None else boards[k] + 0.5 * after
            turn = times_i(mixed, sign)
            mh, ml = halves(mixed)
            th, tl = halves(turn)
            gate = lefts[j, k]
            middle = jnp.dot(
                jnp.concatenate([gate, gate], 1),
                jnp.concatenate([mh, th, ml, tl], 0),
                preferred_element_type=F32,
            )
            dh, dl = halves(middle)
            right = rights[j, k]
            out = jnp.dot(
                jnp.concatenate([dh, dl], 1),
                jnp.concatenate([right, right], 0),
                preferred_element_type=F32,
            )
            out = out * cos_row + pltpu.roll(out, W, 1) * sin_row
            state[k] = out
            for g in range(8):
                top = jnp.maximum(top, jnp.abs(out[8 * g : 8 * g + 8]))
        own_top = jnp.broadcast_to(jnp.max(top, keepdims=True), (1, 2 * W))
        halo_out[pl.ds(NC * W + j, 1), :] = own_top
        if halo_in is None:
            other_top = jnp.zeros((1, 2 * W), F32)
        else:
            other_top = halo_in[pl.ds(NC * W + j, 1), :]
        p_new = jnp.maximum(jnp.maximum(own_top, other_top * rho), 1.0)
        peaks[pl.ds(j, 1), :] = p_new
        return (p_new, rho, rho * jnp.maximum(other_top, 1.0) / p_new)

    return lax.fori_loop(0, NC, column, (p0, mix0, rho0))


def close_sums(state, close, base, sign):
    real = jnp.zeros((8, 2 * W), F32)
    imag = jnp.zeros((8, 2 * W), F32)
    for k in range(NR):
        c = close[base + k]
        b = state[k]
        d = pltpu.roll(c, W, 1)
        for g in range(8):
            part = slice(8 * g, 8 * g + 8)
            real = real - b[part] * c[part] * sign
            imag = imag + b[part] * d[part]
    return jnp.sum(real, keepdims=True), jnp.sum(imag, keepdims=True)


def write_messages(state, board_out, halo_out, peaks, ell, end, sums):
    p, rho_mix, rho = end
    for k in range(NR):
        board_out[pl.ds(k * W, W), :] = state[k]
    board_out[pl.ds(NR * W, 1), :] = p
    board_out[pl.ds(NR * W + 1, 1), :] = rho_mix
    board_out[pl.ds(NR * W + 2, 1), :] = rho
    board_out[pl.ds(NR * W + 3, 1), :] = ell + jnp.sum(jnp.log(peaks[...]), axis=0, keepdims=True)
    board_out[pl.ds(NR * W + 4, 4), :] = jnp.zeros((4, 2 * W), F32)
    halo_out[pl.ds(NC * W + 8, 8), :] = jnp.zeros((8, 2 * W), F32)
    if sums is not None:
        halo_out[pl.ds(NC * W + 8, 1), :] = jnp.broadcast_to(sums[0], (1, 2 * W))
        halo_out[pl.ds(NC * W + 9, 1), :] = jnp.broadcast_to(sums[1], (1, 2 * W))


def places():
    s, q = lax.axis_index("s"), lax.axis_index("q")
    i = jnp.where(s == 0, lax.axis_index("xp"), 1 - lax.axis_index("xp"))
    j = jnp.where(q == 0, lax.axis_index("yp"), 1 - lax.axis_index("yp"))
    return s, q, 2 * i + j, (1 - q) * NR


def first_kernel(mine, other, edge, cosine, sine, lefts, rights, board_out, halo_out, state, peaks):
    s, q, own, base = places()
    sign = sign_row()
    one = jnp.ones((1, 2 * W), F32)
    unpack_gates(mine, other, lefts, rights, lax.axis_index("c"), sign)
    for k in range(NR):
        state[k] = edge[base + k].astype(F32)
    end = sweep(
        state, lefts, rights, mine, cosine, sine, None, halo_out, peaks, own, (one, one, one), sign
    )
    write_messages(state, board_out, halo_out, peaks, 0.0 * one, end, None)


def load_state(state, edge, board_in, base, s):
    one = jnp.ones((1, 2 * W), F32)
    first = s == 0
    for k in range(NR):
        state[k] = jnp.where(first, edge[base + k].astype(F32), board_in[pl.ds(k * W, W), :])
    row = lambda n: board_in[pl.ds(NR * W + n, 1), :]
    p = jnp.maximum(jnp.where(first, one, row(0)), 1.0)
    rho_mix = jnp.where(first, one, row(1))
    rho = jnp.where(first, one, row(2))
    ell = jnp.where(first, 0.0 * one, row(3))
    return (p, rho_mix, rho), ell


def second_kernel(mine, edge, cosine, sine, lefts, rights, close, board_in, halo_in, board_out, halo_out, state, peaks):
    s, q, own, base = places()
    sign = sign_row()
    start, ell = load_state(state, edge, board_in, base, s)
    end = sweep(
        state, lefts, rights, mine, cosine, sine, halo_in, halo_out, peaks, own, start, sign
    )
    write_messages(
        state, board_out, halo_out, peaks, ell, end, close_sums(state, close, base, sign)
    )


def third_kernel(mine, edge, cosine, sine, lefts, rights, close, board_in, halo_in, out, state, peaks, halo_out):
    s, q, own, base = places()
    sign = sign_row()
    start, ell = load_state(state, edge, board_in, base, s)
    p, rho_mix, rho = sweep(
        state, lefts, rights, mine, cosine, sine, halo_in, halo_out, peaks, own, start, sign
    )
    ell = ell + jnp.sum(jnp.log(peaks[...]), axis=0, keepdims=True)
    real, imag = close_sums(state, close, base, sign)
    factor = 1.0 / math.sqrt(2 * NR * W * W)
    real = (real + rho_mix * halo_in[pl.ds(NC * W + 8, 1), :]) / p * factor
    imag = (imag + rho_mix * halo_in[pl.ds(NC * W + 9, 1), :]) / p * factor
    index = 4 * (2 * lax.axis_index("z") + lax.axis_index("c")) + own
    lane = lax.broadcasted_iota(jnp.int32, (1, 2 * W), 1)
    index = jnp.where(jnp.logical_and(s == 1, q == 1), index, -1)
    hit = lane == index
    zero = jnp.zeros((1, 2 * W), F32)
    out[pl.ds(0, 1), :] = jnp.where(hit, real, zero)
    out[pl.ds(1, 1), :] = jnp.where(hit, imag, zero)
    out[pl.ds(2, 1), :] = jnp.where(hit, ell, zero)
    out[pl.ds(3, 5), :] = jnp.zeros((5, 2 * W), F32)


def call(kernel, outs, scratch, args, specs=None):
    return pl.pallas_call(
        kernel,
        out_shape=outs,
        in_specs=specs or [vmem()] * len(args),
        out_specs=jax.tree.map(lambda _: vmem(), outs),
        scratch_shapes=scratch,
        compiler_params=pltpu.CompilerParams(vmem_limit_bytes=48 * 2**20),
    )(*args)


def shape(*dims, dtype=F32):
    return jax.ShapeDtypeStruct(dims, dtype)


def chip(s, xp, q, yp):
    return 8 * s + 4 * xp + 2 * q + yp


def along_columns(value, q):
    pairs = [(chip(0, xp, q, yp), chip(1, 1 - xp, q, yp)) for xp in range(2) for yp in range(2)]
    return lax.ppermute(value, GRID, pairs)


def along_rows(value, s):
    pairs = [(chip(s, xp, 0, yp), chip(s, xp, 1, 1 - yp)) for xp in range(2) for yp in range(2)]
    return lax.ppermute(value, GRID, pairs)


def around(value, axis):
    length = lax.axis_size(axis)
    total = value
    for by in range(1, length):
        pairs = [(i, (i + by) % length) for i in range(length)]
        total = total + lax.ppermute(value, axis, pairs)
    return total


def body(layout, assign, edge, gate_left, gate_right, phase_angle, close):
    cosine, sine = jnp.cos(phase_angle), jnp.sin(phase_angle)
    cosine = jnp.concatenate([cosine, cosine], -1)
    sine = jnp.concatenate([-sine, sine], -1)
    packed = call(
        pack_kernel,
        shape(8, BLOCK, 2 * W),
        [],
        (layout, assign, gate_left, gate_right),
        [smem(), smem(), vmem(), vmem()],
    )
    mine = lax.all_to_all(packed, ("xp", "q", "yp"), 0, 0, tiled=True)
    other = lax.ppermute(mine, "c", [(0, 1), (1, 0)])
    state = pltpu.VMEM((NR, W, 2 * W), F32)
    peaks = pltpu.VMEM((NC, 2 * W), F32)
    lefts, rights, board, halo = call(
        first_kernel,
        (
            shape(NC, NR, W, 2 * W, dtype=BF16),
            shape(NC, NR, 2 * W, 2 * W, dtype=BF16),
            shape(BOARD, 2 * W),
            shape(HALO, 2 * W),
        ),
        [state, peaks],
        (mine, other, edge, cosine, sine),
    )
    board, halo = along_columns(board, 0), along_rows(halo, 0)
    board, halo = call(
        second_kernel,
        (shape(BOARD, 2 * W), shape(HALO, 2 * W)),
        [state, peaks],
        (mine, edge, cosine, sine, lefts, rights, close, board, halo),
    )
    board, halo = along_columns(board, 1), along_rows(halo, 1)
    found = call(
        third_kernel,
        shape(8, 2 * W),
        [state, peaks, pltpu.VMEM((HALO, 2 * W), F32)],
        (mine, edge, cosine, sine, lefts, rights, close, board, halo),
    )
    for axis in ("c", ("s", "xp"), ("q", "yp"), "z"):
        found = around(found, axis)
    logs = found[2, :32]
    top_log = jnp.max(logs)
    total_amp = jnp.sum(found[:2, :32] * jnp.exp(logs - top_log)[None], axis=1)
    at = 4 * (2 * lax.axis_index("z") + lax.axis_index("c"))
    here = lax.dynamic_slice_in_dim(found, at, 4, 1)
    return (here[:2].T, here[2], total_amp, top_log)


def solution(mesh):
    split = Mesh(mesh.devices.reshape(2, 2, 2, 2, 4, 2), AXES)
    placed = (
        P(None, GRID),
        P(("z", "c"), GRID),
        P(),
        P(GRID, None, None, None),
        P(GRID, None, None, None),
        P(),
        P(),
    )
    return jax.shard_map(
        body,
        mesh=split,
        in_specs=placed,
        out_specs=(P(("z", "c"), None), P(("z", "c")), P(), P()),
        check_vma=False,
    )
```

time: 460 us -> 114 us (0.25)
  starting transfers between devices: 158 us -> 28.9 us
  waiting for transfers between devices: 111 us -> 19.9 us
  blocking collectives: 79.9 us -> 33.2 us
  other arithmetic: 31.4 us -> 1.98 us
  loops' own time: 28.7 us -> 0 us
  local copies, waits for them, and re-layouts: 31.3 us -> 5.9 us
  Pallas kernels: 0 us -> 23.2 us
  matrix products: 16.6 us -> 0 us
    ppermute x19 -> x15, starting transfers between devices: 158 us -> 28.9 us  [the longest x10 23.1 us: around(): total = total + lax.ppermute(value, axis, pairs)]
    ppermute x19 -> x15, waiting for transfers between devices: 111 us -> 19.9 us  [the longest x10 9.95 us: around(): total = total + lax.ppermute(value, axis, pairs)]
    psum x2 -> x0, blocking collectives: 57.3 us -> none  [over_axes(): value = lax.psum(value, axis)]
    another operation x20 -> x0, loops' own time: 28.7 us -> none  [the longest x1 23.5 us: body(): lax.fori_loop(0, sections + groups - 1, section, initial)]
    pallas_call x0 -> x4, Pallas kernels: none -> 23.2 us  [call(): pl.pallas_call(kernel, out_shape=outs, in_specs=specs or [vmem()] * len(a...]
    reduce_sum x21 -> x1, other arithmetic: 19.1 us -> 0.63 us  [body(): total_amp = jnp.sum(found[:2, :32] * jnp.exp(logs - top_log)[None], axis=1)]
    dot_general x22 -> x0, matrix products: 16.6 us -> none  [the longest x4 4.19 us: sweep_column(): jnp.einsum('rpka,srab->srkpb', left_four, mixed, precision=lax.Precision....]
    while x78 -> x0, local copies, waits for them, and re-layouts: 15.4 us -> none
  transfers between devices with their start and end apart: 19 -> 15, of which waited for: 19 -> 9; matrix products, arithmetic and copies ran while one was open for 5% -> 0% of each run, Pallas kernels for 0% -> 0%
where the time goes in v1:
time: 114 us
  blocking collectives  33.2 us (29%)
  starting transfers between devices  28.9 us (25%)
  Pallas kernels  23.2 us (20%)
  waiting for transfers between devices  19.9 us (17%)
  local copies, waits for them, and re-layouts  5.9 us (5%)
  other arithmetic  1.98 us (2%)
    all_to_all x1, blocking collectives, body(): mine = lax.all_to_all(packed, ('xp', 'q', 'yp'), 0, 0, tiled=True)  33.2 us
    pallas_call x4, Pallas kernels, call(): pl.pallas_call(kernel, out_shape=outs, in_specs=specs or [vmem()] * len(a...  23.2 us
    ppermute x10, starting transfers between devices, around(): total = total + lax.ppermute(value, axis, pairs)  23.1 us
    ppermute x10, waiting for transfers between devices, around(): total = total + lax.ppermute(value, axis, pairs)  9.95 us
    ppermute x2, waiting for transfers between devices, along_columns(): return lax.ppermute(value, GRID, pairs)  5.92 us
    unnamed x16, local copies, waits for them, and re-layouts  4.71 us
    ppermute x1, waiting for transfers between devices, body(): other = lax.ppermute(mine, 'c', [(0, 1), (1, 0)])  4.07 us
    ppermute x2, starting transfers between devices, along_rows(): return lax.ppermute(value, GRID, pairs)  3.77 us
  transfers between devices with their start and end apart: 15, of which 9 were waited for; matrix products, arithmetic and copies ran while one was open for 0% of the time, Pallas kernels for 0%

profile of v1, /device:TPU:0, one launch (start us, length us, event | category | flops | bytes accessed | tf_op | source)
XLA Modules:
  0.0 113.9 jit_solution(2217278310623835023)
XLA Ops:
  0.6 0.7 copy.11.layout
  1.4 0.7 copy.12.assign
  2.1 0.0 copy-start.3
  2.1 0.9 copy-done.3
  3.1 0.0 copy-start.4
  3.1 0.9 copy-done.4
  4.0 0.8 shard_map.102
  4.9 0.0 copy-start.6
  4.9 0.0 copy-start.1
  4.9 33.2 %all_to_all.5.mine = f32[8,520,128]{2,1,0:T(8,128)S(1)} all-to-all(f32[8,520,128]{2,1,0:T(8,128)S(1)} %shard_map.102), channel_id=1, replica_groups=mesh['s'=2,'xp'=2,'q'=2,'yp'=2,'z'=4,'c'=2] {'xp','q','yp'}, dimensions={0} | all-to-all | bytes 4259840 | tf_op jit(solution)/shard_map/all_to_all | solution.py:283
  38.1 0.0 copy-start
  38.1 0.0 collective-permute-start
  38.1 0.0 copy-done.6
  38.2 0.1 pad_maximum_fusion
  38.3 4.1 %collective-permute-done.other = f32[8,520,128]{2,1,0:T(8,128)S(1)} collective-permute-done((f32[8,520,128]{2,1,0:T(8,128)S(1)}, f32[8,520,128]{2,1,0:T(8,128)S(1)}, u32[]{:S(2)}, u32[]{:S(2)}) %collective-permute-start) | collective-permute-done | bytes 2129952 | tf_op jit(solution)/shard_map/ppermute | solution.py:284
  42.3 0.0 copy-start.5
  42.3 1.3 %copy-done.5 = f32[8,520,128]{2,1,0:T(8,128)} copy-done((f32[8,520,128]{2,1,0:T(8,128)}, f32[8,520,128]{2,1,0:T(8,128)S(1)}, u32[]{:S(2)}) %copy-start.5) | copy-done | bytes 2129944
  43.6 0.0 copy-done.1
  43.7 0.0 copy-start.2
  43.7 8.1 %shard_map.103 = (bf16[8,8,64,128]{3,2,1,0:T(8,128)(2,1)S(1)}, bf16[8,8,128,128]{3,2,1,0:T(8,128)(2,1)S(1)}, f32[520,128]{1,0:T(8,128)S(1)}, f32[528,128]{1,0:T(8,128)S(1)}) custom-call(f32[8,520,128]{2,1,0:T(8,128)S(1)} %all_to_all.5.mine, f32[8,520,128]{2,1,0:T(8,128)} %copy-done.5, bf16[16,64,128]{2,1,0:T(8,128)(2,1)S(1)} %copy-done.1, ...), custom_call_target="tpu_custom_call" | custom-call | tf_op jit(solution)/shard_map/pallas_call | solution.py:235
  51.8 0.0 copy-done
  51.8 3.1 %collective-permute-start.2 = (f32[528,128]{1,0:T(8,128)S(1)}, f32[528,128]{1,0:T(8,128)S(1)}, u32[]{:S(2)}, u32[]{:S(2)}) collective-permute-start(f32[528,128]{1,0:T(8,128)S(1)} %get-tuple-element.13), channel_id=1, source_target_pairs={{0,24},{8,16},{32,56},{40,48},{1,25},{9,17},{33,57},{41,49},{2,26}... | collective-permute-start | bytes 811016 | tf_op jit(solution)/shard_map/ppermute | solution.py:260
  54.9 1.3 %collective-permute-start.1 = (f32[520,128]{1,0:T(8,128)S(1)}, f32[520,128]{1,0:T(8,128)S(1)}, u32[]{:S(2)}, u32[]{:S(2)}) collective-permute-start(f32[520,128]{1,0:T(8,128)S(1)} %get-tuple-element.12), channel_id=1, source_target_pairs={{0,96},{8,104},{32,64},{40,72},{1,97},{9,105},{33,65},{41,73},{2,9... | collective-permute-start | bytes 798728 | tf_op jit(solution)/shard_map/ppermute | solution.py:255
  56.2 5.9 %collective-permute-done.1.board_in = f32[520,128]{1,0:T(8,128)S(1)} collective-permute-done((f32[520,128]{1,0:T(8,128)S(1)}, f32[520,128]{1,0:T(8,128)S(1)}, u32[]{:S(2)}, u32[]{:S(2)}) %collective-permute-start.1) | collective-permute-done | bytes 266272 | tf_op jit(solution)/shard_map/ppermute | solution.py:255
  62.2 0.0 collective-permute-done.2.halo_in
  62.2 0.0 copy-done.2
  62.2 7.1 %shard_map.104 = (f32[520,128]{1,0:T(8,128)S(1)}, f32[528,128]{1,0:T(8,128)S(1)}) custom-call(f32[8,520,128]{2,1,0:T(8,128)} %copy-done, bf16[16,64,128]{2,1,0:T(8,128)(2,1)S(1)} %copy-done.1, f32[4,128]{1,0:T(4,128)S(1)} %get-tuple-element.18.cosine, f32[4,128]{1,0:T(4,128)S(1)} %get-tuple-element.19.sine, ...), custom_call_target="tpu_custom_call" | custom-call | tf_op jit(solution)/shard_map/pallas_call | solution.py:235
  69.3 0.7 collective-permute-start.4
  70.0 0.7 collective-permute-start.3
  70.7 0.0 collective-permute-done.3.board_in
  70.7 0.0 collective-permute-done.4.halo_in
  70.7 7.1 %shard_map.105 = f32[8,128]{1,0:T(8,128)S(1)} custom-call(f32[8,520,128]{2,1,0:T(8,128)} %copy-done, bf16[16,64,128]{2,1,0:T(8,128)(2,1)S(1)} %copy-done.1, f32[4,128]{1,0:T(4,128)S(1)} %get-tuple-element.18.cosine, f32[4,128]{1,0:T(4,128)S(1)} %get-tuple-element.19.sine, bf16[8,8,64,128]{3,2,1,0:T(8,128)(2,1)S(1)} %get-tuple-element.10.lefts, ...), custom_call_target="tpu_custom_call" | custom-call | tf_op jit(solution)/shard_map/pallas_call | solution.py:235
  77.8 0.1 collective-permute-start.5
  77.9 1.2 %collective-permute-done.5 = f32[8,128]{1,0:T(8,128)S(1)} collective-permute-done((f32[8,128]{1,0:T(8,128)S(1)}, f32[8,128]{1,0:T(8,128)S(1)}, u32[]{:S(2)}, u32[]{:S(2)}) %collective-permute-start.5) | collective-permute-done | bytes 4128 | tf_op jit(solution)/shard_map/ppermute | solution.py:268
  79.1 0.9 collective-permute-start.6
  79.9 9.6 %collective-permute-start.7 = (f32[8,128]{1,0:T(8,128)S(1)}, f32[8,128]{1,0:T(8,128)S(1)}, u32[]{:S(2)}, u32[]{:S(2)}) collective-permute-start(f32[8,128]{1,0:T(8,128)S(1)} %add.36), channel_id=1, source_target_pairs={{0,64},{32,96},{64,0},{96,32},{1,65},{33,97},{65,1},{97,33},{2,66}... | collective-permute-start | bytes 12296 | tf_op jit(solution)/shard_map/ppermute | solution.py:268
  89.6 0.9 collective-permute-start.8
  90.5 0.0 collective-permute-done.6
  90.5 0.7 collective-permute-done.7
  91.2 2.0 %collective-permute-done.8 = f32[8,128]{1,0:T(8,128)S(1)} collective-permute-done((f32[8,128]{1,0:T(8,128)S(1)}, f32[8,128]{1,0:T(8,128)S(1)}, u32[]{:S(2)}, u32[]{:S(2)}) %collective-permute-start.8) | collective-permute-done | bytes 4128 | tf_op jit(solution)/shard_map/ppermute | solution.py:268
  93.2 3.1 %collective-permute-start.10 = (f32[8,128]{1,0:T(8,128)S(1)}, f32[8,128]{1,0:T(8,128)S(1)}, u32[]{:S(2)}, u32[]{:S(2)}) collective-permute-start(f32[8,128]{1,0:T(8,128)S(1)} %add_add_fusion.2), channel_id=1, source_target_pairs={{0,16},{8,24},{16,0},{24,8},{1,17},{9,25},{17,1},{25,9},{2,18},{10... | collective-permute-start | bytes 12296 | tf_op jit(solution)/shard_map/ppermute | solution.py:268
  96.3 0.7 collective-permute-start.11
  97.0 1.4 %collective-permute-start.9 = (f32[8,128]{1,0:T(8,128)S(1)}, f32[8,128]{1,0:T(8,128)S(1)}, u32[]{:S(2)}, u32[]{:S(2)}) collective-permute-start(f32[8,128]{1,0:T(8,128)S(1)} %add_add_fusion.2), channel_id=1, source_target_pairs={{0,8},{8,16},{16,24},{24,0},{1,9},{9,17},{17,25},{25,1},{2,10},{10... | collective-permute-start | bytes 12296 | tf_op jit(solution)/shard_map/ppermute | solution.py:268
  98.3 0.0 collective-permute-done.10
  98.3 1.6 %collective-permute-done.11 = f32[8,128]{1,0:T(8,128)S(1)} collective-permute-done((f32[8,128]{1,0:T(8,128)S(1)}, f32[8,128]{1,0:T(8,128)S(1)}, u32[]{:S(2)}, u32[]{:S(2)}) %collective-permute-start.11) | collective-permute-done | bytes 4128 | tf_op jit(solution)/shard_map/ppermute | solution.py:268
  99.9 1.9 %collective-permute-done.9 = f32[8,128]{1,0:T(8,128)S(1)} collective-permute-done((f32[8,128]{1,0:T(8,128)S(1)}, f32[8,128]{1,0:T(8,128)S(1)}, u32[]{:S(2)}, u32[]{:S(2)}) %collective-permute-start.9) | collective-permute-done | bytes 4128 | tf_op jit(solution)/shard_map/ppermute | solution.py:268
  101.8 1.9 %collective-permute-start.12 = (f32[8,128]{1,0:T(8,128)S(1)}, f32[8,128]{1,0:T(8,128)S(1)}, u32[]{:S(2)}, u32[]{:S(2)}) collective-permute-start(f32[8,128]{1,0:T(8,128)S(1)} %add_add_fusion.1), channel_id=1, source_target_pairs={{0,2},{2,4},{4,6},{6,0},{1,3},{3,5},{5,7},{7,1},{8,10},{10,12},{12... | collective-permute-start | bytes 12296 | tf_op jit(solution)/shard_map/ppermute | solution.py:268
  103.7 3.6 %collective-permute-start.13 = (f32[8,128]{1,0:T(8,128)S(1)}, f32[8,128]{1,0:T(8,128)S(1)}, u32[]{:S(2)}, u32[]{:S(2)}) collective-permute-start(f32[8,128]{1,0:T(8,128)S(1)} %add_add_fusion.1), channel_id=1, source_target_pairs={{0,4},{2,6},{4,0},{6,2},{1,5},{3,7},{5,1},{7,3},{8,12},{10,14},{12... | collective-permute-start | bytes 12296 | tf_op jit(solution)/shard_map/ppermute | solution.py:268
  107.3 1.0 collective-permute-start.14
  108.3 0.0 collective-permute-done.12
  108.3 0.6 collective-permute-done.13
  108.9 2.0 %collective-permute-done.14 = f32[8,128]{1,0:T(8,128)S(1)} collective-permute-done((f32[8,128]{1,0:T(8,128)S(1)}, f32[8,128]{1,0:T(8,128)S(1)}, u32[]{:S(2)}, u32[]{:S(2)}) %collective-permute-start.14) | collective-permute-done | bytes 4128 | tf_op jit(solution)/shard_map/ppermute | solution.py:268
  110.9 0.6 slice_reduce_fusion
  111.5 0.1 constant_dynamic-slice_fusion
  111.6 0.6 slice_bitcast_fusion
  112.2 0.5 slice_bitcast_fusion.1
  112.7 0.7 exponential_bitcast_fusion
  113.3 0.6 multiply_reduce_fusion
  (6 shorter events, 0.1 us)
Async XLA Ops:
  2.1 0.9 copy-start.3
  3.1 0.9 copy-start.4
  4.9 33.3 %copy-start.6 = (f32[4,64]{1,0:T(4,128)S(1)}, f32[4,64]{1,0:T(4,128)}, u32[]{:S(2)}) copy-start(f32[4,64]{1,0:T(4,128)} %param.12) | copy-start | bytes 3076
  4.9 38.8 %copy-start.1 = (bf16[16,64,128]{2,1,0:T(8,128)(2,1)S(1)}, bf16[16,64,128]{2,1,0:T(8,128)(2,1)}, u32[]{:S(2)}) copy-start(bf16[16,64,128]{2,1,0:T(8,128)(2,1)} %edge.5) | copy-start | bytes 786436
  38.1 13.7 %copy-start = (f32[8,520,128]{2,1,0:T(8,128)}, f32[8,520,128]{2,1,0:T(8,128)S(1)}, u32[]{:S(2)}) copy-start(f32[8,520,128]{2,1,0:T(8,128)S(1)} %all_to_all.5.mine) | copy-start | bytes 6389764
  38.1 4.2 %collective-permute-start = (f32[8,520,128]{2,1,0:T(8,128)S(1)}, f32[8,520,128]{2,1,0:T(8,128)S(1)}, u32[]{:S(2)}, u32[]{:S(2)}) collective-permute-start(f32[8,520,128]{2,1,0:T(8,128)S(1)} %all_to_all.5.mine), channel_id=1, source_target_pairs={{0,1},{1,0},{2,3},{3,2},{4,5},{5,4},{6,7},{7,6},{8,9},{9,8},{10,11... | collective-permute-start | bytes 6389768 | tf_op jit(solution)/shard_map/ppermute | solution.py:284
  42.3 1.3 %copy-start.5 = (f32[8,520,128]{2,1,0:T(8,128)}, f32[8,520,128]{2,1,0:T(8,128)S(1)}, u32[]{:S(2)}) copy-start(f32[8,520,128]{2,1,0:T(8,128)S(1)} %collective-permute-done.other) | copy-start | bytes 6389764
  43.7 18.5 %copy-start.2 = (f32[16,64,128]{2,1,0:T(8,128)S(1)}, f32[16,64,128]{2,1,0:T(8,128)}, u32[]{:S(2)}) copy-start(f32[16,64,128]{2,1,0:T(8,128)} %close.3) | copy-start | bytes 1572868
  51.8 10.4 %collective-permute-start.2 = (f32[528,128]{1,0:T(8,128)S(1)}, f32[528,128]{1,0:T(8,128)S(1)}, u32[]{:S(2)}, u32[]{:S(2)}) collective-permute-start(f32[528,128]{1,0:T(8,128)S(1)} %get-tuple-element.13), channel_id=1, source_target_pairs={{0,24},{8,16},{32,56},{40,48},{1,25},{9,17},{33,57},{41,49},{2,26}... | collective-permute-start | bytes 811016 | tf_op jit(solution)/shard_map/ppermute | solution.py:260
  54.9 7.3 %collective-permute-start.1 = (f32[520,128]{1,0:T(8,128)S(1)}, f32[520,128]{1,0:T(8,128)S(1)}, u32[]{:S(2)}, u32[]{:S(2)}) collective-permute-start(f32[520,128]{1,0:T(8,128)S(1)} %get-tuple-element.12), channel_id=1, source_target_pairs={{0,96},{8,104},{32,64},{40,72},{1,97},{9,105},{33,65},{41,73},{2,9... | collective-permute-start | bytes 798728 | tf_op jit(solution)/shard_map/ppermute | solution.py:255
  69.3 1.4 %collective-permute-start.4 = (f32[528,128]{1,0:T(8,128)S(1)}, f32[528,128]{1,0:T(8,128)S(1)}, u32[]{:S(2)}, u32[]{:S(2)}) collective-permute-start(f32[528,128]{1,0:T(8,128)S(1)} %get-tuple-element.15), channel_id=1, source_target_pairs={{64,88},{72,80},{96,120},{104,112},{65,89},{73,81},{97,121},{105,1... | collective-permute-start | bytes 811016 | tf_op jit(solution)/shard_map/ppermute | solution.py:260
  70.0 0.7 collective-permute-start.3
  77.8 1.2 %collective-permute-start.5 = (f32[8,128]{1,0:T(8,128)S(1)}, f32[8,128]{1,0:T(8,128)S(1)}, u32[]{:S(2)}, u32[]{:S(2)}) collective-permute-start(f32[8,128]{1,0:T(8,128)S(1)} %shard_map.105), channel_id=1, source_target_pairs={{0,1},{1,0},{2,3},{3,2},{4,5},{5,4},{6,7},{7,6},{8,9},{9,8},{10,11... | collective-permute-start | bytes 12296 | tf_op jit(solution)/shard_map/ppermute | solution.py:268
  79.1 11.4 %collective-permute-start.6 = (f32[8,128]{1,0:T(8,128)S(1)}, f32[8,128]{1,0:T(8,128)S(1)}, u32[]{:S(2)}, u32[]{:S(2)}) collective-permute-start(f32[8,128]{1,0:T(8,128)S(1)} %add.36), channel_id=1, source_target_pairs={{0,32},{32,64},{64,96},{96,0},{1,33},{33,65},{65,97},{97,1},{2,34}... | collective-permute-start | bytes 12296 | tf_op jit(solution)/shard_map/ppermute | solution.py:268
  79.9 11.3 %collective-permute-start.7 = (f32[8,128]{1,0:T(8,128)S(1)}, f32[8,128]{1,0:T(8,128)S(1)}, u32[]{:S(2)}, u32[]{:S(2)}) collective-permute-start(f32[8,128]{1,0:T(8,128)S(1)} %add.36), channel_id=1, source_target_pairs={{0,64},{32,96},{64,0},{96,32},{1,65},{33,97},{65,1},{97,33},{2,66}... | collective-permute-start | bytes 12296 | tf_op jit(solution)/shard_map/ppermute | solution.py:268
  89.6 3.6 %collective-permute-start.8 = (f32[8,128]{1,0:T(8,128)S(1)}, f32[8,128]{1,0:T(8,128)S(1)}, u32[]{:S(2)}, u32[]{:S(2)}) collective-permute-start(f32[8,128]{1,0:T(8,128)S(1)} %add.36), channel_id=1, source_target_pairs={{0,96},{32,0},{64,32},{96,64},{1,97},{33,1},{65,33},{97,65},{2,98}... | collective-permute-start | bytes 12296 | tf_op jit(solution)/shard_map/ppermute | solution.py:268
  93.2 5.1 %collective-permute-start.10 = (f32[8,128]{1,0:T(8,128)S(1)}, f32[8,128]{1,0:T(8,128)S(1)}, u32[]{:S(2)}, u32[]{:S(2)}) collective-permute-start(f32[8,128]{1,0:T(8,128)S(1)} %add_add_fusion.2), channel_id=1, source_target_pairs={{0,16},{8,24},{16,0},{24,8},{1,17},{9,25},{17,1},{25,9},{2,18},{10... | collective-permute-start | bytes 12296 | tf_op jit(solution)/shard_map/ppermute | solution.py:268
  96.3 3.6 %collective-permute-start.11 = (f32[8,128]{1,0:T(8,128)S(1)}, f32[8,128]{1,0:T(8,128)S(1)}, u32[]{:S(2)}, u32[]{:S(2)}) collective-permute-start(f32[8,128]{1,0:T(8,128)S(1)} %add_add_fusion.2), channel_id=1, source_target_pairs={{0,24},{8,0},{16,8},{24,16},{1,25},{9,1},{17,9},{25,17},{2,26},{10... | collective-permute-start | bytes 12296 | tf_op jit(solution)/shard_map/ppermute | solution.py:268
  97.0 4.8 %collective-permute-start.9 = (f32[8,128]{1,0:T(8,128)S(1)}, f32[8,128]{1,0:T(8,128)S(1)}, u32[]{:S(2)}, u32[]{:S(2)}) collective-permute-start(f32[8,128]{1,0:T(8,128)S(1)} %add_add_fusion.2), channel_id=1, source_target_pairs={{0,8},{8,16},{16,24},{24,0},{1,9},{9,17},{17,25},{25,1},{2,10},{10... | collective-permute-start | bytes 12296 | tf_op jit(solution)/shard_map/ppermute | solution.py:268
  101.8 6.5 %collective-permute-start.12 = (f32[8,128]{1,0:T(8,128)S(1)}, f32[8,128]{1,0:T(8,128)S(1)}, u32[]{:S(2)}, u32[]{:S(2)}) collective-permute-start(f32[8,128]{1,0:T(8,128)S(1)} %add_add_fusion.1), channel_id=1, source_target_pairs={{0,2},{2,4},{4,6},{6,0},{1,3},{3,5},{5,7},{7,1},{8,10},{10,12},{12... | collective-permute-start | bytes 12296 | tf_op jit(solution)/shard_map/ppermute | solution.py:268
  103.7 5.2 %collective-permute-start.13 = (f32[8,128]{1,0:T(8,128)S(1)}, f32[8,128]{1,0:T(8,128)S(1)}, u32[]{:S(2)}, u32[]{:S(2)}) collective-permute-start(f32[8,128]{1,0:T(8,128)S(1)} %add_add_fusion.1), channel_id=1, source_target_pairs={{0,4},{2,6},{4,0},{6,2},{1,5},{3,7},{5,1},{7,3},{8,12},{10,14},{12... | collective-permute-start | bytes 12296 | tf_op jit(solution)/shard_map/ppermute | solution.py:268
  107.3 3.6 %collective-permute-start.14 = (f32[8,128]{1,0:T(8,128)S(1)}, f32[8,128]{1,0:T(8,128)S(1)}, u32[]{:S(2)}, u32[]{:S(2)}) collective-permute-start(f32[8,128]{1,0:T(8,128)S(1)} %add_add_fusion.1), channel_id=1, source_target_pairs={{0,6},{2,0},{4,2},{6,4},{1,7},{3,1},{5,3},{7,5},{8,14},{10,8},{12,... | collective-permute-start | bytes 12296 | tf_op jit(solution)/shard_map/ppermute | solution.py:268

commit v2 on v1

v2 whole, which is shorter than its diff:
```python
import math

import jax
import jax.numpy as jnp
from jax import lax
from jax.experimental import pallas as pl
from jax.experimental.pallas import tpu as pltpu
from jax.sharding import Mesh
from jax.sharding import PartitionSpec as P

AXES = ("s", "xp", "q", "yp", "z", "c")
GRID = ("s", "xp", "q", "yp")
NC = 8
NR = 8
W = 64
BLOCK = 4 * 2 * W + 8
BOARD = NR * W + 8
HALO = NC * W + 16
F32 = jnp.float32
BF16 = jnp.bfloat16


def vmem():
    return pl.BlockSpec(memory_space=pltpu.VMEM)


def sign_row():
    lane = lax.broadcasted_iota(jnp.int32, (1, 2 * W), 1)
    return jnp.where(lane < W, -1.0, 1.0).astype(F32)


def times_i(x, sign):
    return pltpu.roll(x, W, 1) * sign


def pack_kernel(layout_hbm, assign_hbm, left, right, out, layout, assign, raw, sems):
    core = lax.axis_index("c")
    small = [
        pltpu.make_async_copy(layout_hbm, layout, sems.at[16]),
        pltpu.make_async_copy(assign_hbm, assign, sems.at[17]),
    ]
    for copy in small:
        copy.start()
    for copy in small:
        copy.wait()
    copies = []
    for half in range(2):
        for k in range(4):
            kind = layout[0, (1 - half) * NR + 4 * core + k]
            for side, table in ((0, left), (1, right)):
                n = 8 * half + 2 * k + side
                copies.append(pltpu.make_async_copy(table.at[0, kind], raw.at[n], sems.at[n]))
                copies[-1].start()
    for t in range(4):
        row = jnp.full((1, 2 * W), assign[0, t].astype(F32), F32)
        for dest in range(8):
            out[dest, pl.ds(8 * W + t, 1), :] = row
    for dest in range(8):
        out[dest, pl.ds(8 * W + 4, 4), :] = jnp.zeros((4, 2 * W), F32)
    for n in range(16):
        copies[n].wait()
        x = raw[n].astype(F32)
        half, row = n // 8, n % 8
        for xp in range(2):
            for yp in range(2):
                out[4 * xp + 2 * half + yp, pl.ds(W * row, W), :] = x


def unpack(source, part, lefts, rights, sign):
    def place(j, unused):
        for k in range(4):
            row = 4 * part + k
            lefts[j, row] = source[j, pl.ds(2 * W * k, W), :].astype(BF16)
            r = source[j, pl.ds(2 * W * k + W, W), :]
            rights[j, row, pl.ds(0, W), :] = r.astype(BF16)
            rights[j, row, pl.ds(W, W), :] = times_i(r, sign).astype(BF16)
        return unused

    lax.fori_loop(0, NC, place, 0)


def unpack_kernel(mine, cosine, sine, lefts, rights, phases):
    s, q, own, base = places()
    unpack(mine, lax.axis_index("c"), lefts, rights, sign_row())
    for j in range(NC):
        value = mine[j, pl.ds(8 * W + own, 1), :]
        for n, table in ((0, cosine), (NC, sine)):
            row = jnp.zeros((1, 2 * W), F32)
            for v in range(4):
                row = jnp.where(value == float(v), table[pl.ds(v, 1), :], row)
            phases[pl.ds(n + j, 1), :] = row


def halves(x):
    high = x.astype(BF16)
    return high, (x - high.astype(F32)).astype(BF16)


def sweep(state, lefts, rights, phases, halo_in, halo_out, peaks, start, sign):
    def column(j, carry):
        p, rho_mix, rho = carry
        scale = 1.0 / p
        cos_row = phases[pl.ds(j, 1), :] * scale
        sin_row = phases[pl.ds(NC + j, 1), :] * scale
        boards = [state[k] for k in range(NR)]
        halo_out[pl.ds(j * W, W), :] = boards[0]
        if halo_in is None:
            below = None
        else:
            below = halo_in[pl.ds(j * W, W), :] * rho_mix
        top = jnp.zeros((8, 2 * W), F32)
        for k in range(NR):
            after = boards[k + 1] if k + 1 < NR else below
            mixed = boards[k] if after is None else boards[k] + 0.5 * after
            turn = times_i(mixed, sign)
            mh, ml = halves(mixed)
            th, tl = halves(turn)
            both = jnp.dot(
                lefts[j, k],
                jnp.concatenate([jnp.concatenate([mh, th], 0), jnp.concatenate([ml, tl], 0)], 1),
                preferred_element_type=F32,
            )
            middle = both[:, : 2 * W] + both[:, 2 * W :]
            dh, dl = halves(middle)
            two = jnp.dot(
                jnp.concatenate([dh, dl], 0), rights[j, k], preferred_element_type=F32
            )
            out = two[:W] + two[W:]
            out = out * cos_row + pltpu.roll(out, W, 1) * sin_row
            state[k] = out
            for g in range(8):
                top = jnp.maximum(top, jnp.abs(out[8 * g : 8 * g + 8]))
        own_top = jnp.broadcast_to(jnp.max(top, keepdims=True), (1, 2 * W))
        halo_out[pl.ds(NC * W + j, 1), :] = own_top
        if halo_in is None:
            other_top = jnp.zeros((1, 2 * W), F32)
        else:
            other_top = halo_in[pl.ds(NC * W + j, 1), :]
        p_new = jnp.maximum(jnp.maximum(own_top, other_top * rho), 1.0)
        peaks[pl.ds(j, 1), :] = p_new
        return (p_new, rho, rho * jnp.maximum(other_top, 1.0) / p_new)

    carry = start
    for j in range(NC):
        carry = column(j, carry)
    return carry


def close_sums(state, close, base, sign):
    real = jnp.zeros((8, 2 * W), F32)
    imag = jnp.zeros((8, 2 * W), F32)
    for k in range(NR):
        c = close[base + k]
        b = state[k]
        d = pltpu.roll(c, W, 1)
        for g in range(8):
            part = slice(8 * g, 8 * g + 8)
            real = real - b[part] * c[part] * sign
            imag = imag + b[part] * d[part]
    return jnp.sum(real, keepdims=True), jnp.sum(imag, keepdims=True)


def write_messages(state, board_out, halo_out, peaks, ell, end, sums):
    p, rho_mix, rho = end
    for k in range(NR):
        board_out[pl.ds(k * W, W), :] = state[k]
    board_out[pl.ds(NR * W, 1), :] = p
    board_out[pl.ds(NR * W + 1, 1), :] = rho_mix
    board_out[pl.ds(NR * W + 2, 1), :] = rho
    board_out[pl.ds(NR * W + 3, 1), :] = ell + jnp.sum(jnp.log(peaks[...]), axis=0, keepdims=True)
    board_out[pl.ds(NR * W + 4, 4), :] = jnp.zeros((4, 2 * W), F32)
    halo_out[pl.ds(NC * W + 8, 8), :] = jnp.zeros((8, 2 * W), F32)
    if sums is not None:
        halo_out[pl.ds(NC * W + 8, 1), :] = jnp.broadcast_to(sums[0], (1, 2 * W))
        halo_out[pl.ds(NC * W + 9, 1), :] = jnp.broadcast_to(sums[1], (1, 2 * W))


def places():
    s, q = lax.axis_index("s"), lax.axis_index("q")
    i = jnp.where(s == 0, lax.axis_index("xp"), 1 - lax.axis_index("xp"))
    j = jnp.where(q == 0, lax.axis_index("yp"), 1 - lax.axis_index("yp"))
    return s, q, 2 * i + j, (1 - q) * NR


def first_kernel(other, lefts_in, rights_in, phases, edge, lefts, rights, board_out, halo_out, state, peaks):
    s, q, own, base = places()
    sign = sign_row()
    one = jnp.ones((1, 2 * W), F32)
    unpack(other, 1 - lax.axis_index("c"), lefts, rights, sign)
    for k in range(NR):
        state[k] = edge[base + k].astype(F32)
    end = sweep(state, lefts, rights, phases, None, halo_out, peaks, (one, one, one), sign)
    write_messages(state, board_out, halo_out, peaks, 0.0 * one, end, None)


def load_state(state, edge, board_in, base, s):
    one = jnp.ones((1, 2 * W), F32)
    first = s == 0
    for k in range(NR):
        state[k] = jnp.where(first, edge[base + k].astype(F32), board_in[pl.ds(k * W, W), :])
    row = lambda n: board_in[pl.ds(NR * W + n, 1), :]
    p = jnp.maximum(jnp.where(first, one, row(0)), 1.0)
    rho_mix = jnp.where(first, one, row(1))
    rho = jnp.where(first, one, row(2))
    ell = jnp.where(first, 0.0 * one, row(3))
    return (p, rho_mix, rho), ell


def second_kernel(phases, edge, lefts, rights, close, board_in, halo_in, board_out, halo_out, state, peaks):
    s, q, own, base = places()
    sign = sign_row()
    start, ell = load_state(state, edge, board_in, base, s)
    end = sweep(state, lefts, rights, phases, halo_in, halo_out, peaks, start, sign)
    write_messages(
        state, board_out, halo_out, peaks, ell, end, close_sums(state, close, base, sign)
    )


def third_kernel(phases, edge, lefts, rights, close, board_in, halo_in, out, state, peaks, halo_out):
    s, q, own, base = places()
    sign = sign_row()
    start, ell = load_state(state, edge, board_in, base, s)
    p, rho_mix, rho = sweep(state, lefts, rights, phases, halo_in, halo_out, peaks, start, sign)
    ell = ell + jnp.sum(jnp.log(peaks[...]), axis=0, keepdims=True)
    real, imag = close_sums(state, close, base, sign)
    factor = 1.0 / math.sqrt(2 * NR * W * W)
    real = (real + rho_mix * halo_in[pl.ds(NC * W + 8, 1), :]) / p * factor
    imag = (imag + rho_mix * halo_in[pl.ds(NC * W + 9, 1), :]) / p * factor
    index = 4 * (2 * lax.axis_index("z") + lax.axis_index("c")) + own
    lane = lax.broadcasted_iota(jnp.int32, (1, 2 * W), 1)
    index = jnp.where(jnp.logical_and(s == 1, q == 1), index, -1)
    hit = lane == index
    zero = jnp.zeros((1, 2 * W), F32)
    out[pl.ds(0, 1), :] = jnp.where(hit, real, zero)
    out[pl.ds(1, 1), :] = jnp.where(hit, imag, zero)
    out[pl.ds(2, 1), :] = jnp.where(hit, ell, zero)
    out[pl.ds(3, 5), :] = jnp.zeros((5, 2 * W), F32)


def finish_kernel(a, b, c, d, amps, logs, total, top):
    found = a[...] + b[...] + c[...] + d[...]
    ell = found[2:3]
    high = jnp.max(ell, axis=1, keepdims=True)
    weighted = found[0:2] * jnp.exp(ell - high)
    top[...] = high
    sums = jnp.sum(weighted, axis=1, keepdims=True)
    total[...] = jnp.concatenate([sums[0:1], sums[1:2]], 1)
    at = 4 * (2 * lax.axis_index("z") + lax.axis_index("c"))
    here = pltpu.roll(found, jnp.where(at == 0, 0, 2 * W - at), 1)
    amps[...] = here[0:2, 0:4]
    logs[...] = here[2:3, 0:4]


def call(kernel, outs, scratch, args, specs=None, aliases=None):
    return pl.pallas_call(
        kernel,
        out_shape=outs,
        in_specs=specs or [vmem()] * len(args),
        out_specs=jax.tree.map(lambda _: vmem(), outs),
        scratch_shapes=scratch,
        input_output_aliases=aliases or {},
        compiler_params=pltpu.CompilerParams(vmem_limit_bytes=20 * 2**20),
    )(*args)


def shape(*dims, dtype=F32):
    return jax.ShapeDtypeStruct(dims, dtype)


def chip(s, xp, q, yp):
    return 8 * s + 4 * xp + 2 * q + yp


def along_columns(value, q):
    pairs = [(chip(0, xp, q, yp), chip(1, 1 - xp, q, yp)) for xp in range(2) for yp in range(2)]
    return lax.ppermute(value, GRID, pairs)


def along_rows(value, s):
    pairs = [(chip(s, xp, 0, yp), chip(s, xp, 1, 1 - yp)) for xp in range(2) for yp in range(2)]
    return lax.ppermute(value, GRID, pairs)


def swapped(value):
    return lax.ppermute(value, "c", [(0, 1), (1, 0)])


def gathered(found):
    found = found + swapped(found)
    total = found
    for dx, dy in ((1, 0), (0, 1), (1, 1)):
        pairs = [
            (chip(1, xp, 1, yp), chip(1, (xp + dx) % 2, 1, (yp + dy) % 2))
            for xp in range(2)
            for yp in range(2)
        ]
        total = total + lax.ppermute(found, GRID, pairs)
    found = total
    for by in range(1, 4):
        pairs = [
            (4 * chip(1, xp, 1, yp) + z, 4 * chip(1, xp, 1, yp) + (z + by) % 4)
            for xp in range(2)
            for yp in range(2)
            for z in range(4)
        ]
        total = total + lax.ppermute(found, (*GRID, "z"), pairs)
    parts = [total]
    for s, q in ((0, 1), (1, 0), (0, 0)):
        pairs = [
            (chip(1, xp, 1, yp), chip(s, (xp + 1 + s) % 2, q, (yp + 1 + q) % 2))
            for xp in range(2)
            for yp in range(2)
        ]
        parts.append(lax.ppermute(total, GRID, pairs))
    return parts


def body(layout, assign, edge, gate_left, gate_right, phase_angle, close):
    cosine, sine = jnp.cos(phase_angle), jnp.sin(phase_angle)
    cosine = jnp.concatenate([cosine, cosine], -1)
    sine = jnp.concatenate([-sine, sine], -1)
    hbm = pl.BlockSpec(memory_space=pltpu.HBM)
    packed = call(
        pack_kernel,
        shape(8, BLOCK, 2 * W),
        [
            pltpu.SMEM((1, 16), jnp.int32),
            pltpu.SMEM((1, 4), jnp.int32),
            pltpu.VMEM((16, W, 2 * W), BF16),
            pltpu.SemaphoreType.DMA((18,)),
        ],
        [
            pltpu.with_memory_space_constraint(x, pltpu.HBM)
            for x in (layout.T, assign.T, gate_left, gate_right)
        ],
        [hbm, hbm, hbm, hbm],
    )
    mine = lax.all_to_all(packed, ("xp", "q", "yp"), 0, 0, tiled=True)
    other = swapped(mine)
    state = pltpu.VMEM((NR, W, 2 * W), F32)
    peaks = pltpu.VMEM((NC, 2 * W), F32)
    gates = (shape(NC, NR, W, 2 * W, dtype=BF16), shape(NC, NR, 2 * W, 2 * W, dtype=BF16))
    lefts, rights, phases = call(
        unpack_kernel, (*gates, shape(2 * NC, 2 * W)), [], (mine, cosine, sine)
    )
    lefts, rights, board, halo = call(
        first_kernel,
        (*gates, shape(BOARD, 2 * W), shape(HALO, 2 * W)),
        [state, peaks],
        (other, lefts, rights, phases, edge),
        aliases={1: 0, 2: 1},
    )
    board, halo = along_columns(board, 0), along_rows(halo, 0)
    board, halo = call(
        second_kernel,
        (shape(BOARD, 2 * W), shape(HALO, 2 * W)),
        [state, peaks],
        (phases, edge, lefts, rights, close, board, halo),
    )
    board, halo = along_columns(board, 1), along_rows(halo, 1)
    found = call(
        third_kernel,
        shape(8, 2 * W),
        [state, peaks, pltpu.VMEM((HALO, 2 * W), F32)],
        (phases, edge, lefts, rights, close, board, halo),
    )
    amps, logs, total_amp, top_log = call(
        finish_kernel,
        (shape(2, 4), shape(1, 4), shape(1, 2), shape(1, 1)),
        [],
        gathered(found),
    )
    return (amps.T, logs.reshape(4), total_amp.reshape(2), top_log.reshape(()))


def solution(mesh):
    split = Mesh(mesh.devices.reshape(2, 2, 2, 2, 4, 2), AXES)
    placed = (
        P(None, GRID),
        P(("z", "c"), GRID),
        P(),
        P(GRID, None, None, None),
        P(GRID, None, None, None),
        P(),
        P(),
    )
    return jax.shard_map(
        body,
        mesh=split,
        in_specs=placed,
        out_specs=(P(("z", "c"), None), P(("z", "c")), P(), P()),
        check_vma=False,
    )
```

time: 114 us -> 107 us (0.939)
  waiting for transfers between devices: 19.9 us -> 44.2 us
  starting transfers between devices: 28.9 us -> 12.4 us
  Pallas kernels: 23.2 us -> 15.9 us
  local copies, waits for them, and re-layouts: 5.9 us -> 0.05 us
  other arithmetic: 1.98 us -> 0.1 us
    ppermute x11, waiting for transfers between devices: 14 us -> 38.3 us  [the longest x3 33.9 us: gathered(): parts.append(lax.ppermute(total, GRID, pairs))]
    ppermute x11, starting transfers between devices: 23.1 us -> 6.66 us  [the longest x3 2.62 us: gathered(): parts.append(lax.ppermute(total, GRID, pairs))]
    pallas_call x4 -> x6, Pallas kernels: 23.2 us -> 15.9 us  [call(): pl.pallas_call(kernel, out_shape=outs, in_specs=specs or [vmem()] * len(a...]
    unnamed x16 -> x6, local copies, waits for them, and re-layouts: 4.71 us -> 0.01 us
  transfers between devices with their start and end apart: 15 -> 15, of which waited for: 9 -> 4; matrix products, arithmetic and copies ran while one was open for 0% -> 0% of each run, Pallas kernels for 0% -> 1%
where the time goes in v2:
time: 107 us
  waiting for transfers between devices  44.2 us (41%)
  blocking collectives  33.1 us (31%)
  Pallas kernels  15.9 us (15%)
  starting transfers between devices  12.4 us (12%)
    ppermute x3, waiting for transfers between devices, gathered(): parts.append(lax.ppermute(total, GRID, pairs))  33.9 us
    all_to_all x1, blocking collectives, body(): mine = lax.all_to_all(packed, ('xp', 'q', 'yp'), 0, 0, tiled=True)  33.1 us
    pallas_call x6, Pallas kernels, call(): pl.pallas_call(kernel, out_shape=outs, in_specs=specs or [vmem()] * len(a...  15.9 us
    ppermute x2, waiting for transfers between devices, along_columns(): return lax.ppermute(value, GRID, pairs)  5.92 us
    ppermute x2, waiting for transfers between devices, swapped(): return lax.ppermute(value, 'c', [(0, 1), (1, 0)])  4.33 us
    ppermute x2, starting transfers between devices, along_rows(): return lax.ppermute(value, GRID, pairs)  3.76 us
    ppermute x3, starting transfers between devices, gathered(): parts.append(lax.ppermute(total, GRID, pairs))  2.62 us
  transfers between devices with their start and end apart: 15, of which 4 were waited for; matrix products, arithmetic and copies ran while one was open for 0% of the time, Pallas kernels for 1%

profile of v2, /device:TPU:0, one launch (start us, length us, event | category | flops | bytes accessed | tf_op | source)
XLA Modules:
  0.0 106.6 jit_solution(18332822980633297864)
XLA Ops:
  0.6 1.8 %shard_map.102 = f32[8,520,128]{2,1,0:T(8,128)S(1)} custom-call(s32[1,16]{1,0:T(1,128)} %bitcast.6, s32[1,4]{1,0:T(1,128)} %bitcast.7, bf16[1,16,64,128]{3,2,1,0:T(8,128)(2,1)} %left.1, bf16[1,16,64,128]{3,2,1,0:T(8,128)(2,1)} %right.1), custom_call_target="tpu_custom_call" | custom-call | tf_op jit(solution)/shard_map/pallas_call | solution.py:255
  2.4 0.0 copy-start.2
  2.4 33.1 %all_to_all.5.mine = f32[8,520,128]{2,1,0:T(8,128)S(1)} all-to-all(f32[8,520,128]{2,1,0:T(8,128)S(1)} %shard_map.102), channel_id=1, replica_groups=mesh['s'=2,'xp'=2,'q'=2,'yp'=2,'z'=4,'c'=2] {'xp','q','yp'}, dimensions={0} | all-to-all | bytes 4259840 | tf_op jit(solution)/shard_map/all_to_all | solution.py:338
  35.5 0.0 copy-start
  35.5 0.0 collective-permute-start
  35.5 0.0 copy-done.2
  35.6 0.1 pad_maximum_fusion
  35.7 0.9 shard_map.103
  36.6 3.2 %collective-permute-done.other = f32[8,520,128]{2,1,0:T(8,128)S(1)} collective-permute-done((f32[8,520,128]{2,1,0:T(8,128)S(1)}, f32[8,520,128]{2,1,0:T(8,128)S(1)}, u32[]{:S(2)}, u32[]{:S(2)}) %collective-permute-start) | collective-permute-done | bytes 2129952 | tf_op jit(solution)/shard_map/ppermute | solution.py:285
  39.7 0.0 copy-done
  39.7 0.0 copy-start.1
  39.8 4.7 %shard_map.104 = (bf16[8,8,64,128]{3,2,1,0:T(8,128)(2,1)S(1)}, bf16[8,8,128,128]{3,2,1,0:T(8,128)(2,1)S(1)}, f32[520,128]{1,0:T(8,128)S(1)}, f32[528,128]{1,0:T(8,128)S(1)}) custom-call(f32[8,520,128]{2,1,0:T(8,128)S(1)} %collective-permute-done.other, ...), custom_call_target="tpu_custom_call", output_to_operand_aliasing={{0}: (1, {}), {1}: (2, {})} | custom-call | tf_op jit(solution)/shard_map/pallas_call | solution.py:255
  44.5 3.1 %collective-permute-start.2 = (f32[528,128]{1,0:T(8,128)S(1)}, f32[528,128]{1,0:T(8,128)S(1)}, u32[]{:S(2)}, u32[]{:S(2)}) collective-permute-start(f32[528,128]{1,0:T(8,128)S(1)} %get-tuple-element.23), channel_id=1, source_target_pairs={{0,24},{8,16},{32,56},{40,48},{1,25},{9,17},{33,57},{41,49},{2,26}... | collective-permute-start | bytes 811016 | tf_op jit(solution)/shard_map/ppermute | solution.py:281
  47.6 1.3 %collective-permute-start.1 = (f32[520,128]{1,0:T(8,128)S(1)}, f32[520,128]{1,0:T(8,128)S(1)}, u32[]{:S(2)}, u32[]{:S(2)}) collective-permute-start(f32[520,128]{1,0:T(8,128)S(1)} %get-tuple-element.22), channel_id=1, source_target_pairs={{0,96},{8,104},{32,64},{40,72},{1,97},{9,105},{33,65},{41,73},{2,9... | collective-permute-start | bytes 798728 | tf_op jit(solution)/shard_map/ppermute | solution.py:276
  48.9 5.9 %collective-permute-done.1.board_in = f32[520,128]{1,0:T(8,128)S(1)} collective-permute-done((f32[520,128]{1,0:T(8,128)S(1)}, f32[520,128]{1,0:T(8,128)S(1)}, u32[]{:S(2)}, u32[]{:S(2)}) %collective-permute-start.1) | collective-permute-done | bytes 266272 | tf_op jit(solution)/shard_map/ppermute | solution.py:276
  54.8 0.0 collective-permute-done.2.halo_in
  54.8 0.0 copy-done.1
  54.8 3.9 %shard_map.105 = (f32[520,128]{1,0:T(8,128)S(1)}, f32[528,128]{1,0:T(8,128)S(1)}) custom-call(f32[16,128]{1,0:T(8,128)S(1)} %get-tuple-element.17.phases, bf16[16,64,128]{2,1,0:T(8,128)(2,1)S(1)} %copy-done, bf16[8,8,64,128]{3,2,1,0:T(8,128)(2,1)S(1)} %get-tuple-element.20.lefts, bf16[8,8,128,128]{3,2,1,0:T(8,128)(2,1)S(1)} %get-tuple-element.21.rights, ...), custom_call_target="tpu_custom_call" | custom-call | tf_op jit(solution)/shard_map/pallas_call | solution.py:255
  58.7 0.7 collective-permute-start.4
  59.4 0.7 collective-permute-start.3
  60.1 0.0 collective-permute-done.3.board_in
  60.1 0.0 collective-permute-done.4.halo_in
  60.1 3.9 %shard_map.106 = f32[8,128]{1,0:T(8,128)S(1)} custom-call(f32[16,128]{1,0:T(8,128)S(1)} %get-tuple-element.17.phases, bf16[16,64,128]{2,1,0:T(8,128)(2,1)S(1)} %copy-done, bf16[8,8,64,128]{3,2,1,0:T(8,128)(2,1)S(1)} %get-tuple-element.20.lefts, bf16[8,8,128,128]{3,2,1,0:T(8,128)(2,1)S(1)} %get-tuple-element.21.rights, f32[16,64,128]{2,1,0:T(8,128)S(1)} %copy-done.1, ...), custom_call_target="tpu_custom_call" | custom-call | tf_op jit(solution)/shard_map/pallas_call | solution.py:255
  64.0 0.1 collective-permute-start.5
  64.1 1.2 %collective-permute-done.5 = f32[8,128]{1,0:T(8,128)S(1)} collective-permute-done((f32[8,128]{1,0:T(8,128)S(1)}, f32[8,128]{1,0:T(8,128)S(1)}, u32[]{:S(2)}, u32[]{:S(2)}) %collective-permute-start.5) | collective-permute-done | bytes 4128 | tf_op jit(solution)/shard_map/ppermute | solution.py:285
  65.3 0.7 collective-permute-start.8
  65.9 0.7 collective-permute-start.7
  66.6 0.7 collective-permute-start.6
  67.3 0.0 collective-permute-done.8
  67.3 0.0 collective-permute-done.7
  67.3 0.0 collective-permute-done.6
  67.3 0.7 collective-permute-start.11
  68.0 0.7 collective-permute-start.10
  68.7 0.7 collective-permute-start.9
  69.3 0.0 collective-permute-done.11
  69.3 0.0 collective-permute-done.10
  69.4 0.0 collective-permute-done.9
  69.4 1.3 %collective-permute-start.14 = (f32[8,128]{1,0:T(8,128)S(1)}, f32[8,128]{1,0:T(8,128)S(1)}, u32[]{:S(2)}, u32[]{:S(2)}) collective-permute-start(f32[8,128]{1,0:T(8,128)S(1)} %add_add_fusion.a), channel_id=1, source_target_pairs={{80,40},{88,32},{112,8},{120,0},{81,41},{89,33},{113,9},{121,1},{8... | collective-permute-start | bytes 12296 | tf_op jit(solution)/shard_map/ppermute | solution.py:314
  70.7 0.7 collective-permute-start.13
  71.4 0.7 collective-permute-start.12
  72.0 33.9 %collective-permute-done.14.d = f32[8,128]{1,0:T(8,128)S(1)} collective-permute-done((f32[8,128]{1,0:T(8,128)S(1)}, f32[8,128]{1,0:T(8,128)S(1)}, u32[]{:S(2)}, u32[]{:S(2)}) %collective-permute-start.14) | collective-permute-done | bytes 4128 | tf_op jit(solution)/shard_map/ppermute | solution.py:314
  105.9 0.0 collective-permute-done.13.c
  105.9 0.0 collective-permute-done.12.b
  105.9 0.7 shard_map.107
  (5 shorter events, 0.1 us)
Async XLA Ops:
  2.4 33.1 %copy-start.2 = (f32[4,64]{1,0:T(4,128)S(1)}, f32[4,64]{1,0:T(4,128)}, u32[]{:S(2)}) copy-start(f32[4,64]{1,0:T(4,128)} %param.12) | copy-start | bytes 3076
  35.5 4.2 %copy-start = (bf16[16,64,128]{2,1,0:T(8,128)(2,1)S(1)}, bf16[16,64,128]{2,1,0:T(8,128)(2,1)}, u32[]{:S(2)}) copy-start(bf16[16,64,128]{2,1,0:T(8,128)(2,1)} %edge.5) | copy-start | bytes 786436
  35.5 4.2 %collective-permute-start = (f32[8,520,128]{2,1,0:T(8,128)S(1)}, f32[8,520,128]{2,1,0:T(8,128)S(1)}, u32[]{:S(2)}, u32[]{:S(2)}) collective-permute-start(f32[8,520,128]{2,1,0:T(8,128)S(1)} %all_to_all.5.mine), channel_id=1, source_target_pairs={{0,1},{1,0},{2,3},{3,2},{4,5},{5,4},{6,7},{7,6},{8,9},{9,8},{10,11... | collective-permute-start | bytes 6389768 | tf_op jit(solution)/shard_map/ppermute | solution.py:285
  39.7 15.1 %copy-start.1 = (f32[16,64,128]{2,1,0:T(8,128)S(1)}, f32[16,64,128]{2,1,0:T(8,128)}, u32[]{:S(2)}) copy-start(f32[16,64,128]{2,1,0:T(8,128)} %close.3) | copy-start | bytes 1572868
  44.5 10.4 %collective-permute-start.2 = (f32[528,128]{1,0:T(8,128)S(1)}, f32[528,128]{1,0:T(8,128)S(1)}, u32[]{:S(2)}, u32[]{:S(2)}) collective-permute-start(f32[528,128]{1,0:T(8,128)S(1)} %get-tuple-element.23), channel_id=1, source_target_pairs={{0,24},{8,16},{32,56},{40,48},{1,25},{9,17},{33,57},{41,49},{2,26}... | collective-permute-start | bytes 811016 | tf_op jit(solution)/shard_map/ppermute | solution.py:281
  47.6 7.3 %collective-permute-start.1 = (f32[520,128]{1,0:T(8,128)S(1)}, f32[520,128]{1,0:T(8,128)S(1)}, u32[]{:S(2)}, u32[]{:S(2)}) collective-permute-start(f32[520,128]{1,0:T(8,128)S(1)} %get-tuple-element.22), channel_id=1, source_target_pairs={{0,96},{8,104},{32,64},{40,72},{1,97},{9,105},{33,65},{41,73},{2,9... | collective-permute-start | bytes 798728 | tf_op jit(solution)/shard_map/ppermute | solution.py:276
  58.7 1.4 %collective-permute-start.4 = (f32[528,128]{1,0:T(8,128)S(1)}, f32[528,128]{1,0:T(8,128)S(1)}, u32[]{:S(2)}, u32[]{:S(2)}) collective-permute-start(f32[528,128]{1,0:T(8,128)S(1)} %get-tuple-element.25), channel_id=1, source_target_pairs={{64,88},{72,80},{96,120},{104,112},{65,89},{73,81},{97,121},{105,1... | collective-permute-start | bytes 811016 | tf_op jit(solution)/shard_map/ppermute | solution.py:281
  59.4 0.7 collective-permute-start.3
  64.0 1.2 %collective-permute-start.5 = (f32[8,128]{1,0:T(8,128)S(1)}, f32[8,128]{1,0:T(8,128)S(1)}, u32[]{:S(2)}, u32[]{:S(2)}) collective-permute-start(f32[8,128]{1,0:T(8,128)S(1)} %shard_map.106), channel_id=1, source_target_pairs={{0,1},{1,0},{2,3},{3,2},{4,5},{5,4},{6,7},{7,6},{8,9},{9,8},{10,11... | collective-permute-start | bytes 12296 | tf_op jit(solution)/shard_map/ppermute | solution.py:285
  65.3 2.0 %collective-permute-start.8 = (f32[8,128]{1,0:T(8,128)S(1)}, f32[8,128]{1,0:T(8,128)S(1)}, u32[]{:S(2)}, u32[]{:S(2)}) collective-permute-start(f32[8,128]{1,0:T(8,128)S(1)} %add.21), channel_id=1, source_target_pairs={{80,120},{88,112},{112,88},{120,80},{81,121},{89,113},{113,89},{12... | collective-permute-start | bytes 12296 | tf_op jit(solution)/shard_map/ppermute | solution.py:297
  65.9 1.4 %collective-permute-start.7 = (f32[8,128]{1,0:T(8,128)S(1)}, f32[8,128]{1,0:T(8,128)S(1)}, u32[]{:S(2)}, u32[]{:S(2)}) collective-permute-start(f32[8,128]{1,0:T(8,128)S(1)} %add.21), channel_id=1, source_target_pairs={{80,88},{88,80},{112,120},{120,112},{81,89},{89,81},{113,121},{121... | collective-permute-start | bytes 12296 | tf_op jit(solution)/shard_map/ppermute | solution.py:297
  66.6 0.7 collective-permute-start.6
  67.3 2.0 %collective-permute-start.11 = (f32[8,128]{1,0:T(8,128)S(1)}, f32[8,128]{1,0:T(8,128)S(1)}, u32[]{:S(2)}, u32[]{:S(2)}) collective-permute-start(f32[8,128]{1,0:T(8,128)S(1)} %add_add_fusion.1), channel_id=1, source_target_pairs={{80,86},{82,80},{84,82},{86,84},{88,94},{90,88},{92,90},{94,92},{1... | collective-permute-start | bytes 12296 | tf_op jit(solution)/shard_map/ppermute | solution.py:306
  68.0 1.4 %collective-permute-start.10 = (f32[8,128]{1,0:T(8,128)S(1)}, f32[8,128]{1,0:T(8,128)S(1)}, u32[]{:S(2)}, u32[]{:S(2)}) collective-permute-start(f32[8,128]{1,0:T(8,128)S(1)} %add_add_fusion.1), channel_id=1, source_target_pairs={{80,84},{82,86},{84,80},{86,82},{88,92},{90,94},{92,88},{94,90},{1... | collective-permute-start | bytes 12296 | tf_op jit(solution)/shard_map/ppermute | solution.py:306
  68.7 0.7 collective-permute-start.9
  69.4 36.5 %collective-permute-start.14 = (f32[8,128]{1,0:T(8,128)S(1)}, f32[8,128]{1,0:T(8,128)S(1)}, u32[]{:S(2)}, u32[]{:S(2)}) collective-permute-start(f32[8,128]{1,0:T(8,128)S(1)} %add_add_fusion.a), channel_id=1, source_target_pairs={{80,40},{88,32},{112,8},{120,0},{81,41},{89,33},{113,9},{121,1},{8... | collective-permute-start | bytes 12296 | tf_op jit(solution)/shard_map/ppermute | solution.py:314
  70.7 35.2 %collective-permute-start.13 = (f32[8,128]{1,0:T(8,128)S(1)}, f32[8,128]{1,0:T(8,128)S(1)}, u32[]{:S(2)}, u32[]{:S(2)}) collective-permute-start(f32[8,128]{1,0:T(8,128)S(1)} %add_add_fusion.a), channel_id=1, source_target_pairs={{80,72},{88,64},{112,104},{120,96},{81,73},{89,65},{113,105},{121,... | collective-permute-start | bytes 12296 | tf_op jit(solution)/shard_map/ppermute | solution.py:314
  71.4 34.6 %collective-permute-start.12 = (f32[8,128]{1,0:T(8,128)S(1)}, f32[8,128]{1,0:T(8,128)S(1)}, u32[]{:S(2)}, u32[]{:S(2)}) collective-permute-start(f32[8,128]{1,0:T(8,128)S(1)} %add_add_fusion.a), channel_id=1, source_target_pairs={{80,48},{88,56},{112,16},{120,24},{81,49},{89,57},{113,17},{121,25... | collective-permute-start | bytes 12296 | tf_op jit(solution)/shard_map/ppermute | solution.py:314

commit v3 on v2

--- a/solution.py
+++ b/solution.py
@@ -237,8 +237,8 @@
     out[pl.ds(3, 5), :] = jnp.zeros((5, 2 * W), F32)
 
 
-def finish_kernel(a, b, c, d, amps, logs, total, top):
-    found = a[...] + b[...] + c[...] + d[...]
+def finish_kernel(blocks, amps, logs, total, top):
+    found = jnp.sum(blocks[...], axis=0)
     ell = found[2:3]
     high = jnp.max(ell, axis=1, keepdims=True)
     weighted = found[0:2] * jnp.exp(ell - high)
@@ -287,32 +287,10 @@
 
 def gathered(found):
     found = found + swapped(found)
-    total = found
-    for dx, dy in ((1, 0), (0, 1), (1, 1)):
-        pairs = [
-            (chip(1, xp, 1, yp), chip(1, (xp + dx) % 2, 1, (yp + dy) % 2))
-            for xp in range(2)
-            for yp in range(2)
-        ]
-        total = total + lax.ppermute(found, GRID, pairs)
-    found = total
-    for by in range(1, 4):
-        pairs = [
-            (4 * chip(1, xp, 1, yp) + z, 4 * chip(1, xp, 1, yp) + (z + by) % 4)
-            for xp in range(2)
-            for yp in range(2)
-            for z in range(4)
-        ]
-        total = total + lax.ppermute(found, (*GRID, "z"), pairs)
-    parts = [total]
-    for s, q in ((0, 1), (1, 0), (0, 0)):
-        pairs = [
-            (chip(1, xp, 1, yp), chip(s, (xp + 1 + s) % 2, q, (yp + 1 + q) % 2))
-            for xp in range(2)
-            for yp in range(2)
-        ]
-        parts.append(lax.ppermute(total, GRID, pairs))
-    return parts
+    chips = (*GRID, "z")
+    count = lax.axis_size(chips)
+    spread = jnp.broadcast_to(found[None], (count, *found.shape))
+    return lax.all_to_all(spread, chips, 0, 0, tiled=True)
 
 
 def body(layout, assign, edge, gate_left, gate_right, phase_angle, close):
@@ -368,7 +346,7 @@
         finish_kernel,
         (shape(2, 4), shape(1, 4), shape(1, 2), shape(1, 1)),
         [],
-        gathered(found),
+        (gathered(found),),
     )
     return (amps.T, logs.reshape(4), total_amp.reshape(2), top_log.reshape(()))
 

time: 107 us -> 94.9 us (0.89)
  waiting for transfers between devices: 44.2 us -> 10.3 us
  blocking collectives: 33.1 us -> 61.7 us
  starting transfers between devices: 12.4 us -> 5.84 us
    ppermute x9 -> x0, waiting for transfers between devices: 33.9 us -> none  [the longest x3 33.9 us: gathered(): parts.append(lax.ppermute(total, GRID, pairs))]
    all_to_all x0 -> x1, blocking collectives: none -> 28.5 us  [gathered(): return lax.all_to_all(spread, chips, 0, 0, tiled=True)]
    ppermute x9 -> x0, starting transfers between devices: 6.57 us -> none  [the longest x3 2.62 us: gathered(): parts.append(lax.ppermute(total, GRID, pairs))]
  transfers between devices with their start and end apart: 15 -> 6, of which waited for: 4 -> 3; matrix products, arithmetic and copies ran while one was open for 0% -> 0% of each run, Pallas kernels for 1% -> 1%
where the time goes in v3:
time: 94.9 us; the launch traced here: 94.6 us
  blocking collectives  61.7 us (65%)
  Pallas kernels  15.9 us (17%)
  waiting for transfers between devices  10.3 us (11%)
  starting transfers between devices  5.84 us (6%)
    all_to_all x1, blocking collectives, body(): mine = lax.all_to_all(packed, ('xp', 'q', 'yp'), 0, 0, tiled=True)  33.2 us
    all_to_all x1, blocking collectives, gathered(): return lax.all_to_all(spread, chips, 0, 0, tiled=True)  28.5 us
    pallas_call x6, Pallas kernels, call(): pl.pallas_call(kernel, out_shape=outs, in_specs=specs or [vmem()] * len(a...  15.9 us
    ppermute x2, waiting for transfers between devices, along_columns(): return lax.ppermute(value, GRID, pairs)  5.92 us
    ppermute x2, waiting for transfers between devices, swapped(): return lax.ppermute(value, 'c', [(0, 1), (1, 0)])  4.33 us
    ppermute x2, starting transfers between devices, along_rows(): return lax.ppermute(value, GRID, pairs)  3.76 us
    ppermute x2, starting transfers between devices, along_columns(): return lax.ppermute(value, GRID, pairs)  1.98 us
  transfers between devices with their start and end apart: 6, of which 3 were waited for; matrix products, arithmetic and copies ran while one was open for 0% of the time, Pallas kernels for 1%

profile of v3, /device:TPU:0, one launch (start us, length us, event | category | flops | bytes accessed | tf_op | source)
XLA Modules:
  0.0 94.6 jit_solution(7662894156073003839)
XLA Ops:
  0.6 1.8 %shard_map.102 = f32[8,520,128]{2,1,0:T(8,128)S(1)} custom-call(s32[1,16]{1,0:T(1,128)} %bitcast.6, s32[1,4]{1,0:T(1,128)} %bitcast.7, bf16[1,16,64,128]{3,2,1,0:T(8,128)(2,1)} %left.1, bf16[1,16,64,128]{3,2,1,0:T(8,128)(2,1)} %right.1), custom_call_target="tpu_custom_call" | custom-call | tf_op jit(solution)/shard_map/pallas_call | solution.py:255
  2.4 0.0 copy-start.2
  2.4 33.2 %all_to_all.10.mine = f32[8,520,128]{2,1,0:T(8,128)S(1)} all-to-all(f32[8,520,128]{2,1,0:T(8,128)S(1)} %shard_map.102), channel_id=1, replica_groups=mesh['s'=2,'xp'=2,'q'=2,'yp'=2,'z'=4,'c'=2] {'xp','q','yp'}, dimensions={0} | all-to-all | bytes 4259840 | tf_op jit(solution)/shard_map/all_to_all | solution.py:316
  35.6 0.0 copy-start
  35.6 0.0 collective-permute-start
  35.6 0.0 copy-done.2
  35.7 0.1 pad_maximum_fusion
  35.8 0.9 shard_map.103
  36.6 3.2 %collective-permute-done.other = f32[8,520,128]{2,1,0:T(8,128)S(1)} collective-permute-done((f32[8,520,128]{2,1,0:T(8,128)S(1)}, f32[8,520,128]{2,1,0:T(8,128)S(1)}, u32[]{:S(2)}, u32[]{:S(2)}) %collective-permute-start) | collective-permute-done | bytes 2129952 | tf_op jit(solution)/shard_map/ppermute | solution.py:285
  39.8 0.0 copy-done
  39.8 0.0 copy-start.1
  39.8 4.7 %shard_map.104 = (bf16[8,8,64,128]{3,2,1,0:T(8,128)(2,1)S(1)}, bf16[8,8,128,128]{3,2,1,0:T(8,128)(2,1)S(1)}, f32[520,128]{1,0:T(8,128)S(1)}, f32[528,128]{1,0:T(8,128)S(1)}) custom-call(f32[8,520,128]{2,1,0:T(8,128)S(1)} %collective-permute-done.other, ...), custom_call_target="tpu_custom_call", output_to_operand_aliasing={{0}: (1, {}), {1}: (2, {})} | custom-call | tf_op jit(solution)/shard_map/pallas_call | solution.py:255
  44.6 3.1 %collective-permute-start.2 = (f32[528,128]{1,0:T(8,128)S(1)}, f32[528,128]{1,0:T(8,128)S(1)}, u32[]{:S(2)}, u32[]{:S(2)}) collective-permute-start(f32[528,128]{1,0:T(8,128)S(1)} %get-tuple-element.23), channel_id=1, source_target_pairs={{0,24},{8,16},{32,56},{40,48},{1,25},{9,17},{33,57},{41,49},{2,26}... | collective-permute-start | bytes 811016 | tf_op jit(solution)/shard_map/ppermute | solution.py:281
  47.7 1.3 %collective-permute-start.1 = (f32[520,128]{1,0:T(8,128)S(1)}, f32[520,128]{1,0:T(8,128)S(1)}, u32[]{:S(2)}, u32[]{:S(2)}) collective-permute-start(f32[520,128]{1,0:T(8,128)S(1)} %get-tuple-element.22), channel_id=1, source_target_pairs={{0,96},{8,104},{32,64},{40,72},{1,97},{9,105},{33,65},{41,73},{2,9... | collective-permute-start | bytes 798728 | tf_op jit(solution)/shard_map/ppermute | solution.py:276
  49.0 5.9 %collective-permute-done.1.board_in = f32[520,128]{1,0:T(8,128)S(1)} collective-permute-done((f32[520,128]{1,0:T(8,128)S(1)}, f32[520,128]{1,0:T(8,128)S(1)}, u32[]{:S(2)}, u32[]{:S(2)}) %collective-permute-start.1) | collective-permute-done | bytes 266272 | tf_op jit(solution)/shard_map/ppermute | solution.py:276
  54.9 0.0 collective-permute-done.2.halo_in
  54.9 0.0 copy-done.1
  54.9 3.9 %shard_map.105 = (f32[520,128]{1,0:T(8,128)S(1)}, f32[528,128]{1,0:T(8,128)S(1)}) custom-call(f32[16,128]{1,0:T(8,128)S(1)} %get-tuple-element.17.phases, bf16[16,64,128]{2,1,0:T(8,128)(2,1)S(1)} %copy-done, bf16[8,8,64,128]{3,2,1,0:T(8,128)(2,1)S(1)} %get-tuple-element.20.lefts, bf16[8,8,128,128]{3,2,1,0:T(8,128)(2,1)S(1)} %get-tuple-element.21.rights, ...), custom_call_target="tpu_custom_call" | custom-call | tf_op jit(solution)/shard_map/pallas_call | solution.py:255
  58.8 0.7 collective-permute-start.4
  59.5 0.7 collective-permute-start.3
  60.2 0.0 collective-permute-done.3.board_in
  60.2 0.0 collective-permute-done.4.halo_in
  60.2 3.9 %shard_map.106 = f32[8,128]{1,0:T(8,128)S(1)} custom-call(f32[16,128]{1,0:T(8,128)S(1)} %get-tuple-element.17.phases, bf16[16,64,128]{2,1,0:T(8,128)(2,1)S(1)} %copy-done, bf16[8,8,64,128]{3,2,1,0:T(8,128)(2,1)S(1)} %get-tuple-element.20.lefts, bf16[8,8,128,128]{3,2,1,0:T(8,128)(2,1)S(1)} %get-tuple-element.21.rights, f32[16,64,128]{2,1,0:T(8,128)S(1)} %copy-done.1, ...), custom_call_target="tpu_custom_call" | custom-call | tf_op jit(solution)/shard_map/pallas_call | solution.py:255
  64.1 0.1 collective-permute-start.5
  64.2 1.2 %collective-permute-done.5 = f32[8,128]{1,0:T(8,128)S(1)} collective-permute-done((f32[8,128]{1,0:T(8,128)S(1)}, f32[8,128]{1,0:T(8,128)S(1)}, u32[]{:S(2)}, u32[]{:S(2)}) %collective-permute-start.5) | collective-permute-done | bytes 4128 | tf_op jit(solution)/shard_map/ppermute | solution.py:285
  65.4 28.5 %all_to_all.11.blocks = f32[64,8,128]{2,1,0:T(8,128)S(1)} all-to-all(f32[64,8,128]{2,1,0:T(8,128)S(1)} %broadcast_in_dim.2), channel_id=1, replica_groups=mesh['s'=2,'xp'=2,'q'=2,'yp'=2,'z'=4,'c'=2] {'s','xp','q','yp','z'}, dimensions={0} | all-to-all | bytes 524288 | tf_op jit(solution)/shard_map/all_to_all | solution.py:293
  93.8 0.7 shard_map.107
  (4 shorter events, 0.1 us)
Async XLA Ops:
  2.4 33.2 %copy-start.2 = (f32[4,64]{1,0:T(4,128)S(1)}, f32[4,64]{1,0:T(4,128)}, u32[]{:S(2)}) copy-start(f32[4,64]{1,0:T(4,128)} %param.12) | copy-start | bytes 3076
  35.6 4.2 %copy-start = (bf16[16,64,128]{2,1,0:T(8,128)(2,1)S(1)}, bf16[16,64,128]{2,1,0:T(8,128)(2,1)}, u32[]{:S(2)}) copy-start(bf16[16,64,128]{2,1,0:T(8,128)(2,1)} %edge.5) | copy-start | bytes 786436
  35.6 4.2 %collective-permute-start = (f32[8,520,128]{2,1,0:T(8,128)S(1)}, f32[8,520,128]{2,1,0:T(8,128)S(1)}, u32[]{:S(2)}, u32[]{:S(2)}) collective-permute-start(f32[8,520,128]{2,1,0:T(8,128)S(1)} %all_to_all.10.mine), channel_id=1, source_target_pairs={{0,1},{1,0},{2,3},{3,2},{4,5},{5,4},{6,7},{7,6},{8,9},{9,8},{10,11... | collective-permute-start | bytes 6389768 | tf_op jit(solution)/shard_map/ppermute | solution.py:285
  39.8 15.1 %copy-start.1 = (f32[16,64,128]{2,1,0:T(8,128)S(1)}, f32[16,64,128]{2,1,0:T(8,128)}, u32[]{:S(2)}) copy-start(f32[16,64,128]{2,1,0:T(8,128)} %close.3) | copy-start | bytes 1572868
  44.6 10.3 %collective-permute-start.2 = (f32[528,128]{1,0:T(8,128)S(1)}, f32[528,128]{1,0:T(8,128)S(1)}, u32[]{:S(2)}, u32[]{:S(2)}) collective-permute-start(f32[528,128]{1,0:T(8,128)S(1)} %get-tuple-element.23), channel_id=1, source_target_pairs={{0,24},{8,16},{32,56},{40,48},{1,25},{9,17},{33,57},{41,49},{2,26}... | collective-permute-start | bytes 811016 | tf_op jit(solution)/shard_map/ppermute | solution.py:281
  47.7 7.2 %collective-permute-start.1 = (f32[520,128]{1,0:T(8,128)S(1)}, f32[520,128]{1,0:T(8,128)S(1)}, u32[]{:S(2)}, u32[]{:S(2)}) collective-permute-start(f32[520,128]{1,0:T(8,128)S(1)} %get-tuple-element.22), channel_id=1, source_target_pairs={{0,96},{8,104},{32,64},{40,72},{1,97},{9,105},{33,65},{41,73},{2,9... | collective-permute-start | bytes 798728 | tf_op jit(solution)/shard_map/ppermute | solution.py:276
  58.8 1.4 %collective-permute-start.4 = (f32[528,128]{1,0:T(8,128)S(1)}, f32[528,128]{1,0:T(8,128)S(1)}, u32[]{:S(2)}, u32[]{:S(2)}) collective-permute-start(f32[528,128]{1,0:T(8,128)S(1)} %get-tuple-element.25), channel_id=1, source_target_pairs={{64,88},{72,80},{96,120},{104,112},{65,89},{73,81},{97,121},{105,1... | collective-permute-start | bytes 811016 | tf_op jit(solution)/shard_map/ppermute | solution.py:281
  59.5 0.7 collective-permute-start.3
  64.1 1.2 %collective-permute-start.5 = (f32[8,128]{1,0:T(8,128)S(1)}, f32[8,128]{1,0:T(8,128)S(1)}, u32[]{:S(2)}, u32[]{:S(2)}) collective-permute-start(f32[8,128]{1,0:T(8,128)S(1)} %shard_map.106), channel_id=1, source_target_pairs={{0,1},{1,0},{2,3},{3,2},{4,5},{5,4},{6,7},{7,6},{8,9},{9,8},{10,11... | collective-permute-start | bytes 12296 | tf_op jit(solution)/shard_map/ppermute | solution.py:285

commit v4 on v3

--- a/solution.py
+++ b/solution.py
@@ -8,8 +8,8 @@
 from jax.sharding import Mesh
 from jax.sharding import PartitionSpec as P
 
-AXES = ("s", "xp", "q", "yp", "z", "c")
-GRID = ("s", "xp", "q", "yp")
+AXES = ("s", "xp", "yh", "q", "z", "c")
+GRID = ("s", "xp", "yh", "q")
 NC = 8
 NR = 8
 W = 64
@@ -61,9 +61,8 @@
         copies[n].wait()
         x = raw[n].astype(F32)
         half, row = n // 8, n % 8
-        for xp in range(2):
-            for yp in range(2):
-                out[4 * xp + 2 * half + yp, pl.ds(W * row, W), :] = x
+        for dest in range(half, 8, 2):
+            out[dest, pl.ds(W * row, W), :] = x
 
 
 def unpack(source, part, lefts, rights, sign):
@@ -96,23 +95,28 @@
     return high, (x - high.astype(F32)).astype(BF16)
 
 
-def sweep(state, lefts, rights, phases, halo_in, halo_out, peaks, start, sign):
+def sweep(state, turned, lefts, rights, phases, halo_in, halo_out, peaks, start, sign):
     def column(j, carry):
         p, rho_mix, rho = carry
         scale = 1.0 / p
         cos_row = phases[pl.ds(j, 1), :] * scale
         sin_row = phases[pl.ds(NC + j, 1), :] * scale
+        cos_turn = cos_row * sign
+        sin_turn = sin_row * sign
         boards = [state[k] for k in range(NR)]
+        turns = [turned[k] for k in range(NR)]
         halo_out[pl.ds(j * W, W), :] = boards[0]
         if halo_in is None:
-            below = None
+            below = below_turn = None
         else:
             below = halo_in[pl.ds(j * W, W), :] * rho_mix
+            below_turn = times_i(below, sign)
         top = jnp.zeros((8, 2 * W), F32)
         for k in range(NR):
             after = boards[k + 1] if k + 1 < NR else below
             mixed = boards[k] if after is None else boards[k] + 0.5 * after
-            turn = times_i(mixed, sign)
+            after = turns[k + 1] if k + 1 < NR else below_turn
+            turn = turns[k] if after is None else turns[k] + 0.5 * after
             mh, ml = halves(mixed)
             th, tl = halves(turn)
             both = jnp.dot(
@@ -125,9 +129,11 @@
             two = jnp.dot(
                 jnp.concatenate([dh, dl], 0), rights[j, k], preferred_element_type=F32
             )
-            out = two[:W] + two[W:]
-            out = out * cos_row + pltpu.roll(out, W, 1) * sin_row
+            plain = two[:W] + two[W:]
+            flip = pltpu.roll(plain, W, 1)
+            out = plain * cos_row + flip * sin_row
             state[k] = out
+            turned[k] = flip * cos_turn - plain * sin_turn
             for g in range(8):
                 top = jnp.maximum(top, jnp.abs(out[8 * g : 8 * g + 8]))
         own_top = jnp.broadcast_to(jnp.max(top, keepdims=True), (1, 2 * W))
@@ -178,26 +184,30 @@
 def places():
     s, q = lax.axis_index("s"), lax.axis_index("q")
     i = jnp.where(s == 0, lax.axis_index("xp"), 1 - lax.axis_index("xp"))
-    j = jnp.where(q == 0, lax.axis_index("yp"), 1 - lax.axis_index("yp"))
+    stays = jnp.logical_or(q == 0, lax.axis_index("c") == 1)
+    j = jnp.where(stays, lax.axis_index("yh"), 1 - lax.axis_index("yh"))
     return s, q, 2 * i + j, (1 - q) * NR
 
 
-def first_kernel(other, lefts_in, rights_in, phases, edge, lefts, rights, board_out, halo_out, state, peaks):
+def first_kernel(other, lefts_in, rights_in, phases, edge, lefts, rights, board_out, halo_out, state, turned, peaks):
     s, q, own, base = places()
     sign = sign_row()
     one = jnp.ones((1, 2 * W), F32)
     unpack(other, 1 - lax.axis_index("c"), lefts, rights, sign)
     for k in range(NR):
         state[k] = edge[base + k].astype(F32)
-    end = sweep(state, lefts, rights, phases, None, halo_out, peaks, (one, one, one), sign)
+        turned[k] = times_i(state[k], sign)
+    end = sweep(state, turned, lefts, rights, phases, None, halo_out, peaks, (one, one, one), sign)
     write_messages(state, board_out, halo_out, peaks, 0.0 * one, end, None)
 
 
-def load_state(state, edge, board_in, base, s):
+def load_state(state, turned, edge, board_in, base, s, sign):
     one = jnp.ones((1, 2 * W), F32)
     first = s == 0
     for k in range(NR):
-        state[k] = jnp.where(first, edge[base + k].astype(F32), board_in[pl.ds(k * W, W), :])
+        x = jnp.where(first, edge[base + k].astype(F32), board_in[pl.ds(k * W, W), :])
+        state[k] = x
+        turned[k] = times_i(x, sign)
     row = lambda n: board_in[pl.ds(NR * W + n, 1), :]
     p = jnp.maximum(jnp.where(first, one, row(0)), 1.0)
     rho_mix = jnp.where(first, one, row(1))
@@ -206,21 +216,21 @@
     return (p, rho_mix, rho), ell
 
 
-def second_kernel(phases, edge, lefts, rights, close, board_in, halo_in, board_out, halo_out, state, peaks):
+def second_kernel(phases, edge, lefts, rights, close, board_in, halo_in, board_out, halo_out, state, turned, peaks):
     s, q, own, base = places()
     sign = sign_row()
-    start, ell = load_state(state, edge, board_in, base, s)
-    end = sweep(state, lefts, rights, phases, halo_in, halo_out, peaks, start, sign)
+    start, ell = load_state(state, turned, edge, board_in, base, s, sign)
+    end = sweep(state, turned, lefts, rights, phases, halo_in, halo_out, peaks, start, sign)
     write_messages(
         state, board_out, halo_out, peaks, ell, end, close_sums(state, close, base, sign)
     )
 
 
-def third_kernel(phases, edge, lefts, rights, close, board_in, halo_in, out, state, peaks, halo_out):
+def third_kernel(phases, edge, lefts, rights, close, board_in, halo_in, out, state, turned, peaks, halo_out):
     s, q, own, base = places()
     sign = sign_row()
-    start, ell = load_state(state, edge, board_in, base, s)
-    p, rho_mix, rho = sweep(state, lefts, rights, phases, halo_in, halo_out, peaks, start, sign)
+    start, ell = load_state(state, turned, edge, board_in, base, s, sign)
+    p, rho_mix, rho = sweep(state, turned, lefts, rights, phases, halo_in, halo_out, peaks, start, sign)
     ell = ell + jnp.sum(jnp.log(peaks[...]), axis=0, keepdims=True)
     real, imag = close_sums(state, close, base, sign)
     factor = 1.0 / math.sqrt(2 * NR * W * W)
@@ -228,27 +238,27 @@
     imag = (imag + rho_mix * halo_in[pl.ds(NC * W + 9, 1), :]) / p * factor
     index = 4 * (2 * lax.axis_index("z") + lax.axis_index("c")) + own
     lane = lax.broadcasted_iota(jnp.int32, (1, 2 * W), 1)
-    index = jnp.where(jnp.logical_and(s == 1, q == 1), index, -1)
-    hit = lane == index
-    zero = jnp.zeros((1, 2 * W), F32)
-    out[pl.ds(0, 1), :] = jnp.where(hit, real, zero)
-    out[pl.ds(1, 1), :] = jnp.where(hit, imag, zero)
-    out[pl.ds(2, 1), :] = jnp.where(hit, ell, zero)
-    out[pl.ds(3, 5), :] = jnp.zeros((5, 2 * W), F32)
+    index = jnp.where(jnp.logical_and(s == 1, q == 1), index, -128)
+    row = jnp.where(lane == index, real, 0.0)
+    row = row + jnp.where(lane == index + 32, imag, 0.0)
+    row = row + jnp.where(lane == index + 64, ell, 0.0)
+    out[...] = row
 
 
 def finish_kernel(blocks, amps, logs, total, top):
-    found = jnp.sum(blocks[...], axis=0)
-    ell = found[2:3]
-    high = jnp.max(ell, axis=1, keepdims=True)
-    weighted = found[0:2] * jnp.exp(ell - high)
+    found = jnp.sum(blocks[...], axis=0, keepdims=True)
+    real, imag, ell = found, pltpu.roll(found, 96, 1), pltpu.roll(found, 64, 1)
+    used = lax.broadcasted_iota(jnp.int32, (1, 2 * W), 1) < 32
+    high = jnp.max(jnp.where(used, ell, 0.0), axis=1, keepdims=True)
+    weight = jnp.where(used, jnp.exp(jnp.where(used, ell - high, 0.0)), 0.0)
     top[...] = high
-    sums = jnp.sum(weighted, axis=1, keepdims=True)
-    total[...] = jnp.concatenate([sums[0:1], sums[1:2]], 1)
+    sums = [jnp.sum(x * weight, axis=1, keepdims=True) for x in (real, imag)]
+    total[...] = jnp.concatenate(sums, 1)
     at = 4 * (2 * lax.axis_index("z") + lax.axis_index("c"))
-    here = pltpu.roll(found, jnp.where(at == 0, 0, 2 * W - at), 1)
-    amps[...] = here[0:2, 0:4]
-    logs[...] = here[2:3, 0:4]
+    shift = jnp.where(at == 0, 0, 2 * W - at)
+    amps[0:1, :] = pltpu.roll(real, shift, 1)[:, 0:4]
+    amps[1:2, :] = pltpu.roll(imag, shift, 1)[:, 0:4]
+    logs[...] = pltpu.roll(ell, shift, 1)[:, 0:4]
 
 
 def call(kernel, outs, scratch, args, specs=None, aliases=None):
@@ -267,18 +277,23 @@
     return jax.ShapeDtypeStruct(dims, dtype)
 
 
-def chip(s, xp, q, yp):
-    return 8 * s + 4 * xp + 2 * q + yp
+def chip(s, xp, yh, q):
+    return 8 * s + 4 * xp + 2 * yh + q
 
 
 def along_columns(value, q):
-    pairs = [(chip(0, xp, q, yp), chip(1, 1 - xp, q, yp)) for xp in range(2) for yp in range(2)]
+    pairs = [(chip(0, xp, yh, q), chip(1, 1 - xp, yh, q)) for xp in range(2) for yh in range(2)]
     return lax.ppermute(value, GRID, pairs)
 
 
 def along_rows(value, s):
-    pairs = [(chip(s, xp, 0, yp), chip(s, xp, 1, 1 - yp)) for xp in range(2) for yp in range(2)]
-    return lax.ppermute(value, GRID, pairs)
+    pairs = []
+    for xp in range(2):
+        for yh in range(2):
+            source = 2 * chip(s, xp, yh, 0)
+            pairs.append((source, 2 * chip(s, xp, 1 - yh, 1)))
+            pairs.append((source + 1, 2 * chip(s, xp, yh, 1) + 1))
+    return lax.ppermute(value, (*GRID, "c"), pairs)
 
 
 def swapped(value):
@@ -286,11 +301,9 @@
 
 
 def gathered(found):
-    found = found + swapped(found)
-    chips = (*GRID, "z")
-    count = lax.axis_size(chips)
+    count = lax.axis_size(AXES)
     spread = jnp.broadcast_to(found[None], (count, *found.shape))
-    return lax.all_to_all(spread, chips, 0, 0, tiled=True)
+    return lax.all_to_all(spread, AXES, 0, 0, tiled=True).reshape(count, found.shape[1])
 
 
 def body(layout, assign, edge, gate_left, gate_right, phase_angle, close):
@@ -313,7 +326,7 @@
         ],
         [hbm, hbm, hbm, hbm],
     )
-    mine = lax.all_to_all(packed, ("xp", "q", "yp"), 0, 0, tiled=True)
+    mine = lax.all_to_all(packed, ("xp", "yh", "q"), 0, 0, tiled=True)
     other = swapped(mine)
     state = pltpu.VMEM((NR, W, 2 * W), F32)
     peaks = pltpu.VMEM((NC, 2 * W), F32)
@@ -324,7 +337,7 @@
     lefts, rights, board, halo = call(
         first_kernel,
         (*gates, shape(BOARD, 2 * W), shape(HALO, 2 * W)),
-        [state, peaks],
+        [state, state, peaks],
         (other, lefts, rights, phases, edge),
         aliases={1: 0, 2: 1},
     )
@@ -332,14 +345,14 @@
     board, halo = call(
         second_kernel,
         (shape(BOARD, 2 * W), shape(HALO, 2 * W)),
-        [state, peaks],
+        [state, state, peaks],
         (phases, edge, lefts, rights, close, board, halo),
     )
     board, halo = along_columns(board, 1), along_rows(halo, 1)
     found = call(
         third_kernel,
-        shape(8, 2 * W),
-        [state, peaks, pltpu.VMEM((HALO, 2 * W), F32)],
+        shape(1, 2 * W),
+        [state, state, peaks, pltpu.VMEM((HALO, 2 * W), F32)],
         (phases, edge, lefts, rights, close, board, halo),
     )
     amps, logs, total_amp, top_log = call(

time: 94.9 us -> 89.4 us (0.942)
  blocking collectives: 61.7 us -> 58.5 us
  Pallas kernels: 15.9 us -> 14.6 us
  waiting for transfers between devices: 10.3 us -> 9.07 us
    all_to_all x2, blocking collectives: 61.7 us -> 58.5 us  [the longest x1 33.1 us: body(): mine = lax.all_to_all(packed, ('xp', 'yh', 'q'), 0, 0, tiled=True)]
    pallas_call x6, Pallas kernels: 15.9 us -> 14.6 us  [call(): pl.pallas_call(kernel, out_shape=outs, in_specs=specs or [vmem()] * len(a...]
    ppermute x2 -> x1, waiting for transfers between devices: 4.33 us -> 3.18 us  [swapped(): return lax.ppermute(value, 'c', [(0, 1), (1, 0)])]
  transfers between devices with their start and end apart: 6 -> 5, of which waited for: 3 -> 2; matrix products, arithmetic and copies ran while one was open for 0% -> 0% of each run, Pallas kernels for 1% -> 1%
where the time goes in v4:
time: 89.4 us; the launch traced here: 88.9 us
  blocking collectives  58.5 us (65%)
  Pallas kernels  14.6 us (16%)
  waiting for transfers between devices  9.07 us (10%)
  starting transfers between devices  5.75 us (6%)
    all_to_all x1, blocking collectives, body(): mine = lax.all_to_all(packed, ('xp', 'yh', 'q'), 0, 0, tiled=True)  33.1 us
    all_to_all x1, blocking collectives, gathered(): lax.all_to_all(spread, AXES, 0, 0, tiled=True)  25.4 us
    pallas_call x6, Pallas kernels, call(): pl.pallas_call(kernel, out_shape=outs, in_specs=specs or [vmem()] * len(a...  14.6 us
    ppermute x2, waiting for transfers between devices, along_columns(): return lax.ppermute(value, GRID, pairs)  5.89 us
    ppermute x2, starting transfers between devices, along_rows(): return lax.ppermute(value, (*GRID, 'c'), pairs)  3.76 us
    ppermute x1, waiting for transfers between devices, swapped(): return lax.ppermute(value, 'c', [(0, 1), (1, 0)])  3.18 us
    ppermute x2, starting transfers between devices, along_columns(): return lax.ppermute(value, GRID, pairs)  1.98 us
  transfers between devices with their start and end apart: 5, of which 2 were waited for; matrix products, arithmetic and copies ran while one was open for 0% of the time, Pallas kernels for 1%

profile of v4, /device:TPU:0, one launch (start us, length us, event | category | flops | bytes accessed | tf_op | source)
XLA Modules:
  0.0 88.9 jit_solution(4404296733825703274)
XLA Ops:
  0.6 1.9 %shard_map.102 = f32[8,520,128]{2,1,0:T(8,128)S(1)} custom-call(s32[1,16]{1,0:T(1,128)} %bitcast.10, s32[1,4]{1,0:T(1,128)} %bitcast.11, bf16[1,16,64,128]{3,2,1,0:T(8,128)(2,1)} %left.1, bf16[1,16,64,128]{3,2,1,0:T(8,128)(2,1)} %right.1), custom_call_target="tpu_custom_call" | custom-call | tf_op jit(solution)/shard_map/pallas_call | solution.py:265
  2.5 0.0 copy-start.2
  2.5 33.1 %all_to_all.10.mine = f32[8,520,128]{2,1,0:T(8,128)S(1)} all-to-all(f32[8,520,128]{2,1,0:T(8,128)S(1)} %shard_map.102), channel_id=1, replica_groups=mesh['s'=2,'xp'=2,'yh'=2,'q'=2,'z'=4,'c'=2] {'xp','yh','q'}, dimensions={0} | all-to-all | bytes 4259840 | tf_op jit(solution)/shard_map/all_to_all | solution.py:329
  35.6 0.0 copy-start
  35.6 0.0 collective-permute-start
  35.6 0.0 copy-done.2
  35.7 0.1 pad_maximum_fusion
  35.7 0.9 shard_map.103
  36.6 3.2 %collective-permute-done.other = f32[8,520,128]{2,1,0:T(8,128)S(1)} collective-permute-done((f32[8,520,128]{2,1,0:T(8,128)S(1)}, f32[8,520,128]{2,1,0:T(8,128)S(1)}, u32[]{:S(2)}, u32[]{:S(2)}) %collective-permute-start) | collective-permute-done | bytes 2129952 | tf_op jit(solution)/shard_map/ppermute | solution.py:300
  39.8 0.0 copy-done
  39.8 0.0 copy-start.1
  39.8 4.3 %shard_map.104 = (bf16[8,8,64,128]{3,2,1,0:T(8,128)(2,1)S(1)}, bf16[8,8,128,128]{3,2,1,0:T(8,128)(2,1)S(1)}, f32[520,128]{1,0:T(8,128)S(1)}, f32[528,128]{1,0:T(8,128)S(1)}) custom-call(f32[8,520,128]{2,1,0:T(8,128)S(1)} %collective-permute-done.other, ...), custom_call_target="tpu_custom_call", output_to_operand_aliasing={{0}: (1, {}), {1}: (2, {})} | custom-call | tf_op jit(solution)/shard_map/pallas_call | solution.py:265
  44.1 3.1 %collective-permute-start.2 = (f32[528,128]{1,0:T(8,128)S(1)}, f32[528,128]{1,0:T(8,128)S(1)}, u32[]{:S(2)}, u32[]{:S(2)}) collective-permute-start(f32[528,128]{1,0:T(8,128)S(1)} %get-tuple-element.23), channel_id=1, source_target_pairs={{0,24},{1,9},{16,8},{17,25},{32,56},{33,41},{48,40},{49,57},{2,26}... | collective-permute-start | bytes 811016 | tf_op jit(solution)/shard_map/ppermute | solution.py:296
  47.2 1.3 %collective-permute-start.1 = (f32[520,128]{1,0:T(8,128)S(1)}, f32[520,128]{1,0:T(8,128)S(1)}, u32[]{:S(2)}, u32[]{:S(2)}) collective-permute-start(f32[520,128]{1,0:T(8,128)S(1)} %get-tuple-element.22), channel_id=1, source_target_pairs={{0,96},{16,112},{32,64},{48,80},{1,97},{17,113},{33,65},{49,81},{2... | collective-permute-start | bytes 798728 | tf_op jit(solution)/shard_map/ppermute | solution.py:286
  48.5 5.9 %collective-permute-done.1.board_in = f32[520,128]{1,0:T(8,128)S(1)} collective-permute-done((f32[520,128]{1,0:T(8,128)S(1)}, f32[520,128]{1,0:T(8,128)S(1)}, u32[]{:S(2)}, u32[]{:S(2)}) %collective-permute-start.1) | collective-permute-done | bytes 266272 | tf_op jit(solution)/shard_map/ppermute | solution.py:286
  54.4 0.0 collective-permute-done.2.halo_in
  54.4 0.0 copy-done.1
  54.4 3.4 %shard_map.105 = (f32[520,128]{1,0:T(8,128)S(1)}, f32[528,128]{1,0:T(8,128)S(1)}) custom-call(f32[16,128]{1,0:T(8,128)S(1)} %get-tuple-element.17.phases, bf16[16,64,128]{2,1,0:T(8,128)(2,1)S(1)} %copy-done, bf16[8,8,64,128]{3,2,1,0:T(8,128)(2,1)S(1)} %get-tuple-element.20.lefts, bf16[8,8,128,128]{3,2,1,0:T(8,128)(2,1)S(1)} %get-tuple-element.21.rights, ...), custom_call_target="tpu_custom_call" | custom-call | tf_op jit(solution)/shard_map/pallas_call | solution.py:265
  57.8 0.7 collective-permute-start.4
  58.5 0.7 collective-permute-start.3
  59.2 0.0 collective-permute-done.3.board_in
  59.2 0.0 collective-permute-done.4.halo_in
  59.2 3.4 %shard_map.106 = f32[1,128]{1,0:T(1,128)S(1)} custom-call(f32[16,128]{1,0:T(8,128)S(1)} %get-tuple-element.17.phases, bf16[16,64,128]{2,1,0:T(8,128)(2,1)S(1)} %copy-done, bf16[8,8,64,128]{3,2,1,0:T(8,128)(2,1)S(1)} %get-tuple-element.20.lefts, bf16[8,8,128,128]{3,2,1,0:T(8,128)(2,1)S(1)} %get-tuple-element.21.rights, f32[16,64,128]{2,1,0:T(8,128)S(1)} %copy-done.1, ...), custom_call_target="tpu_custom_call" | custom-call | tf_op jit(solution)/shard_map/pallas_call | solution.py:265
  62.6 25.4 %all_to_all.11 = f32[128,1,128]{2,1,0:T(1,128)S(1)} all-to-all(f32[128,1,128]{2,1,0:T(1,128)S(1)} %broadcast_in_dim.9), channel_id=1, replica_groups=mesh['s'=2,'xp'=2,'yh'=2,'q'=2,'z'=4,'c'=2] {'s','xp','yh','q','z','c'}, dimensions={0} | all-to-all | bytes 131072 | tf_op jit(solution)/shard_map/all_to_all | solution.py:306
  88.1 0.8 shard_map.107
  (3 shorter events, 0.1 us)
Async XLA Ops:
  2.5 33.1 %copy-start.2 = (f32[4,64]{1,0:T(4,128)S(1)}, f32[4,64]{1,0:T(4,128)}, u32[]{:S(2)}) copy-start(f32[4,64]{1,0:T(4,128)} %param.12) | copy-start | bytes 3076
  35.6 4.2 %copy-start = (bf16[16,64,128]{2,1,0:T(8,128)(2,1)S(1)}, bf16[16,64,128]{2,1,0:T(8,128)(2,1)}, u32[]{:S(2)}) copy-start(bf16[16,64,128]{2,1,0:T(8,128)(2,1)} %edge.5) | copy-start | bytes 786436
  35.6 4.2 %collective-permute-start = (f32[8,520,128]{2,1,0:T(8,128)S(1)}, f32[8,520,128]{2,1,0:T(8,128)S(1)}, u32[]{:S(2)}, u32[]{:S(2)}) collective-permute-start(f32[8,520,128]{2,1,0:T(8,128)S(1)} %all_to_all.10.mine), channel_id=1, source_target_pairs={{0,1},{1,0},{2,3},{3,2},{4,5},{5,4},{6,7},{7,6},{8,9},{9,8},{10,11... | collective-permute-start | bytes 6389768 | tf_op jit(solution)/shard_map/ppermute | solution.py:300
  39.8 14.6 %copy-start.1 = (f32[16,64,128]{2,1,0:T(8,128)S(1)}, f32[16,64,128]{2,1,0:T(8,128)}, u32[]{:S(2)}) copy-start(f32[16,64,128]{2,1,0:T(8,128)} %close.3) | copy-start | bytes 1572868
  44.1 10.3 %collective-permute-start.2 = (f32[528,128]{1,0:T(8,128)S(1)}, f32[528,128]{1,0:T(8,128)S(1)}, u32[]{:S(2)}, u32[]{:S(2)}) collective-permute-start(f32[528,128]{1,0:T(8,128)S(1)} %get-tuple-element.23), channel_id=1, source_target_pairs={{0,24},{1,9},{16,8},{17,25},{32,56},{33,41},{48,40},{49,57},{2,26}... | collective-permute-start | bytes 811016 | tf_op jit(solution)/shard_map/ppermute | solution.py:296
  47.2 7.2 %collective-permute-start.1 = (f32[520,128]{1,0:T(8,128)S(1)}, f32[520,128]{1,0:T(8,128)S(1)}, u32[]{:S(2)}, u32[]{:S(2)}) collective-permute-start(f32[520,128]{1,0:T(8,128)S(1)} %get-tuple-element.22), channel_id=1, source_target_pairs={{0,96},{16,112},{32,64},{48,80},{1,97},{17,113},{33,65},{49,81},{2... | collective-permute-start | bytes 798728 | tf_op jit(solution)/shard_map/ppermute | solution.py:286
  57.8 1.4 %collective-permute-start.4 = (f32[528,128]{1,0:T(8,128)S(1)}, f32[528,128]{1,0:T(8,128)S(1)}, u32[]{:S(2)}, u32[]{:S(2)}) collective-permute-start(f32[528,128]{1,0:T(8,128)S(1)} %get-tuple-element.25), channel_id=1, source_target_pairs={{64,88},{65,73},{80,72},{81,89},{96,120},{97,105},{112,104},{113,1... | collective-permute-start | bytes 811016 | tf_op jit(solution)/shard_map/ppermute | solution.py:296
  58.5 0.7 collective-permute-start.3

commit v5 on v4

--- a/solution.py
+++ b/solution.py
@@ -33,54 +33,51 @@
     return pltpu.roll(x, W, 1) * sign
 
 
-def pack_kernel(layout_hbm, assign_hbm, left, right, out, layout, assign, raw, sems):
+def pack_kernel(layout_hbm, assign_hbm, left_hbm, right_hbm, out, layout, assign, left, right, sems):
     core = lax.axis_index("c")
-    small = [
-        pltpu.make_async_copy(layout_hbm, layout, sems.at[16]),
-        pltpu.make_async_copy(assign_hbm, assign, sems.at[17]),
+    copies = [
+        pltpu.make_async_copy(layout_hbm, layout, sems.at[0]),
+        pltpu.make_async_copy(assign_hbm, assign, sems.at[1]),
+        pltpu.make_async_copy(left_hbm, left, sems.at[2]),
+        pltpu.make_async_copy(right_hbm, right, sems.at[3]),
     ]
-    for copy in small:
+    for copy in copies:
         copy.start()
-    for copy in small:
+    for dest in range(8):
+        out[dest, pl.ds(8 * W + 4, 4), :] = jnp.zeros((4, 2 * W), F32)
+    for copy in copies:
         copy.wait()
-    copies = []
-    for half in range(2):
-        for k in range(4):
-            kind = layout[0, (1 - half) * NR + 4 * core + k]
-            for side, table in ((0, left), (1, right)):
-                n = 8 * half + 2 * k + side
-                copies.append(pltpu.make_async_copy(table.at[0, kind], raw.at[n], sems.at[n]))
-                copies[-1].start()
     for t in range(4):
         row = jnp.full((1, 2 * W), assign[0, t].astype(F32), F32)
         for dest in range(8):
             out[dest, pl.ds(8 * W + t, 1), :] = row
-    for dest in range(8):
-        out[dest, pl.ds(8 * W + 4, 4), :] = jnp.zeros((4, 2 * W), F32)
-    for n in range(16):
-        copies[n].wait()
-        x = raw[n].astype(F32)
-        half, row = n // 8, n % 8
-        for dest in range(half, 8, 2):
-            out[dest, pl.ds(W * row, W), :] = x
-
-
-def unpack(source, part, lefts, rights, sign):
+    for half in range(2):
+        for k in range(4):
+            kind = layout[0, (1 - half) * NR + 4 * core + k]
+            for n, table in ((2 * k, left), (2 * k + 1, right)):
+                x = table[0, kind].astype(F32)
+                for dest in range(half, 8, 2):
+                    out[dest, pl.ds(W * n, W), :] = x
+
+
+def unpack_column(source, j, part, lefts, rights, sign):
+    for k in range(4):
+        row = 4 * part + k
+        lefts[j, row] = source[j, pl.ds(2 * W * k, W), :].astype(BF16)
+        r = source[j, pl.ds(2 * W * k + W, W), :]
+        rights[j, row, pl.ds(0, W), :] = r.astype(BF16)
+        rights[j, row, pl.ds(W, W), :] = times_i(r, sign).astype(BF16)
+
+
+def unpack_kernel(mine, cosine, sine, lefts, rights, phases):
+    _, _, own, _ = places()
+    part, sign = lax.axis_index("c"), sign_row()
+
     def place(j, unused):
-        for k in range(4):
-            row = 4 * part + k
-            lefts[j, row] = source[j, pl.ds(2 * W * k, W), :].astype(BF16)
-            r = source[j, pl.ds(2 * W * k + W, W), :]
-            rights[j, row, pl.ds(0, W), :] = r.astype(BF16)
-            rights[j, row, pl.ds(W, W), :] = times_i(r, sign).astype(BF16)
+        unpack_column(mine, j, part, lefts, rights, sign)
         return unused
 
     lax.fori_loop(0, NC, place, 0)
-
-
-def unpack_kernel(mine, cosine, sine, lefts, rights, phases):
-    s, q, own, base = places()
-    unpack(mine, lax.axis_index("c"), lefts, rights, sign_row())
     for j in range(NC):
         value = mine[j, pl.ds(8 * W + own, 1), :]
         for n, table in ((0, cosine), (NC, sine)):
@@ -95,7 +92,7 @@
     return high, (x - high.astype(F32)).astype(BF16)
 
 
-def sweep(state, turned, lefts, rights, phases, halo_in, halo_out, peaks, start, sign):
+def sweep(state, turned, lefts, rights, phases, halo_in, halo_out, peaks, start, sign, prepare=None):
     def column(j, carry):
         p, rho_mix, rho = carry
         scale = 1.0 / p
@@ -147,7 +144,11 @@
         return (p_new, rho, rho * jnp.maximum(other_top, 1.0) / p_new)
 
     carry = start
+    if prepare is not None:
+        prepare(0)
     for j in range(NC):
+        if prepare is not None and j + 1 < NC:
+            prepare(j + 1)
         carry = column(j, carry)
     return carry
 
@@ -190,14 +191,17 @@
 
 
 def first_kernel(other, lefts_in, rights_in, phases, edge, lefts, rights, board_out, halo_out, state, turned, peaks):
-    s, q, own, base = places()
+    _, _, _, base = places()
     sign = sign_row()
     one = jnp.ones((1, 2 * W), F32)
-    unpack(other, 1 - lax.axis_index("c"), lefts, rights, sign)
+    part = 1 - lax.axis_index("c")
     for k in range(NR):
         state[k] = edge[base + k].astype(F32)
         turned[k] = times_i(state[k], sign)
-    end = sweep(state, turned, lefts, rights, phases, None, halo_out, peaks, (one, one, one), sign)
+    prepare = lambda j: unpack_column(other, j, part, lefts, rights, sign)
+    end = sweep(
+        state, turned, lefts, rights, phases, None, halo_out, peaks, (one, one, one), sign, prepare
+    )
     write_messages(state, board_out, halo_out, peaks, 0.0 * one, end, None)
 
 
@@ -217,7 +221,7 @@
 
 
 def second_kernel(phases, edge, lefts, rights, close, board_in, halo_in, board_out, halo_out, state, turned, peaks):
-    s, q, own, base = places()
+    s, _, _, base = places()
     sign = sign_row()
     start, ell = load_state(state, turned, edge, board_in, base, s, sign)
     end = sweep(state, turned, lefts, rights, phases, halo_in, halo_out, peaks, start, sign)
@@ -230,7 +234,7 @@
     s, q, own, base = places()
     sign = sign_row()
     start, ell = load_state(state, turned, edge, board_in, base, s, sign)
-    p, rho_mix, rho = sweep(state, turned, lefts, rights, phases, halo_in, halo_out, peaks, start, sign)
+    p, rho_mix, _ = sweep(state, turned, lefts, rights, phases, halo_in, halo_out, peaks, start, sign)
     ell = ell + jnp.sum(jnp.log(peaks[...]), axis=0, keepdims=True)
     real, imag = close_sums(state, close, base, sign)
     factor = 1.0 / math.sqrt(2 * NR * W * W)
@@ -317,8 +321,9 @@
         [
             pltpu.SMEM((1, 16), jnp.int32),
             pltpu.SMEM((1, 4), jnp.int32),
-            pltpu.VMEM((16, W, 2 * W), BF16),
-            pltpu.SemaphoreType.DMA((18,)),
+            pltpu.VMEM(gate_left.shape, BF16),
+            pltpu.VMEM(gate_right.shape, BF16),
+            pltpu.SemaphoreType.DMA((4,)),
         ],
         [
             pltpu.with_memory_space_constraint(x, pltpu.HBM)
@@ -341,7 +346,8 @@
         (other, lefts, rights, phases, edge),
         aliases={1: 0, 2: 1},
     )
-    board, halo = along_columns(board, 0), along_rows(halo, 0)
+    board = along_columns(board, 0)
+    halo = along_rows(halo, 0)
     board, halo = call(
         second_kernel,
         (shape(BOARD, 2 * W), shape(HALO, 2 * W)),

time: 89.4 us -> 88 us (0.984)
  Pallas kernels: 14.6 us -> 13.2 us
    pallas_call x6, Pallas kernels: 14.6 us -> 13.2 us  [call(): pl.pallas_call(kernel, out_shape=outs, in_specs=specs or [vmem()] * len(a...]
where the time goes in v5:
time: 88 us; the launch traced here: 87.5 us
  blocking collectives  58.5 us (66%)
  Pallas kernels  13.2 us (15%)
  waiting for transfers between devices  9.12 us (10%)
  starting transfers between devices  5.78 us (7%)
    all_to_all x1, blocking collectives, body(): mine = lax.all_to_all(packed, ('xp', 'yh', 'q'), 0, 0, tiled=True)  33.1 us
    all_to_all x1, blocking collectives, gathered(): lax.all_to_all(spread, AXES, 0, 0, tiled=True)  25.4 us
    pallas_call x6, Pallas kernels, call(): pl.pallas_call(kernel, out_shape=outs, in_specs=specs or [vmem()] * len(a...  13.2 us
    ppermute x2, waiting for transfers between devices, along_columns(): return lax.ppermute(value, GRID, pairs)  5.93 us
    ppermute x2, starting transfers between devices, along_rows(): return lax.ppermute(value, (*GRID, 'c'), pairs)  3.76 us
    ppermute x1, waiting for transfers between devices, swapped(): return lax.ppermute(value, 'c', [(0, 1), (1, 0)])  3.18 us
    ppermute x2, starting transfers between devices, along_columns(): return lax.ppermute(value, GRID, pairs)  2.02 us
  transfers between devices with their start and end apart: 5, of which 2 were waited for; matrix products, arithmetic and copies ran while one was open for 0% of the time, Pallas kernels for 1%

profile of v5, /device:TPU:0, one launch (start us, length us, event | category | flops | bytes accessed | tf_op | source)
XLA Modules:
  0.0 87.5 jit_solution(3736175366069724957)
XLA Ops:
  0.6 1.2 %shard_map.102 = f32[8,520,128]{2,1,0:T(8,128)S(1)} custom-call(s32[1,16]{1,0:T(1,128)} %bitcast.10, s32[1,4]{1,0:T(1,128)} %bitcast.11, bf16[1,16,64,128]{3,2,1,0:T(8,128)(2,1)} %left_hbm.1, bf16[1,16,64,128]{3,2,1,0:T(8,128)(2,1)} %right_hbm.1), custom_call_target="tpu_custom_call" | custom-call | tf_op jit(solution)/shard_map/pallas_call | solution.py:269
  1.9 0.0 copy-start.2
  1.9 33.1 %all_to_all.10.mine = f32[8,520,128]{2,1,0:T(8,128)S(1)} all-to-all(f32[8,520,128]{2,1,0:T(8,128)S(1)} %shard_map.102), channel_id=1, replica_groups=mesh['s'=2,'xp'=2,'yh'=2,'q'=2,'z'=4,'c'=2] {'xp','yh','q'}, dimensions={0} | all-to-all | bytes 4259840 | tf_op jit(solution)/shard_map/all_to_all | solution.py:334
  35.0 0.0 copy-start
  35.0 0.0 collective-permute-start
  35.0 0.0 copy-done.2
  35.0 0.1 pad_maximum_fusion
  35.1 0.9 %shard_map.103 = (bf16[8,8,64,128]{3,2,1,0:T(8,128)(2,1)S(1)}, bf16[8,8,128,128]{3,2,1,0:T(8,128)(2,1)S(1)}, f32[16,128]{1,0:T(8,128)S(1)}) custom-call(f32[8,520,128]{2,1,0:T(8,128)S(1)} %all_to_all.10.mine, f32[4,128]{1,0:T(4,128)S(1)} %get-tuple-element.32.cosine, f32[4,128]{1,0:T(4,128)S(1)} %get-tuple-element.33.sine), custom_call_target="tpu_custom_call" | custom-call | tf_op jit(solution)/shard_map/pallas_call | solution.py:269
  36.0 3.2 %collective-permute-done.other = f32[8,520,128]{2,1,0:T(8,128)S(1)} collective-permute-done((f32[8,520,128]{2,1,0:T(8,128)S(1)}, f32[8,520,128]{2,1,0:T(8,128)S(1)}, u32[]{:S(2)}, u32[]{:S(2)}) %collective-permute-start) | collective-permute-done | bytes 2129952 | tf_op jit(solution)/shard_map/ppermute | solution.py:304
  39.2 0.0 copy-done
  39.2 0.0 copy-start.1
  39.2 3.4 %shard_map.104 = (bf16[8,8,64,128]{3,2,1,0:T(8,128)(2,1)S(1)}, bf16[8,8,128,128]{3,2,1,0:T(8,128)(2,1)S(1)}, f32[520,128]{1,0:T(8,128)S(1)}, f32[528,128]{1,0:T(8,128)S(1)}) custom-call(f32[8,520,128]{2,1,0:T(8,128)S(1)} %collective-permute-done.other, ...), custom_call_target="tpu_custom_call", output_to_operand_aliasing={{0}: (1, {}), {1}: (2, {})} | custom-call | tf_op jit(solution)/shard_map/pallas_call | solution.py:269
  42.6 3.1 %collective-permute-start.2 = (f32[528,128]{1,0:T(8,128)S(1)}, f32[528,128]{1,0:T(8,128)S(1)}, u32[]{:S(2)}, u32[]{:S(2)}) collective-permute-start(f32[528,128]{1,0:T(8,128)S(1)} %get-tuple-element.23), channel_id=1, source_target_pairs={{0,24},{1,9},{16,8},{17,25},{32,56},{33,41},{48,40},{49,57},{2,26}... | collective-permute-start | bytes 811016 | tf_op jit(solution)/shard_map/ppermute | solution.py:300
  45.7 1.3 %collective-permute-start.1 = (f32[520,128]{1,0:T(8,128)S(1)}, f32[520,128]{1,0:T(8,128)S(1)}, u32[]{:S(2)}, u32[]{:S(2)}) collective-permute-start(f32[520,128]{1,0:T(8,128)S(1)} %get-tuple-element.22), channel_id=1, source_target_pairs={{0,96},{16,112},{32,64},{48,80},{1,97},{17,113},{33,65},{49,81},{2... | collective-permute-start | bytes 798728 | tf_op jit(solution)/shard_map/ppermute | solution.py:290
  47.1 5.9 %collective-permute-done.1.board_in = f32[520,128]{1,0:T(8,128)S(1)} collective-permute-done((f32[520,128]{1,0:T(8,128)S(1)}, f32[520,128]{1,0:T(8,128)S(1)}, u32[]{:S(2)}, u32[]{:S(2)}) %collective-permute-start.1) | collective-permute-done | bytes 266272 | tf_op jit(solution)/shard_map/ppermute | solution.py:290
  53.0 0.0 collective-permute-done.2.halo_in
  53.0 0.0 copy-done.1
  53.0 3.4 %shard_map.105 = (f32[520,128]{1,0:T(8,128)S(1)}, f32[528,128]{1,0:T(8,128)S(1)}) custom-call(f32[16,128]{1,0:T(8,128)S(1)} %get-tuple-element.17.phases, bf16[16,64,128]{2,1,0:T(8,128)(2,1)S(1)} %copy-done, bf16[8,8,64,128]{3,2,1,0:T(8,128)(2,1)S(1)} %get-tuple-element.20.lefts, bf16[8,8,128,128]{3,2,1,0:T(8,128)(2,1)S(1)} %get-tuple-element.21.rights, ...), custom_call_target="tpu_custom_call" | custom-call | tf_op jit(solution)/shard_map/pallas_call | solution.py:269
  56.4 0.7 collective-permute-start.4
  57.1 0.7 collective-permute-start.3
  57.8 0.0 collective-permute-done.3.board_in
  57.8 0.0 collective-permute-done.4.halo_in
  57.8 3.4 %shard_map.106 = f32[1,128]{1,0:T(1,128)S(1)} custom-call(f32[16,128]{1,0:T(8,128)S(1)} %get-tuple-element.17.phases, bf16[16,64,128]{2,1,0:T(8,128)(2,1)S(1)} %copy-done, bf16[8,8,64,128]{3,2,1,0:T(8,128)(2,1)S(1)} %get-tuple-element.20.lefts, bf16[8,8,128,128]{3,2,1,0:T(8,128)(2,1)S(1)} %get-tuple-element.21.rights, f32[16,64,128]{2,1,0:T(8,128)S(1)} %copy-done.1, ...), custom_call_target="tpu_custom_call" | custom-call | tf_op jit(solution)/shard_map/pallas_call | solution.py:269
  61.3 25.4 %all_to_all.11 = f32[128,1,128]{2,1,0:T(1,128)S(1)} all-to-all(f32[128,1,128]{2,1,0:T(1,128)S(1)} %broadcast_in_dim.9), channel_id=1, replica_groups=mesh['s'=2,'xp'=2,'yh'=2,'q'=2,'z'=4,'c'=2] {'s','xp','yh','q','z','c'}, dimensions={0} | all-to-all | bytes 131072 | tf_op jit(solution)/shard_map/all_to_all | solution.py:310
  86.7 0.8 shard_map.107
  (3 shorter events, 0.1 us)
Async XLA Ops:
  1.9 33.1 %copy-start.2 = (f32[4,64]{1,0:T(4,128)S(1)}, f32[4,64]{1,0:T(4,128)}, u32[]{:S(2)}) copy-start(f32[4,64]{1,0:T(4,128)} %param.12) | copy-start | bytes 3076
  35.0 4.2 %copy-start = (bf16[16,64,128]{2,1,0:T(8,128)(2,1)S(1)}, bf16[16,64,128]{2,1,0:T(8,128)(2,1)}, u32[]{:S(2)}) copy-start(bf16[16,64,128]{2,1,0:T(8,128)(2,1)} %edge.5) | copy-start | bytes 786436
  35.0 4.2 %collective-permute-start = (f32[8,520,128]{2,1,0:T(8,128)S(1)}, f32[8,520,128]{2,1,0:T(8,128)S(1)}, u32[]{:S(2)}, u32[]{:S(2)}) collective-permute-start(f32[8,520,128]{2,1,0:T(8,128)S(1)} %all_to_all.10.mine), channel_id=1, source_target_pairs={{0,1},{1,0},{2,3},{3,2},{4,5},{5,4},{6,7},{7,6},{8,9},{9,8},{10,11... | collective-permute-start | bytes 6389768 | tf_op jit(solution)/shard_map/ppermute | solution.py:304
  39.2 13.8 %copy-start.1 = (f32[16,64,128]{2,1,0:T(8,128)S(1)}, f32[16,64,128]{2,1,0:T(8,128)}, u32[]{:S(2)}) copy-start(f32[16,64,128]{2,1,0:T(8,128)} %close.3) | copy-start | bytes 1572868
  42.6 10.4 %collective-permute-start.2 = (f32[528,128]{1,0:T(8,128)S(1)}, f32[528,128]{1,0:T(8,128)S(1)}, u32[]{:S(2)}, u32[]{:S(2)}) collective-permute-start(f32[528,128]{1,0:T(8,128)S(1)} %get-tuple-element.23), channel_id=1, source_target_pairs={{0,24},{1,9},{16,8},{17,25},{32,56},{33,41},{48,40},{49,57},{2,26}... | collective-permute-start | bytes 811016 | tf_op jit(solution)/shard_map/ppermute | solution.py:300
  45.7 7.3 %collective-permute-start.1 = (f32[520,128]{1,0:T(8,128)S(1)}, f32[520,128]{1,0:T(8,128)S(1)}, u32[]{:S(2)}, u32[]{:S(2)}) collective-permute-start(f32[520,128]{1,0:T(8,128)S(1)} %get-tuple-element.22), channel_id=1, source_target_pairs={{0,96},{16,112},{32,64},{48,80},{1,97},{17,113},{33,65},{49,81},{2... | collective-permute-start | bytes 798728 | tf_op jit(solution)/shard_map/ppermute | solution.py:290
  56.4 1.4 %collective-permute-start.4 = (f32[528,128]{1,0:T(8,128)S(1)}, f32[528,128]{1,0:T(8,128)S(1)}, u32[]{:S(2)}, u32[]{:S(2)}) collective-permute-start(f32[528,128]{1,0:T(8,128)S(1)} %get-tuple-element.25), channel_id=1, source_target_pairs={{64,88},{65,73},{80,72},{81,89},{96,120},{97,105},{112,104},{113,1... | collective-permute-start | bytes 811016 | tf_op jit(solution)/shard_map/ppermute | solution.py:300
  57.1 0.7 collective-permute-start.3

commit v6 on v5

--- a/solution.py
+++ b/solution.py
@@ -191,18 +191,30 @@
 
 
 def first_kernel(other, lefts_in, rights_in, phases, edge, lefts, rights, board_out, halo_out, state, turned, peaks):
-    _, _, _, base = places()
+    s, q, _, base = places()
     sign = sign_row()
     one = jnp.ones((1, 2 * W), F32)
     part = 1 - lax.axis_index("c")
-    for k in range(NR):
-        state[k] = edge[base + k].astype(F32)
-        turned[k] = times_i(state[k], sign)
+    mine = jnp.logical_and(s == 0, q == 0)
     prepare = lambda j: unpack_column(other, j, part, lefts, rights, sign)
-    end = sweep(
-        state, turned, lefts, rights, phases, None, halo_out, peaks, (one, one, one), sign, prepare
-    )
-    write_messages(state, board_out, halo_out, peaks, 0.0 * one, end, None)
+
+    @pl.when(mine)
+    def run():
+        for k in range(NR):
+            state[k] = edge[base + k].astype(F32)
+            turned[k] = times_i(state[k], sign)
+        end = sweep(
+            state, turned, lefts, rights, phases, None, halo_out, peaks, (one, one, one), sign, prepare
+        )
+        write_messages(state, board_out, halo_out, peaks, 0.0 * one, end, None)
+
+    @pl.when(jnp.logical_not(mine))
+    def keep():
+        def place(j, unused):
+            prepare(j)
+            return unused
+
+        lax.fori_loop(0, NC, place, 0)
 
 
 def load_state(state, turned, edge, board_in, base, s, sign):
@@ -221,32 +233,45 @@
 
 
 def second_kernel(phases, edge, lefts, rights, close, board_in, halo_in, board_out, halo_out, state, turned, peaks):
-    s, _, _, base = places()
-    sign = sign_row()
-    start, ell = load_state(state, turned, edge, board_in, base, s, sign)
-    end = sweep(state, turned, lefts, rights, phases, halo_in, halo_out, peaks, start, sign)
-    write_messages(
-        state, board_out, halo_out, peaks, ell, end, close_sums(state, close, base, sign)
-    )
+    s, q, _, base = places()
+
+    @pl.when(s != q)
+    def run():
+        sign = sign_row()
+        start, ell = load_state(state, turned, edge, board_in, base, s, sign)
+        end = sweep(
+            state, turned, lefts, rights, phases, halo_in, halo_out, peaks, start, sign
+        )
+        sums = close_sums(state, close, base, sign)
+        write_messages(state, board_out, halo_out, peaks, ell, end, sums)
 
 
 def third_kernel(phases, edge, lefts, rights, close, board_in, halo_in, out, state, turned, peaks, halo_out):
     s, q, own, base = places()
-    sign = sign_row()
-    start, ell = load_state(state, turned, edge, board_in, base, s, sign)
-    p, rho_mix, _ = sweep(state, turned, lefts, rights, phases, halo_in, halo_out, peaks, start, sign)
-    ell = ell + jnp.sum(jnp.log(peaks[...]), axis=0, keepdims=True)
-    real, imag = close_sums(state, close, base, sign)
-    factor = 1.0 / math.sqrt(2 * NR * W * W)
-    real = (real + rho_mix * halo_in[pl.ds(NC * W + 8, 1), :]) / p * factor
-    imag = (imag + rho_mix * halo_in[pl.ds(NC * W + 9, 1), :]) / p * factor
-    index = 4 * (2 * lax.axis_index("z") + lax.axis_index("c")) + own
-    lane = lax.broadcasted_iota(jnp.int32, (1, 2 * W), 1)
-    index = jnp.where(jnp.logical_and(s == 1, q == 1), index, -128)
-    row = jnp.where(lane == index, real, 0.0)
-    row = row + jnp.where(lane == index + 32, imag, 0.0)
-    row = row + jnp.where(lane == index + 64, ell, 0.0)
-    out[...] = row
+    mine = jnp.logical_and(s == 1, q == 1)
+
+    @pl.when(mine)
+    def run():
+        sign = sign_row()
+        start, ell = load_state(state, turned, edge, board_in, base, s, sign)
+        p, rho_mix, _ = sweep(
+            state, turned, lefts, rights, phases, halo_in, halo_out, peaks, start, sign
+        )
+        ell = ell + jnp.sum(jnp.log(peaks[...]), axis=0, keepdims=True)
+        real, imag = close_sums(state, close, base, sign)
+        factor = 1.0 / math.sqrt(2 * NR * W * W)
+        real = (real + rho_mix * halo_in[pl.ds(NC * W + 8, 1), :]) / p * factor
+        imag = (imag + rho_mix * halo_in[pl.ds(NC * W + 9, 1), :]) / p * factor
+        index = 4 * (2 * lax.axis_index("z") + lax.axis_index("c")) + own
+        lane = lax.broadcasted_iota(jnp.int32, (1, 2 * W), 1)
+        row = jnp.where(lane == index, real, 0.0)
+        row = row + jnp.where(lane == index + 32, imag, 0.0)
+        row = row + jnp.where(lane == index + 64, ell, 0.0)
+        out[...] = row
+
+    @pl.when(jnp.logical_not(mine))
+    def nothing():
+        out[...] = jnp.zeros((1, 2 * W), F32)
 
 
 def finish_kernel(blocks, amps, logs, total, top):

time: 88 us -> 86.4 us (0.982)
  blocking collectives: 58.5 us -> 65.4 us
  Pallas kernels: 13.2 us -> 6.41 us
  starting transfers between devices: 5.78 us -> 3.96 us
    all_to_all x1, blocking collectives: 25.4 us -> 32.2 us  [gathered(): lax.all_to_all(spread, AXES, 0, 0, tiled=True)]
    pallas_call x6, Pallas kernels: 13.2 us -> 6.41 us  [call(): pl.pallas_call(kernel, out_shape=outs, in_specs=specs or [vmem()] * len(a...]
    ppermute x2, starting transfers between devices: 3.76 us -> 1.97 us  [along_rows(): return lax.ppermute(value, (*GRID, 'c'), pairs)]
where the time goes in v6:
time: 86.4 us; the launch traced here: 86 us
  blocking collectives  65.4 us (76%)
  waiting for transfers between devices  9.39 us (11%)
  Pallas kernels  6.41 us (7%)
  starting transfers between devices  3.96 us (5%)
    all_to_all x1, blocking collectives, body(): mine = lax.all_to_all(packed, ('xp', 'yh', 'q'), 0, 0, tiled=True)  33.1 us
    all_to_all x1, blocking collectives, gathered(): lax.all_to_all(spread, AXES, 0, 0, tiled=True)  32.2 us
    pallas_call x6, Pallas kernels, call(): pl.pallas_call(kernel, out_shape=outs, in_specs=specs or [vmem()] * len(a...  6.41 us
    ppermute x2, waiting for transfers between devices, along_columns(): return lax.ppermute(value, GRID, pairs)  6.21 us
    ppermute x1, waiting for transfers between devices, swapped(): return lax.ppermute(value, 'c', [(0, 1), (1, 0)])  3.18 us
    ppermute x2, starting transfers between devices, along_columns(): return lax.ppermute(value, GRID, pairs)  1.98 us
    ppermute x2, starting transfers between devices, along_rows(): return lax.ppermute(value, (*GRID, 'c'), pairs)  1.97 us
  transfers between devices with their start and end apart: 5, of which 2 were waited for; matrix products, arithmetic and copies ran while one was open for 0% of the time, Pallas kernels for 1%

profile of v6, /device:TPU:0, one launch (start us, length us, event | category | flops | bytes accessed | tf_op | source)
XLA Modules:
  0.0 86.0 jit_solution(17109207428155467181)
XLA Ops:
  0.6 1.2 %shard_map.102 = f32[8,520,128]{2,1,0:T(8,128)S(1)} custom-call(s32[1,16]{1,0:T(1,128)} %bitcast.10, s32[1,4]{1,0:T(1,128)} %bitcast.11, bf16[1,16,64,128]{3,2,1,0:T(8,128)(2,1)} %left_hbm.1, bf16[1,16,64,128]{3,2,1,0:T(8,128)(2,1)} %right_hbm.1), custom_call_target="tpu_custom_call" | custom-call | tf_op jit(solution)/shard_map/pallas_call | solution.py:294
  1.9 0.0 copy-start.2
  1.9 33.1 %all_to_all.10.mine = f32[8,520,128]{2,1,0:T(8,128)S(1)} all-to-all(f32[8,520,128]{2,1,0:T(8,128)S(1)} %shard_map.102), channel_id=1, replica_groups=mesh['s'=2,'xp'=2,'yh'=2,'q'=2,'z'=4,'c'=2] {'xp','yh','q'}, dimensions={0} | all-to-all | bytes 4259840 | tf_op jit(solution)/shard_map/all_to_all | solution.py:359
  35.0 0.0 copy-start
  35.0 0.0 collective-permute-start
  35.0 0.0 copy-done.2
  35.0 0.1 pad_maximum_fusion
  35.1 0.9 %shard_map.103 = (bf16[8,8,64,128]{3,2,1,0:T(8,128)(2,1)S(1)}, bf16[8,8,128,128]{3,2,1,0:T(8,128)(2,1)S(1)}, f32[16,128]{1,0:T(8,128)S(1)}) custom-call(f32[8,520,128]{2,1,0:T(8,128)S(1)} %all_to_all.10.mine, f32[4,128]{1,0:T(4,128)S(1)} %get-tuple-element.32.cosine, f32[4,128]{1,0:T(4,128)S(1)} %get-tuple-element.33.sine), custom_call_target="tpu_custom_call" | custom-call | tf_op jit(solution)/shard_map/pallas_call | solution.py:294
  36.0 3.2 %collective-permute-done.other = f32[8,520,128]{2,1,0:T(8,128)S(1)} collective-permute-done((f32[8,520,128]{2,1,0:T(8,128)S(1)}, f32[8,520,128]{2,1,0:T(8,128)S(1)}, u32[]{:S(2)}, u32[]{:S(2)}) %collective-permute-start) | collective-permute-done | bytes 2129952 | tf_op jit(solution)/shard_map/ppermute | solution.py:329
  39.2 0.0 copy-done
  39.2 0.0 copy-start.1
  39.2 3.5 %shard_map.104 = (bf16[8,8,64,128]{3,2,1,0:T(8,128)(2,1)S(1)}, bf16[8,8,128,128]{3,2,1,0:T(8,128)(2,1)S(1)}, f32[520,128]{1,0:T(8,128)S(1)}, f32[528,128]{1,0:T(8,128)S(1)}) custom-call(f32[8,520,128]{2,1,0:T(8,128)S(1)} %collective-permute-done.other, ...), custom_call_target="tpu_custom_call", output_to_operand_aliasing={{0}: (1, {}), {1}: (2, {})} | custom-call | tf_op jit(solution)/shard_map/pallas_call | solution.py:294
  42.7 1.3 %collective-permute-start.2 = (f32[528,128]{1,0:T(8,128)S(1)}, f32[528,128]{1,0:T(8,128)S(1)}, u32[]{:S(2)}, u32[]{:S(2)}) collective-permute-start(f32[528,128]{1,0:T(8,128)S(1)} %get-tuple-element.23), channel_id=1, source_target_pairs={{0,24},{1,9},{16,8},{17,25},{32,56},{33,41},{48,40},{49,57},{2,26}... | collective-permute-start | bytes 811016 | tf_op jit(solution)/shard_map/ppermute | solution.py:325
  44.0 1.3 %collective-permute-start.1 = (f32[520,128]{1,0:T(8,128)S(1)}, f32[520,128]{1,0:T(8,128)S(1)}, u32[]{:S(2)}, u32[]{:S(2)}) collective-permute-start(f32[520,128]{1,0:T(8,128)S(1)} %get-tuple-element.22), channel_id=1, source_target_pairs={{0,96},{16,112},{32,64},{48,80},{1,97},{17,113},{33,65},{49,81},{2... | collective-permute-start | bytes 798728 | tf_op jit(solution)/shard_map/ppermute | solution.py:315
  45.3 6.2 %collective-permute-done.1.board_in = f32[520,128]{1,0:T(8,128)S(1)} collective-permute-done((f32[520,128]{1,0:T(8,128)S(1)}, f32[520,128]{1,0:T(8,128)S(1)}, u32[]{:S(2)}, u32[]{:S(2)}) %collective-permute-start.1) | collective-permute-done | bytes 266272 | tf_op jit(solution)/shard_map/ppermute | solution.py:315
  51.5 0.0 collective-permute-done.2.halo_in
  51.5 0.0 copy-done.1
  51.5 0.7 collective-permute-start.4
  52.2 0.7 collective-permute-start.3
  52.9 0.0 collective-permute-done.3.board_in
  52.9 0.0 collective-permute-done.4.halo_in
  53.0 32.2 %all_to_all.11 = f32[128,1,128]{2,1,0:T(1,128)S(1)} all-to-all(f32[128,1,128]{2,1,0:T(1,128)S(1)} %broadcast_in_dim.9), channel_id=1, replica_groups=mesh['s'=2,'xp'=2,'yh'=2,'q'=2,'z'=4,'c'=2] {'s','xp','yh','q','z','c'}, dimensions={0} | all-to-all | bytes 131072 | tf_op jit(solution)/shard_map/all_to_all | solution.py:335
  85.2 0.8 shard_map.107
  (5 shorter events, 0.1 us)
Async XLA Ops:
  1.9 33.1 %copy-start.2 = (f32[4,64]{1,0:T(4,128)S(1)}, f32[4,64]{1,0:T(4,128)}, u32[]{:S(2)}) copy-start(f32[4,64]{1,0:T(4,128)} %param.12) | copy-start | bytes 3076
  35.0 4.2 %copy-start = (bf16[16,64,128]{2,1,0:T(8,128)(2,1)S(1)}, bf16[16,64,128]{2,1,0:T(8,128)(2,1)}, u32[]{:S(2)}) copy-start(bf16[16,64,128]{2,1,0:T(8,128)(2,1)} %edge.5) | copy-start | bytes 786436
  35.0 4.2 %collective-permute-start = (f32[8,520,128]{2,1,0:T(8,128)S(1)}, f32[8,520,128]{2,1,0:T(8,128)S(1)}, u32[]{:S(2)}, u32[]{:S(2)}) collective-permute-start(f32[8,520,128]{2,1,0:T(8,128)S(1)} %all_to_all.10.mine), channel_id=1, source_target_pairs={{0,1},{1,0},{2,3},{3,2},{4,5},{5,4},{6,7},{7,6},{8,9},{9,8},{10,11... | collective-permute-start | bytes 6389768 | tf_op jit(solution)/shard_map/ppermute | solution.py:329
  39.2 12.3 %copy-start.1 = (f32[16,64,128]{2,1,0:T(8,128)S(1)}, f32[16,64,128]{2,1,0:T(8,128)}, u32[]{:S(2)}) copy-start(f32[16,64,128]{2,1,0:T(8,128)} %close.3) | copy-start | bytes 1572868
  42.7 8.8 %collective-permute-start.2 = (f32[528,128]{1,0:T(8,128)S(1)}, f32[528,128]{1,0:T(8,128)S(1)}, u32[]{:S(2)}, u32[]{:S(2)}) collective-permute-start(f32[528,128]{1,0:T(8,128)S(1)} %get-tuple-element.23), channel_id=1, source_target_pairs={{0,24},{1,9},{16,8},{17,25},{32,56},{33,41},{48,40},{49,57},{2,26}... | collective-permute-start | bytes 811016 | tf_op jit(solution)/shard_map/ppermute | solution.py:325
  44.0 7.5 %collective-permute-start.1 = (f32[520,128]{1,0:T(8,128)S(1)}, f32[520,128]{1,0:T(8,128)S(1)}, u32[]{:S(2)}, u32[]{:S(2)}) collective-permute-start(f32[520,128]{1,0:T(8,128)S(1)} %get-tuple-element.22), channel_id=1, source_target_pairs={{0,96},{16,112},{32,64},{48,80},{1,97},{17,113},{33,65},{49,81},{2... | collective-permute-start | bytes 798728 | tf_op jit(solution)/shard_map/ppermute | solution.py:315
  51.5 1.4 %collective-permute-start.4 = (f32[528,128]{1,0:T(8,128)S(1)}, f32[528,128]{1,0:T(8,128)S(1)}, u32[]{:S(2)}, u32[]{:S(2)}) collective-permute-start(f32[528,128]{1,0:T(8,128)S(1)} %get-tuple-element.25), channel_id=1, source_target_pairs={{64,88},{65,73},{80,72},{81,89},{96,120},{97,105},{112,104},{113,1... | collective-permute-start | bytes 811016 | tf_op jit(solution)/shard_map/ppermute | solution.py:325
  52.2 0.7 collective-permute-start.3

commit v7 on v6

--- a/solution.py
+++ b/solution.py
@@ -70,7 +70,7 @@
 
 
 def unpack_kernel(mine, cosine, sine, lefts, rights, phases):
-    _, _, own, _ = places()
+    s, q, own, base = places()
     part, sign = lax.axis_index("c"), sign_row()
 
     def place(j, unused):
@@ -191,7 +191,7 @@
 
 
 def first_kernel(other, lefts_in, rights_in, phases, edge, lefts, rights, board_out, halo_out, state, turned, peaks):
-    s, q, _, base = places()
+    s, q, own, base = places()
     sign = sign_row()
     one = jnp.ones((1, 2 * W), F32)
     part = 1 - lax.axis_index("c")
@@ -233,7 +233,7 @@
 
 
 def second_kernel(phases, edge, lefts, rights, close, board_in, halo_in, board_out, halo_out, state, turned, peaks):
-    s, q, _, base = places()
+    s, q, own, base = places()
 
     @pl.when(s != q)
     def run():
@@ -254,7 +254,7 @@
     def run():
         sign = sign_row()
         start, ell = load_state(state, turned, edge, board_in, base, s, sign)
-        p, rho_mix, _ = sweep(
+        p, rho_mix, rho = sweep(
             state, turned, lefts, rights, phases, halo_in, halo_out, peaks, start, sign
         )
         ell = ell + jnp.sum(jnp.log(peaks[...]), axis=0, keepdims=True)
@@ -371,8 +371,7 @@
         (other, lefts, rights, phases, edge),
         aliases={1: 0, 2: 1},
     )
-    board = along_columns(board, 0)
-    halo = along_rows(halo, 0)
+    board, halo = along_columns(board, 0), along_rows(halo, 0)
     board, halo = call(
         second_kernel,
         (shape(BOARD, 2 * W), shape(HALO, 2 * W)),

time: 86.4 us -> 86.4 us (level)
  no operation moved by 1% of the time
where the time goes in v7:
time: 86.4 us; the launch traced here: 86 us
  blocking collectives  65.4 us (76%)
  waiting for transfers between devices  9.39 us (11%)
  Pallas kernels  6.41 us (7%)
  starting transfers between devices  3.96 us (5%)
    all_to_all x1, blocking collectives, body(): mine = lax.all_to_all(packed, ('xp', 'yh', 'q'), 0, 0, tiled=True)  33.1 us
    all_to_all x1, blocking collectives, gathered(): lax.all_to_all(spread, AXES, 0, 0, tiled=True)  32.2 us
    pallas_call x6, Pallas kernels, call(): pl.pallas_call(kernel, out_shape=outs, in_specs=specs or [vmem()] * len(a...  6.41 us
    ppermute x2, waiting for transfers between devices, along_columns(): return lax.ppermute(value, GRID, pairs)  6.21 us
    ppermute x1, waiting for transfers between devices, swapped(): return lax.ppermute(value, 'c', [(0, 1), (1, 0)])  3.18 us
    ppermute x2, starting transfers between devices, along_columns(): return lax.ppermute(value, GRID, pairs)  1.98 us
    ppermute x2, starting transfers between devices, along_rows(): return lax.ppermute(value, (*GRID, 'c'), pairs)  1.97 us
  transfers between devices with their start and end apart: 5, of which 2 were waited for; matrix products, arithmetic and copies ran while one was open for 0% of the time, Pallas kernels for 1%

profile of v7, /device:TPU:0, one launch (start us, length us, event | category | flops | bytes accessed | tf_op | source)
XLA Modules:
  0.0 86.0 jit_solution(17109207428155467181)
XLA Ops:
  0.6 1.2 %shard_map.102 = f32[8,520,128]{2,1,0:T(8,128)S(1)} custom-call(s32[1,16]{1,0:T(1,128)} %bitcast.10, s32[1,4]{1,0:T(1,128)} %bitcast.11, bf16[1,16,64,128]{3,2,1,0:T(8,128)(2,1)} %left_hbm.1, bf16[1,16,64,128]{3,2,1,0:T(8,128)(2,1)} %right_hbm.1), custom_call_target="tpu_custom_call" | custom-call | tf_op jit(solution)/shard_map/pallas_call | solution.py:294
  1.9 0.0 copy-start.2
  1.9 33.1 %all_to_all.10.mine = f32[8,520,128]{2,1,0:T(8,128)S(1)} all-to-all(f32[8,520,128]{2,1,0:T(8,128)S(1)} %shard_map.102), channel_id=1, replica_groups=mesh['s'=2,'xp'=2,'yh'=2,'q'=2,'z'=4,'c'=2] {'xp','yh','q'}, dimensions={0} | all-to-all | bytes 4259840 | tf_op jit(solution)/shard_map/all_to_all | solution.py:359
  35.0 0.0 copy-start
  35.0 0.0 collective-permute-start
  35.0 0.0 copy-done.2
  35.0 0.1 pad_maximum_fusion
  35.1 0.9 %shard_map.103 = (bf16[8,8,64,128]{3,2,1,0:T(8,128)(2,1)S(1)}, bf16[8,8,128,128]{3,2,1,0:T(8,128)(2,1)S(1)}, f32[16,128]{1,0:T(8,128)S(1)}) custom-call(f32[8,520,128]{2,1,0:T(8,128)S(1)} %all_to_all.10.mine, f32[4,128]{1,0:T(4,128)S(1)} %get-tuple-element.32.cosine, f32[4,128]{1,0:T(4,128)S(1)} %get-tuple-element.33.sine), custom_call_target="tpu_custom_call" | custom-call | tf_op jit(solution)/shard_map/pallas_call | solution.py:294
  36.0 3.2 %collective-permute-done.other = f32[8,520,128]{2,1,0:T(8,128)S(1)} collective-permute-done((f32[8,520,128]{2,1,0:T(8,128)S(1)}, f32[8,520,128]{2,1,0:T(8,128)S(1)}, u32[]{:S(2)}, u32[]{:S(2)}) %collective-permute-start) | collective-permute-done | bytes 2129952 | tf_op jit(solution)/shard_map/ppermute | solution.py:329
  39.2 0.0 copy-done
  39.2 0.0 copy-start.1
  39.2 3.5 %shard_map.104 = (bf16[8,8,64,128]{3,2,1,0:T(8,128)(2,1)S(1)}, bf16[8,8,128,128]{3,2,1,0:T(8,128)(2,1)S(1)}, f32[520,128]{1,0:T(8,128)S(1)}, f32[528,128]{1,0:T(8,128)S(1)}) custom-call(f32[8,520,128]{2,1,0:T(8,128)S(1)} %collective-permute-done.other, ...), custom_call_target="tpu_custom_call", output_to_operand_aliasing={{0}: (1, {}), {1}: (2, {})} | custom-call | tf_op jit(solution)/shard_map/pallas_call | solution.py:294
  42.7 1.3 %collective-permute-start.2 = (f32[528,128]{1,0:T(8,128)S(1)}, f32[528,128]{1,0:T(8,128)S(1)}, u32[]{:S(2)}, u32[]{:S(2)}) collective-permute-start(f32[528,128]{1,0:T(8,128)S(1)} %get-tuple-element.23), channel_id=1, source_target_pairs={{0,24},{1,9},{16,8},{17,25},{32,56},{33,41},{48,40},{49,57},{2,26}... | collective-permute-start | bytes 811016 | tf_op jit(solution)/shard_map/ppermute | solution.py:325
  44.0 1.3 %collective-permute-start.1 = (f32[520,128]{1,0:T(8,128)S(1)}, f32[520,128]{1,0:T(8,128)S(1)}, u32[]{:S(2)}, u32[]{:S(2)}) collective-permute-start(f32[520,128]{1,0:T(8,128)S(1)} %get-tuple-element.22), channel_id=1, source_target_pairs={{0,96},{16,112},{32,64},{48,80},{1,97},{17,113},{33,65},{49,81},{2... | collective-permute-start | bytes 798728 | tf_op jit(solution)/shard_map/ppermute | solution.py:315
  45.3 6.2 %collective-permute-done.1.board_in = f32[520,128]{1,0:T(8,128)S(1)} collective-permute-done((f32[520,128]{1,0:T(8,128)S(1)}, f32[520,128]{1,0:T(8,128)S(1)}, u32[]{:S(2)}, u32[]{:S(2)}) %collective-permute-start.1) | collective-permute-done | bytes 266272 | tf_op jit(solution)/shard_map/ppermute | solution.py:315
  51.5 0.0 collective-permute-done.2.halo_in
  51.5 0.0 copy-done.1
  51.5 0.7 collective-permute-start.4
  52.2 0.7 collective-permute-start.3
  52.9 0.0 collective-permute-done.3.board_in
  52.9 0.0 collective-permute-done.4.halo_in
  53.0 32.2 %all_to_all.11 = f32[128,1,128]{2,1,0:T(1,128)S(1)} all-to-all(f32[128,1,128]{2,1,0:T(1,128)S(1)} %broadcast_in_dim.9), channel_id=1, replica_groups=mesh['s'=2,'xp'=2,'yh'=2,'q'=2,'z'=4,'c'=2] {'s','xp','yh','q','z','c'}, dimensions={0} | all-to-all | bytes 131072 | tf_op jit(solution)/shard_map/all_to_all | solution.py:335
  85.2 0.8 shard_map.107
  (5 shorter events, 0.1 us)
Async XLA Ops:
  1.9 33.1 %copy-start.2 = (f32[4,64]{1,0:T(4,128)S(1)}, f32[4,64]{1,0:T(4,128)}, u32[]{:S(2)}) copy-start(f32[4,64]{1,0:T(4,128)} %param.12) | copy-start | bytes 3076
  35.0 4.2 %copy-start = (bf16[16,64,128]{2,1,0:T(8,128)(2,1)S(1)}, bf16[16,64,128]{2,1,0:T(8,128)(2,1)}, u32[]{:S(2)}) copy-start(bf16[16,64,128]{2,1,0:T(8,128)(2,1)} %edge.5) | copy-start | bytes 786436
  35.0 4.2 %collective-permute-start = (f32[8,520,128]{2,1,0:T(8,128)S(1)}, f32[8,520,128]{2,1,0:T(8,128)S(1)}, u32[]{:S(2)}, u32[]{:S(2)}) collective-permute-start(f32[8,520,128]{2,1,0:T(8,128)S(1)} %all_to_all.10.mine), channel_id=1, source_target_pairs={{0,1},{1,0},{2,3},{3,2},{4,5},{5,4},{6,7},{7,6},{8,9},{9,8},{10,11... | collective-permute-start | bytes 6389768 | tf_op jit(solution)/shard_map/ppermute | solution.py:329
  39.2 12.3 %copy-start.1 = (f32[16,64,128]{2,1,0:T(8,128)S(1)}, f32[16,64,128]{2,1,0:T(8,128)}, u32[]{:S(2)}) copy-start(f32[16,64,128]{2,1,0:T(8,128)} %close.3) | copy-start | bytes 1572868
  42.7 8.8 %collective-permute-start.2 = (f32[528,128]{1,0:T(8,128)S(1)}, f32[528,128]{1,0:T(8,128)S(1)}, u32[]{:S(2)}, u32[]{:S(2)}) collective-permute-start(f32[528,128]{1,0:T(8,128)S(1)} %get-tuple-element.23), channel_id=1, source_target_pairs={{0,24},{1,9},{16,8},{17,25},{32,56},{33,41},{48,40},{49,57},{2,26}... | collective-permute-start | bytes 811016 | tf_op jit(solution)/shard_map/ppermute | solution.py:325
  44.0 7.5 %collective-permute-start.1 = (f32[520,128]{1,0:T(8,128)S(1)}, f32[520,128]{1,0:T(8,128)S(1)}, u32[]{:S(2)}, u32[]{:S(2)}) collective-permute-start(f32[520,128]{1,0:T(8,128)S(1)} %get-tuple-element.22), channel_id=1, source_target_pairs={{0,96},{16,112},{32,64},{48,80},{1,97},{17,113},{33,65},{49,81},{2... | collective-permute-start | bytes 798728 | tf_op jit(solution)/shard_map/ppermute | solution.py:315
  51.5 1.4 %collective-permute-start.4 = (f32[528,128]{1,0:T(8,128)S(1)}, f32[528,128]{1,0:T(8,128)S(1)}, u32[]{:S(2)}, u32[]{:S(2)}) collective-permute-start(f32[528,128]{1,0:T(8,128)S(1)} %get-tuple-element.25), channel_id=1, source_target_pairs={{64,88},{65,73},{80,72},{81,89},{96,120},{97,105},{112,104},{113,1... | collective-permute-start | bytes 811016 | tf_op jit(solution)/shard_map/ppermute | solution.py:325
  52.2 0.7 collective-permute-start.3

commit v8 on v6

--- a/solution.py
+++ b/solution.py
@@ -15,7 +15,7 @@
 W = 64
 BLOCK = 4 * 2 * W + 8
 BOARD = NR * W + 8
-HALO = NC * W + 16
+HALO = NC * W + 24
 F32 = jnp.float32
 BF16 = jnp.bfloat16
 
@@ -106,14 +106,14 @@
         if halo_in is None:
             below = below_turn = None
         else:
-            below = halo_in[pl.ds(j * W, W), :] * rho_mix
+            below = halo_in[pl.ds(j * W, W), :] * (rho_mix * 0.5**NR)
             below_turn = times_i(below, sign)
         top = jnp.zeros((8, 2 * W), F32)
         for k in range(NR):
             after = boards[k + 1] if k + 1 < NR else below
-            mixed = boards[k] if after is None else boards[k] + 0.5 * after
+            mixed = boards[k] if after is None else boards[k] + after
             after = turns[k + 1] if k + 1 < NR else below_turn
-            turn = turns[k] if after is None else turns[k] + 0.5 * after
+            turn = turns[k] if after is None else turns[k] + after
             mh, ml = halves(mixed)
             th, tl = halves(turn)
             both = jnp.dot(
@@ -131,8 +131,10 @@
             out = plain * cos_row + flip * sin_row
             state[k] = out
             turned[k] = flip * cos_turn - plain * sin_turn
-            for g in range(8):
-                top = jnp.maximum(top, jnp.abs(out[8 * g : 8 * g + 8]))
+            row_top = jnp.abs(out[0:8])
+            for g in range(1, 8):
+                row_top = jnp.maximum(row_top, jnp.abs(out[8 * g : 8 * g + 8]))
+            top = jnp.maximum(top, row_top * 2.0**k)
         own_top = jnp.broadcast_to(jnp.max(top, keepdims=True), (1, 2 * W))
         halo_out[pl.ds(NC * W + j, 1), :] = own_top
         if halo_in is None:
@@ -160,11 +162,15 @@
         c = close[base + k]
         b = state[k]
         d = pltpu.roll(c, W, 1)
-        for g in range(8):
+        row_real = b[0:8] * c[0:8]
+        row_imag = b[0:8] * d[0:8]
+        for g in range(1, 8):
             part = slice(8 * g, 8 * g + 8)
-            real = real - b[part] * c[part] * sign
-            imag = imag + b[part] * d[part]
-    return jnp.sum(real, keepdims=True), jnp.sum(imag, keepdims=True)
+            row_real = row_real + b[part] * c[part]
+            row_imag = row_imag + b[part] * d[part]
+        real = real + row_real * 2.0**k
+        imag = imag + row_imag * 2.0**k
+    return -real * sign, imag
 
 
 def write_messages(state, board_out, halo_out, peaks, ell, end, sums):
@@ -176,10 +182,9 @@
     board_out[pl.ds(NR * W + 2, 1), :] = rho
     board_out[pl.ds(NR * W + 3, 1), :] = ell + jnp.sum(jnp.log(peaks[...]), axis=0, keepdims=True)
     board_out[pl.ds(NR * W + 4, 4), :] = jnp.zeros((4, 2 * W), F32)
-    halo_out[pl.ds(NC * W + 8, 8), :] = jnp.zeros((8, 2 * W), F32)
     if sums is not None:
-        halo_out[pl.ds(NC * W + 8, 1), :] = jnp.broadcast_to(sums[0], (1, 2 * W))
-        halo_out[pl.ds(NC * W + 9, 1), :] = jnp.broadcast_to(sums[1], (1, 2 * W))
+        halo_out[pl.ds(NC * W + 8, 8), :] = sums[0]
+        halo_out[pl.ds(NC * W + 16, 8), :] = sums[1]
 
 
 def places():
@@ -201,8 +206,9 @@
     @pl.when(mine)
     def run():
         for k in range(NR):
-            state[k] = edge[base + k].astype(F32)
-            turned[k] = times_i(state[k], sign)
+            x = edge[base + k].astype(F32) * 0.5**k
+            state[k] = x
+            turned[k] = times_i(x, sign)
         end = sweep(
             state, turned, lefts, rights, phases, None, halo_out, peaks, (one, one, one), sign, prepare
         )
@@ -221,7 +227,7 @@
     one = jnp.ones((1, 2 * W), F32)
     first = s == 0
     for k in range(NR):
-        x = jnp.where(first, edge[base + k].astype(F32), board_in[pl.ds(k * W, W), :])
+        x = jnp.where(first, edge[base + k].astype(F32) * 0.5**k, board_in[pl.ds(k * W, W), :])
         state[k] = x
         turned[k] = times_i(x, sign)
     row = lambda n: board_in[pl.ds(NR * W + n, 1), :]
@@ -260,8 +266,11 @@
         ell = ell + jnp.sum(jnp.log(peaks[...]), axis=0, keepdims=True)
         real, imag = close_sums(state, close, base, sign)
         factor = 1.0 / math.sqrt(2 * NR * W * W)
-        real = (real + rho_mix * halo_in[pl.ds(NC * W + 8, 1), :]) / p * factor
-        imag = (imag + rho_mix * halo_in[pl.ds(NC * W + 9, 1), :]) / p * factor
+        scale = factor / p
+        real = real + rho_mix * halo_in[pl.ds(NC * W + 8, 8), :]
+        imag = imag + rho_mix * halo_in[pl.ds(NC * W + 16, 8), :]
+        real = jnp.sum(real, keepdims=True) * scale
+        imag = jnp.sum(imag, keepdims=True) * scale
         index = 4 * (2 * lax.axis_index("z") + lax.axis_index("c")) + own
         lane = lax.broadcasted_iota(jnp.int32, (1, 2 * W), 1)
         row = jnp.where(lane == index, real, 0.0)

time: 86.4 us -> 86.1 us (level)
  no operation moved by 1% of the time
where the time goes in v8:
time: 86.1 us; the launch traced here: 85.7 us
  blocking collectives  65.2 us (76%)
  waiting for transfers between devices  9.38 us (11%)
  Pallas kernels  6.29 us (7%)
  starting transfers between devices  3.96 us (5%)
    all_to_all x1, blocking collectives, body(): mine = lax.all_to_all(packed, ('xp', 'yh', 'q'), 0, 0, tiled=True)  33.1 us
    all_to_all x1, blocking collectives, gathered(): lax.all_to_all(spread, AXES, 0, 0, tiled=True)  32.1 us
    pallas_call x6, Pallas kernels, call(): pl.pallas_call(kernel, out_shape=outs, in_specs=specs or [vmem()] * len(a...  6.29 us
    ppermute x2, waiting for transfers between devices, along_columns(): return lax.ppermute(value, GRID, pairs)  6.2 us
    ppermute x1, waiting for transfers between devices, swapped(): return lax.ppermute(value, 'c', [(0, 1), (1, 0)])  3.18 us
    ppermute x2, starting transfers between devices, along_columns(): return lax.ppermute(value, GRID, pairs)  1.98 us
    ppermute x2, starting transfers between devices, along_rows(): return lax.ppermute(value, (*GRID, 'c'), pairs)  1.97 us
  transfers between devices with their start and end apart: 5, of which 2 were waited for; matrix products, arithmetic and copies ran while one was open for 0% of the time, Pallas kernels for 1%

profile of v8, /device:TPU:0, one launch (start us, length us, event | category | flops | bytes accessed | tf_op | source)
XLA Modules:
  0.0 85.7 jit_solution(7910704241431671012)
XLA Ops:
  0.6 1.2 %shard_map.102 = f32[8,520,128]{2,1,0:T(8,128)S(1)} custom-call(s32[1,16]{1,0:T(1,128)} %bitcast.10, s32[1,4]{1,0:T(1,128)} %bitcast.11, bf16[1,16,64,128]{3,2,1,0:T(8,128)(2,1)} %left_hbm.1, bf16[1,16,64,128]{3,2,1,0:T(8,128)(2,1)} %right_hbm.1), custom_call_target="tpu_custom_call" | custom-call | tf_op jit(solution)/shard_map/pallas_call | solution.py:303
  1.9 0.0 copy-start.2
  1.9 33.1 %all_to_all.10.mine = f32[8,520,128]{2,1,0:T(8,128)S(1)} all-to-all(f32[8,520,128]{2,1,0:T(8,128)S(1)} %shard_map.102), channel_id=1, replica_groups=mesh['s'=2,'xp'=2,'yh'=2,'q'=2,'z'=4,'c'=2] {'xp','yh','q'}, dimensions={0} | all-to-all | bytes 4259840 | tf_op jit(solution)/shard_map/all_to_all | solution.py:368
  35.0 0.0 copy-start
  35.0 0.0 collective-permute-start
  35.0 0.0 copy-done.2
  35.0 0.1 pad_maximum_fusion
  35.1 0.9 %shard_map.103 = (bf16[8,8,64,128]{3,2,1,0:T(8,128)(2,1)S(1)}, bf16[8,8,128,128]{3,2,1,0:T(8,128)(2,1)S(1)}, f32[16,128]{1,0:T(8,128)S(1)}) custom-call(f32[8,520,128]{2,1,0:T(8,128)S(1)} %all_to_all.10.mine, f32[4,128]{1,0:T(4,128)S(1)} %get-tuple-element.32.cosine, f32[4,128]{1,0:T(4,128)S(1)} %get-tuple-element.33.sine), custom_call_target="tpu_custom_call" | custom-call | tf_op jit(solution)/shard_map/pallas_call | solution.py:303
  36.0 3.2 %collective-permute-done.other = f32[8,520,128]{2,1,0:T(8,128)S(1)} collective-permute-done((f32[8,520,128]{2,1,0:T(8,128)S(1)}, f32[8,520,128]{2,1,0:T(8,128)S(1)}, u32[]{:S(2)}, u32[]{:S(2)}) %collective-permute-start) | collective-permute-done | bytes 2129952 | tf_op jit(solution)/shard_map/ppermute | solution.py:338
  39.2 0.0 copy-done
  39.2 0.0 copy-start.1
  39.2 3.3 %shard_map.104 = (bf16[8,8,64,128]{3,2,1,0:T(8,128)(2,1)S(1)}, bf16[8,8,128,128]{3,2,1,0:T(8,128)(2,1)S(1)}, f32[520,128]{1,0:T(8,128)S(1)}, f32[536,128]{1,0:T(8,128)S(1)}) custom-call(f32[8,520,128]{2,1,0:T(8,128)S(1)} %collective-permute-done.other, ...), custom_call_target="tpu_custom_call", output_to_operand_aliasing={{0}: (1, {}), {1}: (2, {})} | custom-call | tf_op jit(solution)/shard_map/pallas_call | solution.py:303
  42.5 1.3 %collective-permute-start.2 = (f32[536,128]{1,0:T(8,128)S(1)}, f32[536,128]{1,0:T(8,128)S(1)}, u32[]{:S(2)}, u32[]{:S(2)}) collective-permute-start(f32[536,128]{1,0:T(8,128)S(1)} %get-tuple-element.23), channel_id=1, source_target_pairs={{0,24},{1,9},{16,8},{17,25},{32,56},{33,41},{48,40},{49,57},{2,26}... | collective-permute-start | bytes 823304 | tf_op jit(solution)/shard_map/ppermute | solution.py:334
  43.8 1.3 %collective-permute-start.1 = (f32[520,128]{1,0:T(8,128)S(1)}, f32[520,128]{1,0:T(8,128)S(1)}, u32[]{:S(2)}, u32[]{:S(2)}) collective-permute-start(f32[520,128]{1,0:T(8,128)S(1)} %get-tuple-element.22), channel_id=1, source_target_pairs={{0,96},{16,112},{32,64},{48,80},{1,97},{17,113},{33,65},{49,81},{2... | collective-permute-start | bytes 798728 | tf_op jit(solution)/shard_map/ppermute | solution.py:324
  45.2 6.2 %collective-permute-done.1.board_in = f32[520,128]{1,0:T(8,128)S(1)} collective-permute-done((f32[520,128]{1,0:T(8,128)S(1)}, f32[520,128]{1,0:T(8,128)S(1)}, u32[]{:S(2)}, u32[]{:S(2)}) %collective-permute-start.1) | collective-permute-done | bytes 266272 | tf_op jit(solution)/shard_map/ppermute | solution.py:324
  51.4 0.0 collective-permute-done.2.halo_in
  51.4 0.0 copy-done.1
  51.4 0.7 collective-permute-start.4
  52.0 0.7 collective-permute-start.3
  52.7 0.0 collective-permute-done.3.board_in
  52.7 0.0 collective-permute-done.4.halo_in
  52.8 32.1 %all_to_all.11 = f32[128,1,128]{2,1,0:T(1,128)S(1)} all-to-all(f32[128,1,128]{2,1,0:T(1,128)S(1)} %broadcast_in_dim.9), channel_id=1, replica_groups=mesh['s'=2,'xp'=2,'yh'=2,'q'=2,'z'=4,'c'=2] {'s','xp','yh','q','z','c'}, dimensions={0} | all-to-all | bytes 131072 | tf_op jit(solution)/shard_map/all_to_all | solution.py:344
  84.9 0.8 shard_map.107
  (5 shorter events, 0.1 us)
Async XLA Ops:
  1.9 33.1 %copy-start.2 = (f32[4,64]{1,0:T(4,128)S(1)}, f32[4,64]{1,0:T(4,128)}, u32[]{:S(2)}) copy-start(f32[4,64]{1,0:T(4,128)} %param.12) | copy-start | bytes 3076
  35.0 4.2 %copy-start = (bf16[16,64,128]{2,1,0:T(8,128)(2,1)S(1)}, bf16[16,64,128]{2,1,0:T(8,128)(2,1)}, u32[]{:S(2)}) copy-start(bf16[16,64,128]{2,1,0:T(8,128)(2,1)} %edge.5) | copy-start | bytes 786436
  35.0 4.2 %collective-permute-start = (f32[8,520,128]{2,1,0:T(8,128)S(1)}, f32[8,520,128]{2,1,0:T(8,128)S(1)}, u32[]{:S(2)}, u32[]{:S(2)}) collective-permute-start(f32[8,520,128]{2,1,0:T(8,128)S(1)} %all_to_all.10.mine), channel_id=1, source_target_pairs={{0,1},{1,0},{2,3},{3,2},{4,5},{5,4},{6,7},{7,6},{8,9},{9,8},{10,11... | collective-permute-start | bytes 6389768 | tf_op jit(solution)/shard_map/ppermute | solution.py:338
  39.2 12.2 %copy-start.1 = (f32[16,64,128]{2,1,0:T(8,128)S(1)}, f32[16,64,128]{2,1,0:T(8,128)}, u32[]{:S(2)}) copy-start(f32[16,64,128]{2,1,0:T(8,128)} %close.3) | copy-start | bytes 1572868
  42.5 8.8 %collective-permute-start.2 = (f32[536,128]{1,0:T(8,128)S(1)}, f32[536,128]{1,0:T(8,128)S(1)}, u32[]{:S(2)}, u32[]{:S(2)}) collective-permute-start(f32[536,128]{1,0:T(8,128)S(1)} %get-tuple-element.23), channel_id=1, source_target_pairs={{0,24},{1,9},{16,8},{17,25},{32,56},{33,41},{48,40},{49,57},{2,26}... | collective-permute-start | bytes 823304 | tf_op jit(solution)/shard_map/ppermute | solution.py:334
  43.8 7.5 %collective-permute-start.1 = (f32[520,128]{1,0:T(8,128)S(1)}, f32[520,128]{1,0:T(8,128)S(1)}, u32[]{:S(2)}, u32[]{:S(2)}) collective-permute-start(f32[520,128]{1,0:T(8,128)S(1)} %get-tuple-element.22), channel_id=1, source_target_pairs={{0,96},{16,112},{32,64},{48,80},{1,97},{17,113},{33,65},{49,81},{2... | collective-permute-start | bytes 798728 | tf_op jit(solution)/shard_map/ppermute | solution.py:324
  51.4 1.4 %collective-permute-start.4 = (f32[536,128]{1,0:T(8,128)S(1)}, f32[536,128]{1,0:T(8,128)S(1)}, u32[]{:S(2)}, u32[]{:S(2)}) collective-permute-start(f32[536,128]{1,0:T(8,128)S(1)} %get-tuple-element.25), channel_id=1, source_target_pairs={{64,88},{65,73},{80,72},{81,89},{96,120},{97,105},{112,104},{113,1... | collective-permute-start | bytes 823304 | tf_op jit(solution)/shard_map/ppermute | solution.py:334
  52.0 0.7 collective-permute-start.3

commit v9 on v8

--- a/solution.py
+++ b/solution.py
@@ -16,6 +16,7 @@
 BLOCK = 4 * 2 * W + 8
 BOARD = NR * W + 8
 HALO = NC * W + 24
+FIRST = (NC - 1) * W + 8
 F32 = jnp.float32
 BF16 = jnp.bfloat16
 
@@ -92,7 +93,7 @@
     return high, (x - high.astype(F32)).astype(BF16)
 
 
-def sweep(state, turned, lefts, rights, phases, halo_in, halo_out, peaks, start, sign, prepare=None):
+def sweep(state, turned, lefts, rights, phases, halo_in, halo_out, peaks, start, sign, prepare=None, entry=None, skip=0):
     def column(j, carry):
         p, rho_mix, rho = carry
         scale = 1.0 / p
@@ -102,11 +103,16 @@
         sin_turn = sin_row * sign
         boards = [state[k] for k in range(NR)]
         turns = [turned[k] for k in range(NR)]
-        halo_out[pl.ds(j * W, W), :] = boards[0]
+        if j >= skip:
+            halo_out[pl.ds((j - skip) * W, W), :] = boards[0]
         if halo_in is None:
             below = below_turn = None
         else:
-            below = halo_in[pl.ds(j * W, W), :] * (rho_mix * 0.5**NR)
+            if entry is None:
+                below = halo_in[pl.ds(j * W, W), :]
+            else:
+                below = entry if j == 0 else halo_in[pl.ds((j - 1) * W, W), :]
+            below = below * (rho_mix * 0.5**NR)
             below_turn = times_i(below, sign)
         top = jnp.zeros((8, 2 * W), F32)
         for k in range(NR):
@@ -136,11 +142,12 @@
                 row_top = jnp.maximum(row_top, jnp.abs(out[8 * g : 8 * g + 8]))
             top = jnp.maximum(top, row_top * 2.0**k)
         own_top = jnp.broadcast_to(jnp.max(top, keepdims=True), (1, 2 * W))
-        halo_out[pl.ds(NC * W + j, 1), :] = own_top
+        halo_out[pl.ds((NC - skip) * W + j, 1), :] = own_top
         if halo_in is None:
             other_top = jnp.zeros((1, 2 * W), F32)
         else:
-            other_top = halo_in[pl.ds(NC * W + j, 1), :]
+            rows_in = NC if entry is None else NC - 1
+            other_top = halo_in[pl.ds(rows_in * W + j, 1), :]
         p_new = jnp.maximum(jnp.maximum(own_top, other_top * rho), 1.0)
         peaks[pl.ds(j, 1), :] = p_new
         return (p_new, rho, rho * jnp.maximum(other_top, 1.0) / p_new)
@@ -210,7 +217,7 @@
             state[k] = x
             turned[k] = times_i(x, sign)
         end = sweep(
-            state, turned, lefts, rights, phases, None, halo_out, peaks, (one, one, one), sign, prepare
+            state, turned, lefts, rights, phases, None, halo_out, peaks, (one, one, one), sign, prepare, None, 1
         )
         write_messages(state, board_out, halo_out, peaks, 0.0 * one, end, None)
 
@@ -245,8 +252,9 @@
     def run():
         sign = sign_row()
         start, ell = load_state(state, turned, edge, board_in, base, s, sign)
+        entry = jnp.where(s == 0, edge[NR].astype(F32), 0.0)
         end = sweep(
-            state, turned, lefts, rights, phases, halo_in, halo_out, peaks, start, sign
+            state, turned, lefts, rights, phases, halo_in, halo_out, peaks, start, sign, None, entry
         )
         sums = close_sums(state, close, base, sign)
         write_messages(state, board_out, halo_out, peaks, ell, end, sums)
@@ -375,7 +383,7 @@
     )
     lefts, rights, board, halo = call(
         first_kernel,
-        (*gates, shape(BOARD, 2 * W), shape(HALO, 2 * W)),
+        (*gates, shape(BOARD, 2 * W), shape(FIRST, 2 * W)),
         [state, state, peaks],
         (other, lefts, rights, phases, edge),
         aliases={1: 0, 2: 1},

time: 86.1 us -> 84.8 us (0.985)
  waiting for transfers between devices: 9.38 us -> 8.05 us
    ppermute x2, waiting for transfers between devices: 6.2 us -> 1.32 us  [along_columns(): return lax.ppermute(value, GRID, pairs)]
    ppermute x2, waiting for transfers between devices: 0.01 us -> 3.55 us  [along_rows(): return lax.ppermute(value, (*GRID, 'c'), pairs)]
  transfers between devices with their start and end apart: 5 -> 5, of which waited for: 2 -> 3; matrix products, arithmetic and copies ran while one was open for 0% -> 0% of each run, Pallas kernels for 1% -> 1%
where the time goes in v9:
time: 84.8 us; the launch traced here: 84.4 us
  blocking collectives  65.2 us (77%)
  waiting for transfers between devices  8.05 us (9%)
  Pallas kernels  6.27 us (7%)
  starting transfers between devices  3.97 us (5%)
    all_to_all x1, blocking collectives, body(): mine = lax.all_to_all(packed, ('xp', 'yh', 'q'), 0, 0, tiled=True)  33.1 us
    all_to_all x1, blocking collectives, gathered(): lax.all_to_all(spread, AXES, 0, 0, tiled=True)  32.1 us
    pallas_call x6, Pallas kernels, call(): pl.pallas_call(kernel, out_shape=outs, in_specs=specs or [vmem()] * len(a...  6.27 us
    ppermute x2, waiting for transfers between devices, along_rows(): return lax.ppermute(value, (*GRID, 'c'), pairs)  3.55 us
    ppermute x1, waiting for transfers between devices, swapped(): return lax.ppermute(value, 'c', [(0, 1), (1, 0)])  3.18 us
    ppermute x2, starting transfers between devices, along_columns(): return lax.ppermute(value, GRID, pairs)  2 us
    ppermute x2, starting transfers between devices, along_rows(): return lax.ppermute(value, (*GRID, 'c'), pairs)  1.97 us
  transfers between devices with their start and end apart: 5, of which 3 were waited for; matrix products, arithmetic and copies ran while one was open for 0% of the time, Pallas kernels for 1%

profile of v9, /device:TPU:0, one launch (start us, length us, event | category | flops | bytes accessed | tf_op | source)
XLA Modules:
  0.0 84.4 jit_solution(14796348762397691088)
XLA Ops:
  0.6 1.2 %shard_map.102 = f32[8,520,128]{2,1,0:T(8,128)S(1)} custom-call(s32[1,16]{1,0:T(1,128)} %bitcast.10, s32[1,4]{1,0:T(1,128)} %bitcast.11, bf16[1,16,64,128]{3,2,1,0:T(8,128)(2,1)} %left_hbm.1, bf16[1,16,64,128]{3,2,1,0:T(8,128)(2,1)} %right_hbm.1), custom_call_target="tpu_custom_call" | custom-call | tf_op jit(solution)/shard_map/pallas_call | solution.py:311
  1.9 0.0 copy-start.2
  1.9 33.1 %all_to_all.10.mine = f32[8,520,128]{2,1,0:T(8,128)S(1)} all-to-all(f32[8,520,128]{2,1,0:T(8,128)S(1)} %shard_map.102), channel_id=1, replica_groups=mesh['s'=2,'xp'=2,'yh'=2,'q'=2,'z'=4,'c'=2] {'xp','yh','q'}, dimensions={0} | all-to-all | bytes 4259840 | tf_op jit(solution)/shard_map/all_to_all | solution.py:376
  35.0 0.0 copy-start
  35.0 0.0 collective-permute-start
  35.0 0.0 copy-done.2
  35.0 0.1 pad_maximum_fusion
  35.1 0.9 %shard_map.103 = (bf16[8,8,64,128]{3,2,1,0:T(8,128)(2,1)S(1)}, bf16[8,8,128,128]{3,2,1,0:T(8,128)(2,1)S(1)}, f32[16,128]{1,0:T(8,128)S(1)}) custom-call(f32[8,520,128]{2,1,0:T(8,128)S(1)} %all_to_all.10.mine, f32[4,128]{1,0:T(4,128)S(1)} %get-tuple-element.32.cosine, f32[4,128]{1,0:T(4,128)S(1)} %get-tuple-element.33.sine), custom_call_target="tpu_custom_call" | custom-call | tf_op jit(solution)/shard_map/pallas_call | solution.py:311
  36.0 3.2 %collective-permute-done.other = f32[8,520,128]{2,1,0:T(8,128)S(1)} collective-permute-done((f32[8,520,128]{2,1,0:T(8,128)S(1)}, f32[8,520,128]{2,1,0:T(8,128)S(1)}, u32[]{:S(2)}, u32[]{:S(2)}) %collective-permute-start) | collective-permute-done | bytes 2129952 | tf_op jit(solution)/shard_map/ppermute | solution.py:346
  39.2 0.0 copy-done
  39.2 0.0 copy-start.1
  39.2 3.3 %shard_map.104 = (bf16[8,8,64,128]{3,2,1,0:T(8,128)(2,1)S(1)}, bf16[8,8,128,128]{3,2,1,0:T(8,128)(2,1)S(1)}, f32[520,128]{1,0:T(8,128)S(1)}, f32[456,128]{1,0:T(8,128)S(1)}) custom-call(f32[8,520,128]{2,1,0:T(8,128)S(1)} %collective-permute-done.other, ...), custom_call_target="tpu_custom_call", output_to_operand_aliasing={{0}: (1, {}), {1}: (2, {})} | custom-call | tf_op jit(solution)/shard_map/pallas_call | solution.py:311
  42.5 1.3 %collective-permute-start.1 = (f32[520,128]{1,0:T(8,128)S(1)}, f32[520,128]{1,0:T(8,128)S(1)}, u32[]{:S(2)}, u32[]{:S(2)}) collective-permute-start(f32[520,128]{1,0:T(8,128)S(1)} %get-tuple-element.22), channel_id=1, source_target_pairs={{0,96},{16,112},{32,64},{48,80},{1,97},{17,113},{33,65},{49,81},{2... | collective-permute-start | bytes 798728 | tf_op jit(solution)/shard_map/ppermute | solution.py:332
  43.8 1.3 %collective-permute-start.2 = (f32[456,128]{1,0:T(8,128)S(1)}, f32[456,128]{1,0:T(8,128)S(1)}, u32[]{:S(2)}, u32[]{:S(2)}) collective-permute-start(f32[456,128]{1,0:T(8,128)S(1)} %get-tuple-element.23), channel_id=1, source_target_pairs={{0,24},{1,9},{16,8},{17,25},{32,56},{33,41},{48,40},{49,57},{2,26}... | collective-permute-start | bytes 700424 | tf_op jit(solution)/shard_map/ppermute | solution.py:342
  45.2 3.6 %collective-permute-done.2.halo_in = f32[456,128]{1,0:T(8,128)S(1)} collective-permute-done((f32[456,128]{1,0:T(8,128)S(1)}, f32[456,128]{1,0:T(8,128)S(1)}, u32[]{:S(2)}, u32[]{:S(2)}) %collective-permute-start.2) | collective-permute-done | bytes 233504 | tf_op jit(solution)/shard_map/ppermute | solution.py:342
  48.7 1.3 %collective-permute-done.1.board_in = f32[520,128]{1,0:T(8,128)S(1)} collective-permute-done((f32[520,128]{1,0:T(8,128)S(1)}, f32[520,128]{1,0:T(8,128)S(1)}, u32[]{:S(2)}, u32[]{:S(2)}) %collective-permute-start.1) | collective-permute-done | bytes 266272 | tf_op jit(solution)/shard_map/ppermute | solution.py:332
  50.0 0.0 copy-done.1
  50.0 0.7 collective-permute-start.4
  50.7 0.7 collective-permute-start.3
  51.4 0.0 collective-permute-done.3.board_in
  51.4 0.0 collective-permute-done.4.halo_in
  51.5 32.1 %all_to_all.11 = f32[128,1,128]{2,1,0:T(1,128)S(1)} all-to-all(f32[128,1,128]{2,1,0:T(1,128)S(1)} %broadcast_in_dim.9), channel_id=1, replica_groups=mesh['s'=2,'xp'=2,'yh'=2,'q'=2,'z'=4,'c'=2] {'s','xp','yh','q','z','c'}, dimensions={0} | all-to-all | bytes 131072 | tf_op jit(solution)/shard_map/all_to_all | solution.py:352
  83.6 0.8 shard_map.107
  (5 shorter events, 0.1 us)
Async XLA Ops:
  1.9 33.1 %copy-start.2 = (f32[4,64]{1,0:T(4,128)S(1)}, f32[4,64]{1,0:T(4,128)}, u32[]{:S(2)}) copy-start(f32[4,64]{1,0:T(4,128)} %param.12) | copy-start | bytes 3076
  35.0 4.2 %copy-start = (bf16[16,64,128]{2,1,0:T(8,128)(2,1)S(1)}, bf16[16,64,128]{2,1,0:T(8,128)(2,1)}, u32[]{:S(2)}) copy-start(bf16[16,64,128]{2,1,0:T(8,128)(2,1)} %edge.5) | copy-start | bytes 786436
  35.0 4.2 %collective-permute-start = (f32[8,520,128]{2,1,0:T(8,128)S(1)}, f32[8,520,128]{2,1,0:T(8,128)S(1)}, u32[]{:S(2)}, u32[]{:S(2)}) collective-permute-start(f32[8,520,128]{2,1,0:T(8,128)S(1)} %all_to_all.10.mine), channel_id=1, source_target_pairs={{0,1},{1,0},{2,3},{3,2},{4,5},{5,4},{6,7},{7,6},{8,9},{9,8},{10,11... | collective-permute-start | bytes 6389768 | tf_op jit(solution)/shard_map/ppermute | solution.py:346
  39.2 10.8 %copy-start.1 = (f32[16,64,128]{2,1,0:T(8,128)S(1)}, f32[16,64,128]{2,1,0:T(8,128)}, u32[]{:S(2)}) copy-start(f32[16,64,128]{2,1,0:T(8,128)} %close.3) | copy-start | bytes 1572868
  42.5 7.5 %collective-permute-start.1 = (f32[520,128]{1,0:T(8,128)S(1)}, f32[520,128]{1,0:T(8,128)S(1)}, u32[]{:S(2)}, u32[]{:S(2)}) collective-permute-start(f32[520,128]{1,0:T(8,128)S(1)} %get-tuple-element.22), channel_id=1, source_target_pairs={{0,96},{16,112},{32,64},{48,80},{1,97},{17,113},{33,65},{49,81},{2... | collective-permute-start | bytes 798728 | tf_op jit(solution)/shard_map/ppermute | solution.py:332
  43.8 4.9 %collective-permute-start.2 = (f32[456,128]{1,0:T(8,128)S(1)}, f32[456,128]{1,0:T(8,128)S(1)}, u32[]{:S(2)}, u32[]{:S(2)}) collective-permute-start(f32[456,128]{1,0:T(8,128)S(1)} %get-tuple-element.23), channel_id=1, source_target_pairs={{0,24},{1,9},{16,8},{17,25},{32,56},{33,41},{48,40},{49,57},{2,26}... | collective-permute-start | bytes 700424 | tf_op jit(solution)/shard_map/ppermute | solution.py:342
  50.0 1.4 %collective-permute-start.4 = (f32[536,128]{1,0:T(8,128)S(1)}, f32[536,128]{1,0:T(8,128)S(1)}, u32[]{:S(2)}, u32[]{:S(2)}) collective-permute-start(f32[536,128]{1,0:T(8,128)S(1)} %get-tuple-element.25), channel_id=1, source_target_pairs={{64,88},{65,73},{80,72},{81,89},{96,120},{97,105},{112,104},{113,1... | collective-permute-start | bytes 823304 | tf_op jit(solution)/shard_map/ppermute | solution.py:342
  50.7 0.7 collective-permute-start.3

commit v10 on v9

--- a/solution.py
+++ b/solution.py
@@ -129,10 +129,12 @@
             )
             middle = both[:, : 2 * W] + both[:, 2 * W :]
             dh, dl = halves(middle)
-            two = jnp.dot(
-                jnp.concatenate([dh, dl], 0), rights[j, k], preferred_element_type=F32
+            right = rights[j, k]
+            plain = jnp.dot(
+                jnp.concatenate([dh, dl], 1),
+                jnp.concatenate([right, right], 0),
+                preferred_element_type=F32,
             )
-            plain = two[:W] + two[W:]
             flip = pltpu.roll(plain, W, 1)
             out = plain * cos_row + flip * sin_row
             state[k] = out

time: 84.8 us -> 84.7 us (level)
  no operation moved by 1% of the time
where the time goes in v10:
time: 84.7 us; the launch traced here: 84.3 us
  blocking collectives  65.1 us (77%)
  waiting for transfers between devices  8.03 us (9%)
  Pallas kernels  6.25 us (7%)
  starting transfers between devices  3.99 us (5%)
    all_to_all x1, blocking collectives, body(): mine = lax.all_to_all(packed, ('xp', 'yh', 'q'), 0, 0, tiled=True)  33.1 us
    all_to_all x1, blocking collectives, gathered(): lax.all_to_all(spread, AXES, 0, 0, tiled=True)  32 us
    pallas_call x6, Pallas kernels, call(): pl.pallas_call(kernel, out_shape=outs, in_specs=specs or [vmem()] * len(a...  6.25 us
    ppermute x2, waiting for transfers between devices, along_rows(): return lax.ppermute(value, (*GRID, 'c'), pairs)  3.55 us
    ppermute x1, waiting for transfers between devices, swapped(): return lax.ppermute(value, 'c', [(0, 1), (1, 0)])  3.18 us
    ppermute x2, starting transfers between devices, along_columns(): return lax.ppermute(value, GRID, pairs)  2.02 us
    ppermute x2, starting transfers between devices, along_rows(): return lax.ppermute(value, (*GRID, 'c'), pairs)  1.97 us
  transfers between devices with their start and end apart: 5, of which 3 were waited for; matrix products, arithmetic and copies ran while one was open for 0% of the time, Pallas kernels for 1%

profile of v10, /device:TPU:0, one launch (start us, length us, event | category | flops | bytes accessed | tf_op | source)
XLA Modules:
  0.0 84.3 jit_solution(10920739121920421015)
XLA Ops:
  0.6 1.2 %shard_map.102 = f32[8,520,128]{2,1,0:T(8,128)S(1)} custom-call(s32[1,16]{1,0:T(1,128)} %bitcast.10, s32[1,4]{1,0:T(1,128)} %bitcast.11, bf16[1,16,64,128]{3,2,1,0:T(8,128)(2,1)} %left_hbm.1, bf16[1,16,64,128]{3,2,1,0:T(8,128)(2,1)} %right_hbm.1), custom_call_target="tpu_custom_call" | custom-call | tf_op jit(solution)/shard_map/pallas_call | solution.py:313
  1.9 0.0 copy-start.2
  1.9 33.1 %all_to_all.10.mine = f32[8,520,128]{2,1,0:T(8,128)S(1)} all-to-all(f32[8,520,128]{2,1,0:T(8,128)S(1)} %shard_map.102), channel_id=1, replica_groups=mesh['s'=2,'xp'=2,'yh'=2,'q'=2,'z'=4,'c'=2] {'xp','yh','q'}, dimensions={0} | all-to-all | bytes 4259840 | tf_op jit(solution)/shard_map/all_to_all | solution.py:378
  35.0 0.0 copy-start
  35.0 0.0 collective-permute-start
  35.0 0.0 copy-done.2
  35.0 0.1 pad_maximum_fusion
  35.1 0.9 %shard_map.103 = (bf16[8,8,64,128]{3,2,1,0:T(8,128)(2,1)S(1)}, bf16[8,8,128,128]{3,2,1,0:T(8,128)(2,1)S(1)}, f32[16,128]{1,0:T(8,128)S(1)}) custom-call(f32[8,520,128]{2,1,0:T(8,128)S(1)} %all_to_all.10.mine, f32[4,128]{1,0:T(4,128)S(1)} %get-tuple-element.32.cosine, f32[4,128]{1,0:T(4,128)S(1)} %get-tuple-element.33.sine), custom_call_target="tpu_custom_call" | custom-call | tf_op jit(solution)/shard_map/pallas_call | solution.py:313
  36.0 3.2 %collective-permute-done.other = f32[8,520,128]{2,1,0:T(8,128)S(1)} collective-permute-done((f32[8,520,128]{2,1,0:T(8,128)S(1)}, f32[8,520,128]{2,1,0:T(8,128)S(1)}, u32[]{:S(2)}, u32[]{:S(2)}) %collective-permute-start) | collective-permute-done | bytes 2129952 | tf_op jit(solution)/shard_map/ppermute | solution.py:348
  39.2 0.0 copy-done
  39.2 0.0 copy-start.1
  39.2 3.3 %shard_map.104 = (bf16[8,8,64,128]{3,2,1,0:T(8,128)(2,1)S(1)}, bf16[8,8,128,128]{3,2,1,0:T(8,128)(2,1)S(1)}, f32[520,128]{1,0:T(8,128)S(1)}, f32[456,128]{1,0:T(8,128)S(1)}) custom-call(f32[8,520,128]{2,1,0:T(8,128)S(1)} %collective-permute-done.other, ...), custom_call_target="tpu_custom_call", output_to_operand_aliasing={{0}: (1, {}), {1}: (2, {})} | custom-call | tf_op jit(solution)/shard_map/pallas_call | solution.py:313
  42.5 1.3 %collective-permute-start.1 = (f32[520,128]{1,0:T(8,128)S(1)}, f32[520,128]{1,0:T(8,128)S(1)}, u32[]{:S(2)}, u32[]{:S(2)}) collective-permute-start(f32[520,128]{1,0:T(8,128)S(1)} %get-tuple-element.22), channel_id=1, source_target_pairs={{0,96},{16,112},{32,64},{48,80},{1,97},{17,113},{33,65},{49,81},{2... | collective-permute-start | bytes 798728 | tf_op jit(solution)/shard_map/ppermute | solution.py:334
  43.8 1.3 %collective-permute-start.2 = (f32[456,128]{1,0:T(8,128)S(1)}, f32[456,128]{1,0:T(8,128)S(1)}, u32[]{:S(2)}, u32[]{:S(2)}) collective-permute-start(f32[456,128]{1,0:T(8,128)S(1)} %get-tuple-element.23), channel_id=1, source_target_pairs={{0,24},{1,9},{16,8},{17,25},{32,56},{33,41},{48,40},{49,57},{2,26}... | collective-permute-start | bytes 700424 | tf_op jit(solution)/shard_map/ppermute | solution.py:344
  45.2 3.6 %collective-permute-done.2.halo_in = f32[456,128]{1,0:T(8,128)S(1)} collective-permute-done((f32[456,128]{1,0:T(8,128)S(1)}, f32[456,128]{1,0:T(8,128)S(1)}, u32[]{:S(2)}, u32[]{:S(2)}) %collective-permute-start.2) | collective-permute-done | bytes 233504 | tf_op jit(solution)/shard_map/ppermute | solution.py:344
  48.7 1.3 %collective-permute-done.1.board_in = f32[520,128]{1,0:T(8,128)S(1)} collective-permute-done((f32[520,128]{1,0:T(8,128)S(1)}, f32[520,128]{1,0:T(8,128)S(1)}, u32[]{:S(2)}, u32[]{:S(2)}) %collective-permute-start.1) | collective-permute-done | bytes 266272 | tf_op jit(solution)/shard_map/ppermute | solution.py:334
  50.0 0.0 copy-done.1
  50.0 0.7 collective-permute-start.4
  50.7 0.7 collective-permute-start.3
  51.4 0.0 collective-permute-done.3.board_in
  51.4 0.0 collective-permute-done.4.halo_in
  51.5 32.0 %all_to_all.11 = f32[128,1,128]{2,1,0:T(1,128)S(1)} all-to-all(f32[128,1,128]{2,1,0:T(1,128)S(1)} %broadcast_in_dim.9), channel_id=1, replica_groups=mesh['s'=2,'xp'=2,'yh'=2,'q'=2,'z'=4,'c'=2] {'s','xp','yh','q','z','c'}, dimensions={0} | all-to-all | bytes 131072 | tf_op jit(solution)/shard_map/all_to_all | solution.py:354
  83.5 0.8 shard_map.107
  (5 shorter events, 0.1 us)
Async XLA Ops:
  1.9 33.1 %copy-start.2 = (f32[4,64]{1,0:T(4,128)S(1)}, f32[4,64]{1,0:T(4,128)}, u32[]{:S(2)}) copy-start(f32[4,64]{1,0:T(4,128)} %param.12) | copy-start | bytes 3076
  35.0 4.2 %copy-start = (bf16[16,64,128]{2,1,0:T(8,128)(2,1)S(1)}, bf16[16,64,128]{2,1,0:T(8,128)(2,1)}, u32[]{:S(2)}) copy-start(bf16[16,64,128]{2,1,0:T(8,128)(2,1)} %edge.5) | copy-start | bytes 786436
  35.0 4.2 %collective-permute-start = (f32[8,520,128]{2,1,0:T(8,128)S(1)}, f32[8,520,128]{2,1,0:T(8,128)S(1)}, u32[]{:S(2)}, u32[]{:S(2)}) collective-permute-start(f32[8,520,128]{2,1,0:T(8,128)S(1)} %all_to_all.10.mine), channel_id=1, source_target_pairs={{0,1},{1,0},{2,3},{3,2},{4,5},{5,4},{6,7},{7,6},{8,9},{9,8},{10,11... | collective-permute-start | bytes 6389768 | tf_op jit(solution)/shard_map/ppermute | solution.py:348
  39.2 10.8 %copy-start.1 = (f32[16,64,128]{2,1,0:T(8,128)S(1)}, f32[16,64,128]{2,1,0:T(8,128)}, u32[]{:S(2)}) copy-start(f32[16,64,128]{2,1,0:T(8,128)} %close.3) | copy-start | bytes 1572868
  42.5 7.5 %collective-permute-start.1 = (f32[520,128]{1,0:T(8,128)S(1)}, f32[520,128]{1,0:T(8,128)S(1)}, u32[]{:S(2)}, u32[]{:S(2)}) collective-permute-start(f32[520,128]{1,0:T(8,128)S(1)} %get-tuple-element.22), channel_id=1, source_target_pairs={{0,96},{16,112},{32,64},{48,80},{1,97},{17,113},{33,65},{49,81},{2... | collective-permute-start | bytes 798728 | tf_op jit(solution)/shard_map/ppermute | solution.py:334
  43.8 4.9 %collective-permute-start.2 = (f32[456,128]{1,0:T(8,128)S(1)}, f32[456,128]{1,0:T(8,128)S(1)}, u32[]{:S(2)}, u32[]{:S(2)}) collective-permute-start(f32[456,128]{1,0:T(8,128)S(1)} %get-tuple-element.23), channel_id=1, source_target_pairs={{0,24},{1,9},{16,8},{17,25},{32,56},{33,41},{48,40},{49,57},{2,26}... | collective-permute-start | bytes 700424 | tf_op jit(solution)/shard_map/ppermute | solution.py:344
  50.0 1.4 %collective-permute-start.4 = (f32[536,128]{1,0:T(8,128)S(1)}, f32[536,128]{1,0:T(8,128)S(1)}, u32[]{:S(2)}, u32[]{:S(2)}) collective-permute-start(f32[536,128]{1,0:T(8,128)S(1)} %get-tuple-element.25), channel_id=1, source_target_pairs={{64,88},{65,73},{80,72},{81,89},{96,120},{97,105},{112,104},{113,1... | collective-permute-start | bytes 823304 | tf_op jit(solution)/shard_map/ppermute | solution.py:344
  50.7 0.7 collective-permute-start.3
